TPU v7x, 64 devices: a 2x2x8 block of a 4x4x8 slice. The times are simulated.
64 devices in a mesh: dp: 4 (over x, y), tp: 16 (over z, core).
Axes of the slice: x: 2, y: 2, z: 8, core: 2. Of those that a mesh axis runs over, the one named last changes fastest.
The devices are a block of a 4x4x8 slice.
Arguments:
- token_act: bfloat16 [32, 1024, 768], P('dp'), parts along dimension 0
- token_cond: bfloat16 [32, 1024, 384], P('dp'), parts along dimension 0
- pair_bias: bfloat16 [2, 16, 1024, 1024], P(None, 'tp')
- token_mask: int32 [1024], replicated
- ada_scale: float32 [2, 2, 384], replicated
- ada_w: bfloat16 [2, 2, 384, 2, 768], replicated
- ada_bias: float32 [2, 2, 768], replicated
- zero_w: bfloat16 [2, 384, 2, 768], replicated
- zero_b: float32 [2, 2, 768], replicated
- w_qkvg: bfloat16 [2, 768, 4, 768], P(None, None, None, 'tp')
- b_q: float32 [2, 768], P(None, 'tp')
- w_o: bfloat16 [2, 768, 768], P(None, 'tp')
- w_up: bfloat16 [2, 768, 2, 1536], P(None, None, None, 'tp')
- w_down: bfloat16 [2, 1536, 768], P(None, 'tp')
Outputs:
- output: bfloat16 [32, 1024, 768], P('dp'), parts along dimension 0
There are 4 independent parts. A program takes and returns all parts, laid end to end along the dimension named above; an argument that names none is the same for every part.
All inputs are finite; a program needn't handle non-finite values.
Results may differ from a plain program's by a relative error of at most 0.02.
Values are sent between devices in bfloat16 or wider.
A program may use at most 768 MiB of HBM per device.

v0:
```python
import math
import functools
import jax
import jax.numpy as jnp
from jax import lax
from jax.sharding import PartitionSpec as P

LN_EPS = 1e-5


def layer_norm(values_in):
    row_mean = jnp.mean(values_in, axis=-1, keepdims=True)
    centered = values_in - row_mean
    variance = jnp.mean(centered * centered, axis=-1, keepdims=True)
    return centered * lax.rsqrt(variance + LN_EPS)


def ada_norm(act_f32, cond_normed, scale_vec, weight, bias_vec):
    cond_in = (cond_normed * scale_vec).astype(jnp.bfloat16)
    modulation = jnp.einsum('rc,cgd->rgd', cond_in, weight, preferred_element_type=jnp.float32)
    return (jax.nn.sigmoid(modulation[:, 0] + bias_vec) * layer_norm(act_f32) + modulation[:, 1]).astype(jnp.bfloat16)


def attend_sample(bias_layer, mask_add, logit_scale, operands):
    query_one, key_one, value_one = operands
    logits = jnp.einsum('qhc,khc->hqk', query_one, key_one, preferred_element_type=jnp.float32) * logit_scale + bias_layer + mask_add
    attn_probs = jax.nn.softmax(logits, axis=-1).astype(jnp.bfloat16)
    return jnp.einsum('hqk,khc->qhc', attn_probs, value_one, preferred_element_type=jnp.float32)


def solution(mesh):
    def shard_body(token_act, token_cond, pair_bias, token_mask, ada_scale, ada_w, ada_bias, zero_w, zero_b, w_qkvg, b_q, w_o, w_up, w_down):
        samples, tokens, model_width = token_act.shape
        cond_dim = token_cond.shape[-1]
        heads_local = pair_bias.shape[1]
        local_width = w_qkvg.shape[-1]
        head_dim = local_width // heads_local
        row_count = samples * tokens
        head_shape = (samples, tokens, heads_local, head_dim)
        logit_scale = 1.0 / math.sqrt(head_dim)
        mask_add = (token_mask.astype(jnp.float32) - 1.0) * 1e9
        cond_flat = token_cond.reshape(row_count, cond_dim)
        cond_normed = layer_norm(cond_flat.astype(jnp.float32))
        act_flat = token_act.reshape(row_count, model_width)
        for layer_idx in range(pair_bias.shape[0]):
            out_gates = jax.nn.sigmoid(jnp.einsum('rc,cgd->rgd', cond_flat, zero_w[layer_idx], preferred_element_type=jnp.float32) + zero_b[layer_idx])
            act_f32 = act_flat.astype(jnp.float32)
            normed = ada_norm(act_f32, cond_normed, ada_scale[layer_idx, 0], ada_w[layer_idx, 0], ada_bias[layer_idx, 0])
            projected = jnp.einsum('rd,dfe->rfe', normed, w_qkvg[layer_idx], preferred_element_type=jnp.float32)
            query_rows = (projected[:, 0] + b_q[layer_idx]).astype(jnp.bfloat16).reshape(head_shape)
            key_rows = projected[:, 1].astype(jnp.bfloat16).reshape(head_shape)
            value_rows = projected[:, 2].astype(jnp.bfloat16).reshape(head_shape)
            gate_heads = jax.nn.sigmoid(projected[:, 3])
            attend_layer = functools.partial(attend_sample, pair_bias[layer_idx], mask_add, logit_scale)
            mixed_heads = lax.map(attend_layer, (query_rows, key_rows, value_rows)).reshape(row_count, local_width)
            heads_out = (gate_heads * mixed_heads).astype(jnp.bfloat16)
            attn_part = jnp.dot(heads_out, w_o[layer_idx], preferred_element_type=jnp.float32).astype(jnp.bfloat16)
            attn_out = lax.psum(attn_part, 'tp').astype(jnp.float32)
            mid_f32 = (act_f32 + out_gates[:, 0] * attn_out).astype(jnp.bfloat16).astype(jnp.float32)
            normed_mid = ada_norm(mid_f32, cond_normed, ada_scale[layer_idx, 1], ada_w[layer_idx, 1], ada_bias[layer_idx, 1])
            hidden_pre = jnp.einsum('rd,dgf->rgf', normed_mid, w_up[layer_idx], preferred_element_type=jnp.float32)
            hidden = (jax.nn.silu(hidden_pre[:, 0]) * hidden_pre[:, 1]).astype(jnp.bfloat16)
            trans_part = jnp.dot(hidden, w_down[layer_idx], preferred_element_type=jnp.float32).astype(jnp.bfloat16)
            trans_out = lax.psum(trans_part, 'tp').astype(jnp.float32)
            act_flat = (mid_f32 + out_gates[:, 1] * trans_out).astype(jnp.bfloat16)
        return act_flat.reshape(samples, tokens, model_width)

    everywhere = P()
    in_specs = (P('dp', None, None), P('dp', None, None), P(None, 'tp', None, None), P(None), everywhere, everywhere, everywhere, everywhere, everywhere, P(None, None, None, 'tp'), P(None, 'tp'), P(None, 'tp', None), P(None, None, None, 'tp'), P(None, 'tp', None))
    return jax.shard_map(shard_body, mesh=mesh, in_specs=in_specs, out_specs=P('dp', None, None), check_vma=False)
```

profile of v0, /device:TPU:21, one launch (start us, length us, event | category | flops | bytes accessed | tf_op | source)
XLA Modules:
  0.0 1023.3 jit_solution(17283791189606745960)
XLA Ops:
  7.5 4.1 convert_reduce_fusion.3
  11.6 5.1 fusion.85
  16.8 4.2 fusion.133
  21.0 6.4 convert_reduce_fusion.4
  27.4 8.1 multiply_reduce_fusion
  36.9 11.4 %fusion.84 = (bf16[8,1024,384]{2,1,0:T(8,128)(2,1)}, bf16[8,1024,384]{2,1,0:T(8,128)(2,1)}, bf16[8,1024,384]{2,1,0:T(8,128)(2,1)}, bf16[8,1024,384]{2,1,0:T(8,128)(2,1)}) fusion(bf16[8,1024,384]{2,1,0:T(8,128)(2,1)} %param.19, f32[384]{0:T(512)S(1)} %get-tuple-element.113, f32[8,1024]{1,0:T(8,128)S(1)} %add_rsqrt_fusion.3, ...), kind=kLoop, calls=%fused_computation.121 | loop fusion | flops 34603008 | bytes 31528960 | tf_op jit(solution)/shard_map/convert_element_type | solution.py:19
  48.4 23.9 %fusion.113 = f32[8192,2,768]{2,0,1:T(8,128)} fusion(bf16[8192,384,1]{1,0,2:T(8,128)(2,1)} %bitcast.326, bf16[1,1,384,2,768]{4,3,2,1,0:T(2,128)(2,1)S(1)} %get-tuple-element.166), kind=kOutput, calls=%fused_computation.159 | convolution fusion | flops 9663676416 | bytes 57802752 | tf_op jit(solution)/shard_map/rc,cgd->rgd/dot_general | solution.py:20
  72.3 24.8 %fusion.65 = bf16[8192,1,768]{2,0,1:T(8,128)(2,1)} fusion(f32[8192,2,768]{2,0,1:T(8,128)} %fusion.113, bf16[8,1024,768]{2,1,0:T(8,128)(2,1)} %param.18, f32[8192]{0:T(1024)S(1)} %get-tuple-element.185, f32[8192]{0:T(1024)S(1)} %get-tuple-element.186, f32[768]{0:T(1024)S(1)} %get-tuple-element.111), kind=kLoop, calls=%fused_computation.92 | loop fusion | flops 62914560 | bytes 75566080 | tf_op jit(solution)/shard_map/convert_element_type | solution.py:21
  97.1 7.2 fusion.86
  109.4 2.4 fusion.134
  111.8 2.9 copy.51
  114.7 2.5 fusion.98
  118.5 39.1 %while.20 = (s32[]{:T(128)}, f32[8,1024,1,48]{1,3,2,0:T(8,128)}, bf16[8,1024,1,48]{1,3,2,0:T(8,128)(2,1)}, bf16[8,1024,1,48]{1,3,2,0:T(8,128)(2,1)}, bf16[8,1024...) while((s32[]{:T(128)}, f32[8,1024,1,48]{1,3,2,0:T(8,128)}, ...), condition=%wide.region_7.8_spmd, body=%wide.region_4.7_spmd.sunk | while | flops 211810304 | bytes 15198293 | solution.py:55
  125.9 2.4 fusion.165
  130.8 2.4 fusion.165
  135.7 2.4 fusion.165
  140.6 2.4 fusion.165
  150.4 2.4 fusion.165
  159.8 6.6 convolution_convert_fusion.3
  166.6 4.3 fusion.137
  172.3 31.8 %fusion.112 = f32[8192,2,768]{2,0,1:T(8,128)} fusion(bf16[8192,384,1]{1,0,2:T(8,128)(2,1)} %bitcast.325, bf16[1,1,384,2,768]{4,3,2,1,0:T(2,128)(2,1)S(1)} %get-tuple-element.165), kind=kOutput, calls=%fused_computation.157 | convolution fusion | flops 9663676416 | bytes 57802752 | tf_op jit(solution)/shard_map/rc,cgd->rgd/dot_general | solution.py:20
  204.1 29.6 %add_divide_fusion.1 = f32[8192,2,768]{2,0,1:T(8,128)} fusion(f32[2,768]{1,0:T(2,128)S(1)} %get-tuple-element.182, bf16[8192,384,1]{1,0,2:T(8,128)(2,1)} %bitcast.319, bf16[1,384,2,768]{3,2,1,0:T(2,128)(2,1)S(1)} %get-tuple-element.174), kind=kOutput, calls=%fused_computation.33 | convolution fusion | flops 9714008064 | bytes 57808896 | tf_op jit(solution)/shard_map/rc,cgd->rgd/dot_general | solution.py:46
  233.7 88.6 %all-reduce.5.cloned.1.call-done = bf16[8192,768]{1,0:T(8,128)(2,1)} async-done(((bf16[8192,768]{1,0:T(8,128)(2,1)}), bf16[8192,768]{1,0:T(8,128)(2,1)}) %all-reduce.5.cloned.1.call-update) | async-done | bytes 12582928 | tf_op jit(solution)/shard_map/psum | solution.py:58
  322.3 22.0 %convert_reduce_fusion.2 = (f32[8192]{0:T(1024)S(1)}, bf16[8192,768]{1,0:T(8,128)(2,1)}) fusion(bf16[8192,768]{1,0:T(8,128)(2,1)} %all-reduce.5.cloned.1.call-done, f32[8192,2,768]{2,0,1:T(8,128)} %add_divide_fusion.1, bf16[8,1024,768]{2,1,0:T(8,128)(2,1)} %param.18), kind=kLoop, calls=%fused_computation.42 | loop fusion | flops 44032000 | bytes 62947328 | tf_op jit(solution)/shard_map/reduce_sum | solution.py:12
  344.3 8.2 fusion.40
  352.5 21.5 %fusion.88 = f32[8192,192]{0,1:S(1)} fusion(bf16[768,192]{0,1:T(8,128)(2,1)S(1)} %bitcast.346, bf16[8192,768]{1,0:T(8,128)(2,1)} %get-tuple-element.150, f32[8192,2,768]{2,0,1:T(8,128)} %fusion.112, f32[8192]{0:T(1024)S(1)} %add_rsqrt_fusion.2, f32[8192]{0:T(1024)S(1)} %broadcast_multiply_fusion.2, f32[768]{0:T(1024)S(1)} %copy-done.17), kind=kOutput, calls=%fused_computation.126 | convolution fusion | flops 2478833664 | bytes 69569536
  374.1 6.5 convolution_convert_fusion.1
  380.7 3.3 copy.55
  384.0 24.9 %fusion.111 = f32[8192,2,768]{2,0,1:T(8,128)} fusion(bf16[8192,384,1]{1,0,2:T(8,128)(2,1)} %bitcast.324, bf16[1,1,384,2,768]{4,3,2,1,0:T(2,128)(2,1)} %get-tuple-element.164), kind=kOutput, calls=%fused_computation.154 | convolution fusion | flops 9663676416 | bytes 57802752 | tf_op jit(solution)/shard_map/rc,cgd->rgd/dot_general | solution.py:20
  408.9 23.6 %fusion.110 = f32[8192,2,768]{2,0,1:T(8,128)} fusion(bf16[8192,384,1]{1,0,2:T(8,128)(2,1)} %bitcast.323, bf16[1,1,384,2,768]{4,3,2,1,0:T(2,128)(2,1)S(1)} %copy-done.1), kind=kOutput, calls=%fused_computation.152 | convolution fusion | flops 9663676416 | bytes 57802752 | tf_op jit(solution)/shard_map/rc,cgd->rgd/dot_general | solution.py:20
  432.5 98.5 %all-reduce.7.cloned.1.call-done = bf16[8192,768]{1,0:T(8,128)(2,1)} async-done(((bf16[8192,768]{1,0:T(8,128)(2,1)}), bf16[8192,768]{1,0:T(8,128)(2,1)}) %all-reduce.7.cloned.1.call-update) | async-done | bytes 12582928 | tf_op jit(solution)/shard_map/psum | solution.py:64
  531.0 21.9 %convert_reduce_fusion.1 = (f32[8192]{0:T(1024)S(1)}, bf16[8192,768]{1,0:T(8,128)(2,1)}) fusion(bf16[8192,768]{1,0:T(8,128)(2,1)} %all-reduce.7.cloned.1.call-done, f32[8192,2,768]{2,0,1:T(8,128)} %add_divide_fusion.1, bf16[8192,768]{1,0:T(8,128)(2,1)} %get-tuple-element.150), kind=kLoop, calls=%fused_computation.39 | loop fusion | flops 44032000 | bytes 62947328 | tf_op jit(solution)/shard_map/reduce_sum | solution.py:12
  552.9 8.2 fusion.36
  561.2 21.5 %fusion.90 = f32[8192,192]{0,1:S(1)} fusion(bf16[768,192]{0,1:T(8,128)(2,1)S(1)} %bitcast.344, bf16[8192,768]{1,0:T(8,128)(2,1)} %get-tuple-element.148, f32[8192,2,768]{2,0,1:T(8,128)} %fusion.111, f32[8192]{0:T(1024)S(1)} %add_rsqrt_fusion.1, f32[8192]{0:T(1024)S(1)} %broadcast_multiply_fusion.1, f32[768]{0:T(1024)S(1)} %copy-done.16), kind=kOutput, calls=%fused_computation.127 | convolution fusion | flops 2478833664 | bytes 69569536
  588.3 38.9 %while.21 = (s32[]{:T(128)}, f32[8,1024,1,48]{1,3,2,0:T(8,128)}, bf16[8,1024,1,48]{1,3,2,0:T(8,128)(2,1)}, bf16[8,1024,1,48]{1,3,2,0:T(8,128)(2,1)S(1)}, bf16[8,...) while((s32[]{:T(128)}, f32[8,1024,1,48]{1,3,2,0:T(8,128)}, ...), condition=%wide.region_17.18_spmd, body=%wide.region_14.17_spmd.sunk | while | flops 211810304 | bytes 15198293 | solution.py:55
  590.8 2.4 fusion.169
  600.5 2.4 fusion.169
  605.4 2.4 fusion.169
  619.9 2.4 fusion.169
  629.3 6.4 convolution_convert_fusion.2
  635.9 30.0 %add_divide_fusion = f32[8192,2,768]{2,0,1:T(8,128)} fusion(f32[2,768]{1,0:T(2,128)S(1)} %copy-done.14, bf16[8192,384,1]{1,0,2:T(8,128)(2,1)} %bitcast.320, bf16[1,384,2,768]{3,2,1,0:T(2,128)(2,1)S(1)} %copy-done.3), kind=kOutput, calls=%fused_computation.32 | convolution fusion | flops 9714008064 | bytes 57808896 | tf_op jit(solution)/shard_map/rc,cgd->rgd/dot_general | solution.py:46
  665.9 120.3 %all-reduce.9.cloned.1.call-done = bf16[8192,768]{1,0:T(8,128)(2,1)} async-done(((bf16[8192,768]{1,0:T(8,128)(2,1)}), bf16[8192,768]{1,0:T(8,128)(2,1)}) %all-reduce.9.cloned.1.call-update) | async-done | bytes 12582928 | tf_op jit(solution)/shard_map/psum | solution.py:58
  786.1 21.8 %convert_reduce_fusion = (f32[8192]{0:T(1024)S(1)}, bf16[8192,768]{1,0:T(8,128)(2,1)}) fusion(bf16[8192,768]{1,0:T(8,128)(2,1)} %all-reduce.9.cloned.1.call-done, f32[8192,2,768]{2,0,1:T(8,128)} %add_divide_fusion, bf16[8192,768]{1,0:T(8,128)(2,1)} %get-tuple-element.148), kind=kLoop, calls=%fused_computation.36 | loop fusion | flops 44032000 | bytes 62947328 | tf_op jit(solution)/shard_map/reduce_sum | solution.py:12
  807.9 8.2 fusion.32
  816.2 21.7 %fusion.92 = f32[8192,192]{0,1:S(1)} fusion(bf16[768,192]{0,1:T(8,128)(2,1)S(1)} %bitcast.345, bf16[8192,768]{1,0:T(8,128)(2,1)} %get-tuple-element.146, f32[8192,2,768]{2,0,1:T(8,128)} %fusion.110, f32[8192]{0:T(1024)S(1)} %add_rsqrt_fusion, f32[8192]{0:T(1024)S(1)} %broadcast_multiply_fusion, f32[768]{0:T(1024)S(1)} %copy-done.15), kind=kOutput, calls=%fused_computation.128 | convolution fusion | flops 2478833664 | bytes 69569536
  837.9 6.4 convolution_convert_fusion
  844.3 150.4 %all-reduce.11.cloned.1.call-done = bf16[8192,768]{1,0:T(8,128)(2,1)} async-done(((bf16[8192,768]{1,0:T(8,128)(2,1)}), bf16[8192,768]{1,0:T(8,128)(2,1)}) %all-reduce.11.cloned.1.call-update) | async-done | bytes 12582928 | tf_op jit(solution)/shard_map/psum | solution.py:64
  994.7 21.6 %fusion.46 = bf16[8192,768]{1,0:T(8,128)(2,1)} fusion(bf16[8192,768]{1,0:T(8,128)(2,1)} %get-tuple-element.146, f32[8192,2,768]{2,0,1:T(8,128)} %add_divide_fusion, bf16[8192,768]{1,0:T(8,128)(2,1)} %all-reduce.11.cloned.1.call-done), kind=kLoop, calls=%fused_computation.63 | loop fusion | flops 31457280 | bytes 62914560 | tf_op jit(solution)/shard_map/convert_element_type | solution.py:65
  (128 shorter events, 76.8 us)
Async XLA Ops:
  6.5 315.8 %all-reduce.5.cloned.1.call-start = ((), (), s32[]{:S(2)}) async-start(), calls=%async_computation | async-start | bytes 25165824 | tf_op jit(solution)/shard_map/psum | solution.py:58
  6.6 10.2 %copy-start = (bf16[2,2,384,2,768]{4,3,2,1,0:T(2,128)(2,1)S(1)}, bf16[2,2,384,2,768]{4,3,2,1,0:T(2,128)(2,1)}, u32[]{:S(2)}) copy-start(bf16[2,2,384,2,768]{4,3,2,1,0:T(2,128)(2,1)} %param.23) | copy-start | bytes 14155780
  21.0 14.5 %copy-start.12 = (f32[2,2,768]{2,1,0:T(2,128)S(1)}, f32[2,2,768]{2,1,0:T(2,128)}, u32[]{:S(2)}) copy-start(f32[2,2,768]{2,1,0:T(2,128)} %param.24) | copy-start | bytes 36868
  21.0 15.2 %copy-start.4 = (bf16[2,768,4,48]{1,3,2,0:T(8,128)(2,1)S(1)}, bf16[2,768,4,48]{1,3,2,0:T(8,128)(2,1)}, u32[]{:S(2)}) copy-start(bf16[2,768,4,48]{1,3,2,0:T(8,128)(2,1)} %param.27) | copy-start | bytes 1769476
  104.3 2.5 copy-start.20
  104.3 5.1 copy-start.2
  106.4 8.3 copy-start.18
  118.5 41.3 %copy-start.10 = (bf16[2,48,768]{2,1,0:T(8,128)(2,1)S(1)}, bf16[2,48,768]{2,1,0:T(8,128)(2,1)}, u32[]{:S(2)}) copy-start(bf16[2,48,768]{2,1,0:T(8,128)(2,1)} %param.29) | copy-start | bytes 442372
  157.6 8.9 copy-start.6
  166.5 4.5 copy-start.13
  166.5 5.1 copy-start.5
  166.5 364.4 %all-reduce.7.cloned.1.call-start = ((), (), s32[]{:S(2)}) async-start(), calls=%async_computation.1 | async-start | bytes 25165824 | tf_op jit(solution)/shard_map/psum | solution.py:64
  344.3 8.2 copy-start.17
  352.5 21.5 %copy-start.21 = (bf16[2,96,768]{2,1,0:T(8,128)(2,1)S(1)}, bf16[2,96,768]{2,1,0:T(8,128)(2,1)}, u32[]{:S(2)}) copy-start(bf16[2,96,768]{2,1,0:T(8,128)(2,1)} %param.31) | copy-start | bytes 884740
  380.6 405.5 %all-reduce.9.cloned.1.call-start = ((), (), s32[]{:S(2)}) async-start(), calls=%async_computation.2 | async-start | bytes 25165824 | tf_op jit(solution)/shard_map/psum | solution.py:58
  383.9 24.9 %copy-start.1 = (bf16[1,1,384,2,768]{4,3,2,1,0:T(2,128)(2,1)S(1)}, bf16[1,1,384,2,768]{4,3,2,1,0:T(2,128)(2,1)}, u32[]{:S(2)}) copy-start(bf16[1,1,384,2,768]{4,3,2,1,0:T(2,128)(2,1)} %get-tuple-element.163) | copy-start | bytes 3538948
  552.9 8.3 copy-start.8
  552.9 8.3 copy-start.16
  582.7 4.0 copy-start.19
  582.7 5.6 copy-start.7
  588.3 41.0 %copy-start.11 = (bf16[2,48,768]{2,1,0:T(8,128)(2,1)S(1)}, bf16[2,48,768]{2,1,0:T(8,128)(2,1)}, u32[]{:S(2)}) copy-start(bf16[2,48,768]{2,1,0:T(8,128)(2,1)} %param.29) | copy-start | bytes 442372
  629.3 6.5 copy-start.3
  629.3 6.5 copy-start.14
  635.8 359.0 %all-reduce.11.cloned.1.call-start = ((), (), s32[]{:S(2)}) async-start(), calls=%async_computation.3 | async-start | bytes 25165824 | tf_op jit(solution)/shard_map/psum | solution.py:64
  807.9 8.2 copy-start.9
  807.9 8.3 copy-start.15
  816.2 21.7 %copy-start.22 = (bf16[2,96,768]{2,1,0:T(8,128)(2,1)S(1)}, bf16[2,96,768]{2,1,0:T(8,128)(2,1)}, u32[]{:S(2)}) copy-start(bf16[2,96,768]{2,1,0:T(8,128)(2,1)} %param.31) | copy-start | bytes 884740
Sparse Core Ops, SparseCore 0:
  166.6 155.6 all-reduce.4
  380.7 150.2 all-reduce.6
  635.9 150.2 all-reduce.8
  844.5 150.2 all-reduce.10
where the time goes:
time: 1030 us; the launch traced here: 1020 us
  waiting for transfers between devices  458 us (44%)
  matrix products  329 us (32%)
  other arithmetic  193 us (19%)
  local copies, waits for them, and re-layouts  28.2 us (3%)
  between operations  14.1 us (1%)
    psum x2, waiting for transfers between devices, shard_body(): trans_out = lax.psum(trans_part, 'tp').astype(jnp.float32)  249 us
    psum x2, waiting for transfers between devices, shard_body(): attn_out = lax.psum(attn_part, 'tp').astype(jnp.float32)  209 us
    dot_general x4, matrix products, ada_norm(): jnp.einsum('rc,cgd->rgd', cond_in, weight, preferred_element_type=jnp.flo...  104 us
    reduce_sum x5, other arithmetic, layer_norm(): row_mean = jnp.mean(values_in, axis=-1, keepdims=True)  76.2 us
    unnamed x4, matrix products  71.8 us
    dot_general x2, matrix products, shard_body(): jnp.einsum('rc,cgd->rgd', cond_flat, zero_w[layer_idx], preferred_element...  59.6 us
    dot_general x16, matrix products, attend_sample(): jnp.einsum('hqk,khc->qhc', attn_probs, value_one, preferred_element_type=...  38.2 us
    reduce_sum x5, other arithmetic, layer_norm(): variance = jnp.mean(centered * centered, axis=-1, keepdims=True)  37.8 us
  transfers between devices with their start and end apart: 4, of which 4 were waited for; matrix products, arithmetic and copies ran while one was open for 15% of the time, Pallas kernels for 0%

commit v1 on v0

v1 whole, which is shorter than its diff:
```python
import functools
import math

import jax
import jax.numpy as jnp
from jax import lax
from jax.experimental import pallas as pl
from jax.experimental.pallas import tpu as pltpu
from jax.sharding import PartitionSpec as P

LN_EPS = 1e-5
LOG2E = 1.4426950408889634
MESH = pl.DeviceIdType.MESH
BF16 = jnp.bfloat16
F32 = jnp.float32


def _ln(x):
    mean = jnp.mean(x, axis=-1, keepdims=True)
    cen = x - mean
    var = jnp.mean(cen * cen, axis=-1, keepdims=True)
    return cen * lax.rsqrt(var + LN_EPS)


def _sig(x):
    return 0.5 * jnp.tanh(0.5 * x) + 0.5


def _dot(a, b, ca=1, cb=0):
    return lax.dot_general(a, b, (((ca,), (cb,)), ((), ())), preferred_element_type=F32)


def _ada(x_f32, cond_normed, scale, w, bias):
    d = x_f32.shape[-1]
    mod = _dot((cond_normed * scale).astype(BF16), w)
    return (_sig(mod[:, :d] + bias) * _ln(x_f32) + mod[:, d:]).astype(BF16)


def _attn_kernel(first, dims, *refs):
    S, T, D, C, n_tp, hd, hp, layer, q_tile = dims
    if first:
        (x_hbm, cond_hbm, bias_hbm, mask_ref, w_ref, brow_ref, ascale_ref, aw_ref, ab_ref, o_hbm,
         xbuf, cbuf, bias_v, bt, k_s, qt_s, vt_s, gt_s, o_s, ld_sem, cd_sem, b_sem, send_sem, recv_sem) = refs
    else:
        (x_hbm, bias_hbm, mask_ref, w_ref, brow_ref, o_hbm,
         xbuf, bias_v, bt, k_s, qt_s, vt_s, gt_s, o_s, ld_sem, b_sem, send_sem, recv_sem) = refs
    cores = n_tp // S
    half = T // cores
    me = lax.axis_index("tp")
    z = me // cores

    barrier = pltpu.get_barrier_semaphore()
    for i in range(1, n_tp):
        pl.semaphore_signal(barrier, inc=1, device_id={"tp": lax.rem(me + i, n_tp)}, device_id_type=MESH)

    def sample_of(k):
        return lax.rem(z + 1 + k, S)

    def loads(k, slot):
        s = sample_of(k)
        out = [pltpu.make_async_copy(x_hbm.at[s], xbuf.at[slot], ld_sem.at[slot])]
        if first:
            out.append(pltpu.make_async_copy(cond_hbm.at[s], cbuf.at[slot], cd_sem.at[slot]))
        return out

    bias_cp = pltpu.make_async_copy(bias_hbm.at[layer, 0], bias_v, b_sem)
    bias_cp.start()
    for cp in loads(0, 0):
        cp.start()
    mask_add = (mask_ref[...].astype(F32) - 1.0) * 1e9
    qt_s[hp:, :] = jnp.zeros((hp, T), BF16)
    bias_cp.wait()

    def bias_step(i, _):
        r = pl.multiple_of(i * 128, 128)
        rows = (bias_v[pl.ds(r, 128), :].astype(F32) + mask_add) * LOG2E
        bt[:, pl.ds(r, 128)] = rows.T
        return 0

    lax.fori_loop(0, T // 128, bias_step, 0)
    pl.semaphore_wait(barrier, n_tp - 1)

    c1 = LOG2E / math.sqrt(hd)

    def message(k, slot, c):
        dst = sample_of(k) * cores + c
        return dst, pltpu.make_async_remote_copy(
            src_ref=o_s.at[slot, :, pl.ds(c * half, half)], dst_ref=o_hbm.at[me],
            send_sem=send_sem.at[slot, c], recv_sem=recv_sem, device_id={"tp": dst}, device_id_type=MESH)

    def sends(k, slot):
        for c in range(cores):
            dst, cp = message(k, slot, c)

            @pl.when(dst != me)
            def _():
                cp.start()

            @pl.when(dst == me)
            def _():
                pltpu.make_async_copy(o_s.at[slot, :, pl.ds(c * half, half)], o_hbm.at[me], recv_sem).start()

    def wait_sends(k, slot):
        for c in range(cores):
            dst, cp = message(k, slot, c)

            @pl.when(dst != me)
            def _():
                cp.wait_send()

    def step(k, _):
        slot = lax.rem(k, 2)

        @pl.when(k + 1 < S)
        def _():
            for cp in loads(k + 1, 1 - slot):
                cp.start()

        for cp in loads(k, slot):
            cp.wait()

        def proj(i, _):
            r = pl.multiple_of(i * q_tile, q_tile)
            rows = pl.ds(r, q_tile)
            xt = xbuf[slot, rows, :]
            if first:
                cn = _ln(cbuf[slot, rows, :].astype(F32))
                xt = _ada(xt.astype(F32), cn, ascale_ref[...], aw_ref[...], ab_ref[...])
            res = _dot(xt, w_ref[...]) + brow_ref[...]
            k_s[rows, :] = res[:, :2 * hp].astype(BF16)
            rest = res.T
            qt_s[0:hp, rows] = rest[hp:2 * hp].astype(BF16)
            ones = lax.broadcasted_iota(jnp.int32, (hp, q_tile), 0) == hd
            vt_s[:, rows] = jnp.where(ones, 1.0, rest[2 * hp:3 * hp]).astype(BF16)
            gt_s[:, rows] = _sig(rest[3 * hp:3 * hp + hd])
            return 0

        lax.fori_loop(0, T // q_tile, proj, 0)

        @pl.when(k >= 1)
        def _():
            sends(k - 1, 1 - slot)

        @pl.when(k >= 2)
        def _():
            wait_sends(k - 2, slot)

        def attend(i, _):
            r = pl.multiple_of(i * q_tile, q_tile)
            cols = pl.ds(r, q_tile)
            logits = _dot(k_s[...], qt_s[:, cols]) * c1 + bt[:, cols]
            top = jnp.max(logits, axis=0, keepdims=True)
            probs = jnp.exp2(logits - top).astype(BF16)
            mixed = _dot(vt_s[...], probs)
            o_s[slot, :, cols] = (gt_s[:, cols] * (mixed[:hd] / mixed[hd:hd + 1])).astype(BF16)
            return 0

        lax.fori_loop(0, T // q_tile, attend, 0)
        return 0

    lax.fori_loop(0, S, step, 0)
    sends(S - 1, (S - 1) % 2)
    wait_sends(S - 2, S % 2)
    wait_sends(S - 1, (S - 1) % 2)
    pltpu.make_async_copy(o_hbm, o_hbm, recv_sem).wait()


def _attention(layer, n_tp, x, cond, pair_bias, mask_row, w, brow, ada, collective_id):
    S, T, D = x.shape
    first = cond is not None
    hd = w.hd
    hp = w.hp
    C = cond.shape[-1] if first else 0
    q_tile = 256
    cores = n_tp // S
    half = T // cores
    anyspec = pl.BlockSpec(memory_space=pl.ANY)
    vspec = pl.BlockSpec(memory_space=pltpu.VMEM)
    args = [x] + ([cond] if first else []) + [pair_bias, mask_row, w.w, brow] + (list(ada) if first else [])
    specs = [anyspec] + ([anyspec] if first else []) + [anyspec, vspec, vspec, vspec] + ([vspec] * 3 if first else [])
    scratch = [pltpu.VMEM((2, T, D), BF16)] + ([pltpu.VMEM((2, T, C), BF16)] if first else []) + [
        pltpu.VMEM((T, T), BF16), pltpu.VMEM((T, T), F32), pltpu.VMEM((T, 2 * hp), BF16), pltpu.VMEM((2 * hp, T), BF16),
        pltpu.VMEM((hp, T), BF16), pltpu.VMEM((hd, T), F32), pltpu.VMEM((2, hd, T), BF16),
        pltpu.SemaphoreType.DMA((2,))] + ([pltpu.SemaphoreType.DMA((2,))] if first else []) + [
        pltpu.SemaphoreType.DMA, pltpu.SemaphoreType.DMA((2, cores)), pltpu.SemaphoreType.DMA]
    flops = 2 * S * T * (D * 4 * hp + 2 * T * 256 + (2 * C * D if first else 0))
    return pl.pallas_call(
        functools.partial(_attn_kernel, first, (S, T, D, C, n_tp, hd, hp, layer, q_tile)),
        out_shape=jax.ShapeDtypeStruct((n_tp, hd, half), BF16),
        in_specs=specs, out_specs=anyspec, scratch_shapes=scratch,
        cost_estimate=pl.CostEstimate(flops=flops, bytes_accessed=S * T * (D + C) * 2, transcendentals=S * T * T),
        compiler_params=pltpu.CompilerParams(collective_id=collective_id, has_side_effects=True, vmem_limit_bytes=60 << 20),
        name=f"attn{layer}",
    )(*args)


class _W:
    def __init__(self, w, hd, hp):
        self.w, self.hd, self.hp = w, hd, hp


def _mlp_kernel(nxt, dims, *refs):
    R, D, C, n_tp, hd, hu = dims
    if nxt:
        (o_ref, act_hbm, cond_hbm, wall_hbm, zw_ref, zb_ref, sc1_ref, w1_ref, b1_ref, sc2_ref, w2_ref, b2_ref,
         a_out, x_out, act, cond, wall, y_s, h_s, sems) = refs
    else:
        (o_ref, act_hbm, cond_hbm, wall_hbm, zw_ref, zb_ref, sc1_ref, w1_ref, b1_ref,
         a_out, act, cond, wall, y_s, h_s, sems) = refs
    if act_hbm.shape[0] != R:
        row0 = lax.axis_index("tp") * R
        act_src = act_hbm.at[pl.ds(row0, R), :]
    else:
        act_src = act_hbm
    row0 = lax.axis_index("tp") * R
    copies = [pltpu.make_async_copy(cond_hbm.at[pl.ds(row0, R), :], cond, sems.at[0]),
              pltpu.make_async_copy(act_src, act, sems.at[1]),
              pltpu.make_async_copy(wall_hbm, wall, sems.at[2])]
    for cp in copies:
        cp.start()
    copies[0].wait()
    cond_b = cond[...]
    cn = _ln(cond_b.astype(F32))
    gates = _sig(_dot(cond_b, zw_ref[...]) + zb_ref[...])
    copies[1].wait()
    copies[2].wait()
    o_t = o_ref[...].reshape(n_tp * hd, R)
    w_o = wall[:, 0:hd, :].reshape(n_tp * hd, D)
    t = _dot(o_t, w_o, 0, 0).astype(BF16).astype(F32)
    mid = (act[...].astype(F32) + gates[:, :D] * t).astype(BF16).astype(F32)
    y_s[...] = _ada(mid, cn, sc1_ref[...], w1_ref[...], b1_ref[...])
    H = n_tp * hu
    step = 4 * hu
    for j in range(H // step):
        dv = slice(4 * j, 4 * j + 4)
        u1 = _dot(y_s[...], wall[dv, hd + hu:hd + 2 * hu, :].reshape(step, D), 1, 1)
        u2 = _dot(y_s[...], wall[dv, hd + 2 * hu:hd + 3 * hu, :].reshape(step, D), 1, 1)
        h_s[:, j * step:(j + 1) * step] = (u1 * _sig(u1) * u2).astype(BF16)
    r = _dot(h_s[...], wall[:, hd:hd + hu, :].reshape(H, D)).astype(BF16).astype(F32)
    new = (mid + gates[:, D:] * r).astype(BF16)
    a_out[...] = new
    if nxt:
        x_out[...] = _ada(new.astype(F32), cn, sc2_ref[...], w2_ref[...], b2_ref[...])


def _mlp(o, act, cond, wall, zero, ada1, ada2, hd, hu):
    n_tp, _, R = o.shape
    D = act.shape[-1]
    C = cond.shape[-1]
    nxt = ada2 is not None
    anyspec = pl.BlockSpec(memory_space=pl.ANY)
    vspec = pl.BlockSpec(memory_space=pltpu.VMEM)
    args = [o, act, cond, wall, *zero, *ada1] + (list(ada2) if nxt else [])
    specs = [vspec, anyspec, anyspec, anyspec] + [vspec] * (len(args) - 4)
    row = jax.ShapeDtypeStruct((R, D), BF16)
    return pl.pallas_call(
        functools.partial(_mlp_kernel, nxt, (R, D, C, n_tp, hd, hu)),
        out_shape=(row, row) if nxt else row,
        in_specs=specs, out_specs=(vspec, vspec) if nxt else vspec,
        scratch_shapes=[pltpu.VMEM((R, D), BF16), pltpu.VMEM((R, C), BF16), pltpu.VMEM(wall.shape, BF16),
                        pltpu.VMEM((R, D), BF16), pltpu.VMEM((R, n_tp * hu), BF16), pltpu.SemaphoreType.DMA((3,))],
        cost_estimate=pl.CostEstimate(flops=2 * R * D * (D + 3 * n_tp * hu + 6 * C), bytes_accessed=wall.size * 2, transcendentals=R * D),
        compiler_params=pltpu.CompilerParams(vmem_limit_bytes=60 << 20),
        name="mlp" + ("0" if nxt else "1"),
    )(*args)


def solution(mesh):
    n_tp = mesh.shape["tp"]

    def shard_body(token_act, token_cond, pair_bias, token_mask, ada_scale, ada_w, ada_bias, zero_w, zero_b, w_qkvg, b_q, w_o, w_up, w_down):
        S, T, D = token_act.shape
        C = token_cond.shape[-1]
        hd = w_qkvg.shape[-1]
        hp = 64
        hu = w_down.shape[1]
        L = pair_bias.shape[0]
        mask_row = token_mask.reshape(1, T)

        walls = []
        for l in range(L):
            up = jnp.transpose(w_up[l], (1, 2, 0)).reshape(2 * hu, D)
            walls.append(lax.all_gather(jnp.concatenate([w_o[l], w_down[l], up], axis=0), "tp"))

        def qkvg(l):
            w = jnp.pad(w_qkvg[l], ((0, 0), (0, 0), (0, hp - hd)))
            w = jnp.concatenate([w[:, 1], w[:, 0], w[:, 2], w[:, 3]], axis=1)
            brow = jnp.zeros((1, 4 * hp), F32).at[0, hp:hp + hd].set(b_q[l])
            return _W(w, hd, hp), brow

        def ada(l, j):
            return ada_scale[l, j].reshape(1, C), ada_w[l, j].reshape(C, 2 * D), ada_bias[l, j].reshape(1, D)

        def zero(l):
            return zero_w[l].reshape(C, 2 * D), zero_b[l].reshape(1, 2 * D)

        cond_flat = token_cond.reshape(S * T, C)
        act = token_act.reshape(S * T, D)
        x = token_act
        for l in range(L):
            w, brow = qkvg(l)
            o = _attention(l, n_tp, x, token_cond if l == 0 else None, pair_bias, mask_row, w, brow, ada(l, 0), l)
            if l + 1 < L:
                act, x_own = _mlp(o, act, cond_flat, walls[l], zero(l), ada(l, 1), ada(l + 1, 0), hd, hu)
                x = lax.all_gather(x_own, "tp", tiled=True).reshape(S, T, D)
            else:
                act = _mlp(o, act, cond_flat, walls[l], zero(l), ada(l, 1), None, hd, hu)
        return lax.all_gather(act, "tp", tiled=True).reshape(S, T, D)

    everywhere = P()
    in_specs = (P('dp', None, None), P('dp', None, None), P(None, 'tp', None, None), P(None), everywhere, everywhere, everywhere, everywhere, everywhere, P(None, None, None, 'tp'), P(None, 'tp'), P(None, 'tp', None), P(None, None, None, 'tp'), P(None, 'tp', None))
    return jax.shard_map(shard_body, mesh=mesh, in_specs=in_specs, out_specs=P('dp', None, None), check_vma=False)
```

time: 1030 us -> 363 us (0.35)
  matrix products: 329 us -> 0 us
  waiting for transfers between devices: 458 us -> 159 us
  other arithmetic: 193 us -> 4.89 us
  Pallas kernels: 0 us -> 150 us
    psum x4 -> x0, waiting for transfers between devices: 458 us -> none  [the longest x2 249 us: shard_body(): trans_out = lax.psum(trans_part, 'tp').astype(jnp.float32)]
    dot_general x42 -> x0, matrix products: 258 us -> none  [the longest x4 104 us: ada_norm(): jnp.einsum('rc,cgd->rgd', cond_in, weight, preferred_element_type=jnp.flo...]
    all_gather x0 -> x4, waiting for transfers between devices: none -> 159 us  [the longest x1 74.2 us: shard_body(): return lax.all_gather(act, 'tp', tiled=True).reshape(S, T, D)]
    pallas_call x0 -> x4, Pallas kernels: none -> 150 us  [the longest x2 123 us: _attention(): pl.pallas_call(functools.partial(_attn_kernel, first, (S, T, D, C, n_tp,...]
    reduce_sum x26 -> x0, other arithmetic: 124 us -> none  [the longest x5 76.2 us: layer_norm(): row_mean = jnp.mean(values_in, axis=-1, keepdims=True)]
    unnamed x4 -> x0, matrix products: 71.8 us -> none
    convert_element_type x5 -> x0, other arithmetic: 60.6 us -> none  [the longest x1 24.8 us: ada_norm(): (jax.nn.sigmoid(modulation[:, 0] + bias_vec) * layer_norm(act_f32) + modu...]
    unnamed x50 -> x34, local copies, waits for them, and re-layouts: 6.33 us -> 21.5 us
  transfers between devices with their start and end apart: 4 -> 4, of which waited for: 4 -> 3; matrix products, arithmetic and copies ran while one was open for 15% -> 7% of each run, Pallas kernels for 0% -> 34%
where the time goes in v1:
time: 363 us
  waiting for transfers between devices  159 us (44%)
  Pallas kernels  150 us (41%)
  local copies, waits for them, and re-layouts  34.7 us (10%)
  between operations  13.3 us (4%)
  other arithmetic  4.89 us (1%)
    pallas_call x2, Pallas kernels, _attention(): pl.pallas_call(functools.partial(_attn_kernel, first, (S, T, D, C, n_tp,...  123 us
    all_gather x1, waiting for transfers between devices, shard_body(): return lax.all_gather(act, 'tp', tiled=True).reshape(S, T, D)  74.2 us
    all_gather x1, waiting for transfers between devices, shard_body(): x = lax.all_gather(x_own, 'tp', tiled=True).reshape(S, T, D)  64.5 us
    pallas_call x2, Pallas kernels, _mlp(): pl.pallas_call(functools.partial(_mlp_kernel, nxt, (R, D, C, n_tp, hd, hu...  27.3 us
    unnamed x34, local copies, waits for them, and re-layouts  21.5 us
    all_gather x2, waiting for transfers between devices, shard_body(): lax.all_gather(jnp.concatenate([w_o[l], w_down[l], up], axis=0), 'tp')  20.1 us
  transfers between devices with their start and end apart: 4, of which 3 were waited for; matrix products, arithmetic and copies ran while one was open for 7% of the time, Pallas kernels for 34%

profile of v1, /device:TPU:21, one launch (start us, length us, event | category | flops | bytes accessed | tf_op | source)
XLA Modules:
  0.0 362.5 jit_solution(502924342026240429)
XLA Ops:
  6.6 1.1 fusion.10
  7.7 0.0 copy-start.1
  7.7 0.7 slice_bitcast_fusion
  8.4 0.9 pad_maximum_fusion
  9.3 0.1 all-gather.11.cloned.1.call-update
  9.4 0.1 all-gather.7.cloned.1.call-start
  9.4 0.8 fusion.11
  10.2 0.4 copy.17
  10.6 4.9 %fusion.8 = (bf16[1,1,384,2,768]{4,3,2,1,0:T(2,128)(2,1)S(1)}, bf16[1,1,384,2,768]{4,3,2,1,0:T(2,128)(2,1)S(1)}, bf16[1,1,384,2,768]{4,3,2,1,0:T(2,128)(2,1)S(1)}, bf16[1,1,384,2,768]{4,3,2,1,0:T(2,128)(2,1)S(1)}) fusion(bf16[2,2,384,2,768]{4,3,2,1,0:T(2,128)(2,1)} %param.23), kind=kLoop, calls=%fused_computation.38 | loop fusion | bytes 9437184 | tf_op jit(solution)/shard_map/slice | solution.py:292
  15.5 1.2 copy.19
  16.7 0.7 slice.144
  17.3 1.2 copy.22
  18.5 1.2 copy.23
  19.7 0.9 copy-done
  20.6 1.6 fusion.9
  22.2 0.0 copy-start.5
  22.2 0.0 copy-start.8
  22.2 1.3 copy.20
  23.5 0.6 copy.21
  24.1 0.6 and_reduce_fusion
  24.7 0.6 broadcast_select_fusion
  25.3 0.9 scatter.6.refs_5_
  26.3 0.2 fusion
  26.5 1.0 pad_maximum_fusion.2.refs_4_
  27.5 0.6 slice_bitcast_fusion.10
  28.1 0.6 slice_bitcast_fusion.6
  28.7 69.7 %attn0.1.refs_0_ = bf16[16,48,512]{2,1,0:T(8,128)(2,1)} custom-call(bf16[8,1024,768]{2,1,0:T(8,128)(2,1)} %refs_0_.1, bf16[8,1024,384]{2,1,0:T(8,128)(2,1)} %refs_1_.2, bf16[2,1,1024,1024]{3,2,1,0:T(8,128)(2,1)} %refs_1_.3, s32[1,1024]{1,0:T(1,128)} %bitcast.109, bf16[768,256]{1,0:T(8,128)(2,1)} %pad_maximum_fusion.2.refs_4_, f32[1,256]{1,0:T(1,128)} %copy-done.10, ...), custom_call_target="tpu_custom_call" | custom-call | flops 21474836480 | bytes 18874368 | tf_op jit(solution)/shard_map/attn0/pallas_call | solution.py:187
  98.4 0.0 all-gather.11.cloned.1.call-done
  98.5 14.2 %mlp0.1 = (bf16[512,768]{1,0:T(8,128)(2,1)}, bf16[512,768]{1,0:T(8,128)(2,1)}) custom-call(bf16[16,48,512]{2,1,0:T(8,128)(2,1)} %attn0.1.refs_0_, bf16[8192,768]{1,0:T(8,128)(2,1)} %bitcast.84, bf16[8192,384]{1,0:T(8,128)(2,1)} %bitcast.87, bf16[16,336,768]{2,1,0:T(8,128)(2,1)} %bitcast.86, bf16[384,1536]{1,0:T(8,128)(2,1)} %bitcast.92, ...), custom_call_target="tpu_custom_call" | custom-call | flops 6039797760 | bytes 8257536 | tf_op jit(solution)/shard_map/mlp0/pallas_call | solution.py:256
  112.7 0.1 all-gather.7.cloned.1.call-update
  112.7 0.1 all-gather.13.cloned.1.call-start
  112.8 0.8 pad_maximum_fusion.1
  113.7 0.1 all-gather.13.cloned.1.call-update
  113.7 0.1 all-gather.9.cloned.1.call-start
  113.8 1.3 copy.18
  115.1 1.2 copy.26
  116.4 1.2 copy.24
  117.5 0.6 copy.25
  118.1 0.9 scatter.9.refs_4_
  119.1 0.2 fusion.4
  119.3 1.0 pad_maximum_fusion.3.refs_3_
  120.3 64.5 %all-gather.7.cloned.1.call-done = bf16[8192,768]{1,0:T(8,128)(2,1)} async-done(((bf16[512,768]{1,0:T(8,128)(2,1)}), bf16[8192,768]{1,0:T(8,128)(2,1)}) %all-gather.7.cloned.1.call-update) | async-done | bytes 12582928 | tf_op jit(solution)/shard_map/all_gather | solution.py:305
  184.8 53.3 %attn1.1.refs_0_ = bf16[16,48,512]{2,1,0:T(8,128)(2,1)} custom-call(bf16[8,1024,768]{2,1,0:T(8,128)(2,1)} %bitcast.107, bf16[2,1,1024,1024]{3,2,1,0:T(8,128)(2,1)} %refs_1_.3, s32[1,1024]{1,0:T(1,128)} %bitcast.110, bf16[768,256]{1,0:T(8,128)(2,1)} %pad_maximum_fusion.3.refs_3_, f32[1,256]{1,0:T(1,128)} %copy-done.9), custom_call_target="tpu_custom_call" | custom-call | flops 11811160064 | bytes 12582912 | tf_op jit(solution)/shard_map/attn1/pallas_call | solution.py:187
  238.1 20.1 %all-gather.13.cloned.1.call-done = bf16[5376,768]{1,0:T(8,128)(2,1)} async-done(((bf16[336,768]{1,0:T(8,128)(2,1)}), bf16[5376,768]{1,0:T(8,128)(2,1)}) %all-gather.13.cloned.1.call-update) | async-done | bytes 8257552 | tf_op jit(solution)/shard_map/all_gather | solution.py:283
  258.2 13.1 %mlp1.1 = bf16[512,768]{1,0:T(8,128)(2,1)} custom-call(bf16[16,48,512]{2,1,0:T(8,128)(2,1)} %attn1.1.refs_0_, bf16[512,768]{1,0:T(8,128)(2,1)} %get-tuple-element.32.refs_1_, bf16[8192,384]{1,0:T(8,128)(2,1)} %bitcast.88, bf16[16,336,768]{2,1,0:T(8,128)(2,1)} %bitcast.108, bf16[384,1536]{1,0:T(8,128)(2,1)} %bitcast.102, f32[1,1536]{1,0:T(1,128)} %bitcast.106, ...), custom_call_target="tpu_custom_call" | custom-call | flops 6039797760 | bytes 8257536 | tf_op jit(solution)/shard_map/mlp1/pallas_call | solution.py:256
  271.2 0.1 all-gather.9.cloned.1.call-update
  271.3 74.2 %all-gather.9.cloned.1.call-done = bf16[8192,768]{1,0:T(8,128)(2,1)} async-done(((bf16[512,768]{1,0:T(8,128)(2,1)}), bf16[8192,768]{1,0:T(8,128)(2,1)}) %all-gather.9.cloned.1.call-update) | async-done | bytes 12582928 | tf_op jit(solution)/shard_map/all_gather | solution.py:308
  345.5 10.4 %copy.30 = bf16[8,1024,768]{2,1,0:T(8,128)(2,1)} copy(bf16[8,1024,768]{2,1,0:T(8,128)(2,1)} %bitcast.85) | data formatting | bytes 25165824
  (24 shorter events, 0.1 us)
Async XLA Ops:
  6.5 1.2 copy-start.3
  6.5 1.9 copy-start.4
  6.6 91.9 %all-gather.11.cloned.1.call-start = ((), (), s32[]{:S(2)}) async-start(), calls=%async_computation.2 | async-start | bytes 8773632 | tf_op jit(solution)/shard_map/all_gather | solution.py:283
  7.7 1.7 copy-start.1
  9.4 175.4 %all-gather.7.cloned.1.call-start = ((), (), s32[]{:S(2)}) async-start(), calls=%async_computation | async-start | bytes 13369344 | tf_op jit(solution)/shard_map/all_gather | solution.py:305
  18.5 2.1 copy-start
  22.2 1.3 copy-start.5
  22.2 2.5 copy-start.8
  26.3 1.2 copy-start.10
  26.3 1.2 copy-start.7
  26.3 1.8 copy-start.6
  98.5 14.4 %copy-start.2 = (bf16[96,768]{1,0:T(8,128)(2,1)S(1)}, bf16[96,768]{1,0:T(8,128)(2,1)}, u32[]{:S(2)}) copy-start(bf16[96,768]{1,0:T(8,128)(2,1)} %get-tuple-element.51) | copy-start | bytes 442372
  112.7 145.4 %all-gather.13.cloned.1.call-start = ((), (), s32[]{:S(2)}) async-start(), calls=%async_computation.3 | async-start | bytes 8773632 | tf_op jit(solution)/shard_map/all_gather | solution.py:283
  113.7 231.8 %all-gather.9.cloned.1.call-start = ((), (), s32[]{:S(2)}) async-start(), calls=%async_computation.1 | async-start | bytes 13369344 | tf_op jit(solution)/shard_map/all_gather | solution.py:308
  119.1 1.2 copy-start.9
Sparse Core Ops, SparseCore 0:
  9.5 70.0 all-gather.10
  112.9 71.8 all-gather.6
  186.4 71.7 all-gather.12
  271.4 74.0 all-gather.8

commit v2 on v0

v2 whole, which is shorter than its diff:
```python
import functools
import math

import jax
import jax.numpy as jnp
from jax import lax
from jax.experimental import pallas as pl
from jax.experimental.pallas import tpu as pltpu
from jax.sharding import PartitionSpec as P

LN_EPS = 1e-5
LOG2E = 1.4426950408889634
MESH = pl.DeviceIdType.MESH
BF16 = jnp.bfloat16
F32 = jnp.float32
HP = 64
QT = 256
ANY = pl.BlockSpec(memory_space=pl.ANY)
VMEM = pl.BlockSpec(memory_space=pltpu.VMEM)


def _ln(x):
    mean = jnp.mean(x, axis=-1, keepdims=True)
    cen = x - mean
    var = jnp.mean(cen * cen, axis=-1, keepdims=True)
    return cen * lax.rsqrt(var + LN_EPS)


def _sig(x):
    return 0.5 * jnp.tanh(0.5 * x) + 0.5


def _dot(a, b, ca=1, cb=0):
    return lax.dot_general(a, b, (((ca,), (cb,)), ((), ())), preferred_element_type=F32)


def _ada(x_f32, cond_normed, scale, w, bias):
    d = x_f32.shape[-1]
    mod = _dot((cond_normed * scale).astype(BF16), w)
    return (_sig(mod[:, :d] + bias) * _ln(x_f32) + mod[:, d:]).astype(BF16)


class Place:
    def __init__(self, n_tp):
        self.n = n_tp
        self.nz = n_tp // 2
        self.me = lax.axis_index("tp")
        self.z = self.me // 2
        self.c = lax.rem(self.me, 2)
        self.partner = self.z * 2 + (1 - self.c)

    def at(self, off):
        return lax.rem(self.z + off + self.nz, self.nz) * 2 + self.c

    def enter(self, everyone):
        barrier = pltpu.get_barrier_semaphore()
        if everyone:
            peers = [lax.rem(self.me + i, self.n) for i in range(1, self.n)]
        else:
            peers = [self.at(1), self.at(-1), self.partner]
        for p in peers:
            pl.semaphore_signal(barrier, inc=1, device_id={"tp": p}, device_id_type=MESH)
        return lambda: pl.semaphore_wait(barrier, len(peers))


class Ring:
    def __init__(self, place, view, recv_sem, send_sem, n_chunk):
        self.p, self.view, self.recv, self.send, self.n_chunk = place, view, recv_sem, send_sem, n_chunk
        self.far = place.nz // 2

    def _push(self, b, ch, dst, src=None):
        v = self.view(b, ch)
        pltpu.make_async_remote_copy(
            src_ref=v if src is None else src, dst_ref=v, send_sem=self.send, recv_sem=self.recv.at[b, ch],
            device_id={"tp": dst}, device_id_type=MESH).start()

    def own(self, ch, src=None):
        p = self.p
        self._push(p.me, ch, p.at(1), src)
        self._push(p.me, ch, p.at(-1), src)
        self._push(p.me, ch, p.partner, src)

    def wait(self, b, ch):
        v = self.view(b, ch)
        pltpu.make_async_copy(v, v, self.recv.at[b, ch]).wait()

    def service(self, h, ch):
        p = self.p
        for sign, core in ((1, 0), (-1, 1)):
            b = p.at(-sign * h)

            @pl.when((h < self.far) | (p.c == core))
            def _():
                self.wait(b, ch)

                @pl.when((h < self.far - 1) | ((h == self.far - 1) & (p.c == core)))
                def _():
                    self._push(b, ch, p.at(sign))

                self._push(b, ch, p.partner)

    def drain(self, whole):
        pltpu.make_async_copy(whole, whole, self.send).wait()


class Attend:
    def __init__(self, n_tp, hd, w, brow, bt, k_s, qt_s, vt_s, gt_s, lg, o_s, x_rows):
        self.__dict__.update(locals())
        self.T = bt.shape[0]

    def project(self):
        T, hd = self.T, self.hd
        tile = QT
        for i in range(T // tile):
            rows = pl.ds(i * tile, tile)
            res = _dot(self.x_rows(i, tile), self.w[...], 1, 1) + self.brow
            self.k_s[rows, :] = res[:, :2 * HP].astype(BF16)
            rest = res.T
            self.qt_s[0:HP, rows] = rest[HP:2 * HP].astype(BF16)
            ones = lax.broadcasted_iota(jnp.int32, (HP, tile), 0) == hd
            self.vt_s[:, rows] = jnp.where(ones, 1.0, rest[2 * HP:3 * HP]).astype(BF16)
            self.gt_s[:, rows] = _sig(rest[3 * HP:3 * HP + hd])

    def attend(self, slot):
        T, hd = self.T, self.hd
        n = T // QT
        c1 = LOG2E / math.sqrt(hd)

        def scores(i):
            cols = pl.ds(i * QT, QT)
            logits = _dot(self.k_s[...], self.qt_s[:, cols]) * c1 + self.bt[:, cols]
            self.lg[i % 2] = logits
            return jnp.max(logits, axis=0, keepdims=True)

        top = scores(0)
        for i in range(n):
            cols = pl.ds(i * QT, QT)
            nxt = scores(i + 1) if i + 1 < n else None
            probs = jnp.exp2(self.lg[i % 2] - top).astype(BF16)
            mixed = _dot(self.vt_s[...], probs)
            self.o_s[slot, :, cols] = (self.gt_s[:, cols] * (mixed[:hd] / mixed[hd:hd + 1])).astype(BF16)
            top = nxt


def _load_bias(bias_v, mask_ref, bt):
    T = bt.shape[0]
    mask_add = (mask_ref[...].astype(F32) - 1.0) * 1e9

    def step(i, _):
        r = pl.multiple_of(i * 128, 128)
        rows = (bias_v[pl.ds(r, 128), :].astype(F32) + mask_add) * LOG2E
        bt[:, pl.ds(r, 128)] = rows.T
        return 0

    lax.fori_loop(0, T // 128, step, 0)


class Exchange:
    def __init__(self, place, o_s, o_hbm, send_sem, recv_sem):
        self.p, self.o_s, self.o_hbm, self.send, self.recv = place, o_s, o_hbm, send_sem, recv_sem
        self.half = o_s.shape[-1] // 2

    def _each(self, sample, slot, remote, local):
        p = self.p
        for c in range(2):
            dst = sample * 2 + c
            src = self.o_s.at[slot, :, pl.ds(c * self.half, self.half)]
            cp = pltpu.make_async_remote_copy(
                src_ref=src, dst_ref=self.o_hbm.at[p.me], send_sem=self.send.at[slot, c], recv_sem=self.recv,
                device_id={"tp": dst}, device_id_type=MESH)

            @pl.when(dst != p.me)
            def _():
                remote(cp)

            @pl.when(dst == p.me)
            def _():
                local(pltpu.make_async_copy(src, self.o_hbm.at[p.me], self.send.at[slot, c]))

    def start(self, sample, slot):
        self._each(sample, slot, lambda cp: cp.start(), lambda cp: cp.start())

    def sent(self, sample, slot):
        self._each(sample, slot, lambda cp: cp.wait_send(), lambda cp: cp.wait())

    def arrived(self):
        rest = self.o_hbm.at[0:self.p.n - 1]
        pltpu.make_async_copy(rest, rest, self.recv).wait()


def _block0_kernel(dims, x_hbm, cond_hbm, bias_hbm, mask_ref, wq_hbm, brow_ref, asc_ref, aw_hbm, ab_ref, wo_hbm, wup_hbm, wdn_hbm,
                   o_hbm, wg_hbm,
                   xbuf, cbuf, bias_v, bt, w_s, aw_s, k_s, qt_s, vt_s, gt_s, lg, o_s, wst,
                   ld_sem, cd_sem, b_sem, q_sem, a_sem, st_sem, wl_sem, o_send, o_recv, w_send, w_recv):
    S, T, D, C, n_tp, hd, hu, L = dims
    p = Place(n_tp)
    entered = p.enter(True)
    rows_w = hd + 3 * hu
    cuts = (0, hd + hu, rows_w)
    stage = []
    for l in range(L):
        for src, lo, hi in ((wo_hbm.at[l], 0, hd), (wup_hbm.at[l, 0], hd, hd + hu), (wup_hbm.at[l, 1], hd + hu, hd + 2 * hu),
                            (wdn_hbm.at[l], hd + 2 * hu, rows_w)):
            stage.append(pltpu.make_async_copy(src, wst.at[l, lo:hi, :], st_sem.at[len(stage)]))
    for cp in stage:
        cp.start()
    sign = 1 - 2 * p.c

    def sample_of(k):
        return lax.rem(p.z + S + sign * (k + 1), S)

    def loads(k, slot):
        s = sample_of(k)
        return [pltpu.make_async_copy(x_hbm.at[s], xbuf.at[slot], ld_sem.at[slot]),
                pltpu.make_async_copy(cond_hbm.at[s], cbuf.at[slot], cd_sem.at[slot])]

    bias_cp = pltpu.make_async_copy(bias_hbm.at[0, 0], bias_v, b_sem)
    bias_cp.start()
    aw_cp = pltpu.make_async_copy(aw_hbm.at[0, 0], aw_s, a_sem)
    aw_cp.start()
    for cp in loads(0, 0):
        cp.start()
    w_s[...] = jnp.zeros_like(w_s)
    qt_s[HP:, :] = jnp.zeros((HP, T), BF16)
    order = (1, 0, 2, 3)
    wq = [pltpu.make_async_copy(wq_hbm.at[0, f], w_s.at[i * HP:i * HP + hd, :], q_sem.at[i]) for i, f in enumerate(order)]
    for cp in wq:
        cp.start()
    for cp in stage:
        cp.wait()
    keep = [pltpu.make_async_copy(wst.at[l], wg_hbm.at[l, p.me], wl_sem.at[l]) for l in range(L)]
    for cp in keep:
        cp.start()
    entered()
    rings = []
    for l in range(L):
        def view(b, ch, l=l):
            return wg_hbm.at[l, b, cuts[ch]:cuts[ch + 1], :]
        ring = Ring(p, view, w_recv.at[l], w_send.at[l], 2)
        rings.append(ring)
        for ch in range(2):
            ring.own(ch, wst.at[l, cuts[ch]:cuts[ch + 1], :])
    bias_cp.wait()
    _load_bias(bias_v, mask_ref, bt)
    for cp in wq:
        cp.wait()
    aw_cp.wait()
    ex = Exchange(p, o_s, o_hbm, o_send, o_recv)

    def service(e):
        per = 2 * L
        for l in range(L):
            for ch in range(2):
                @pl.when(lax.rem(e, per) == 2 * l + ch)
                def _():
                    rings[l].service(e // per + 1, ch)

    def step(k, _):
        slot = lax.rem(k, 2)

        @pl.when(k + 1 < S)
        def _():
            for cp in loads(k + 1, 1 - slot):
                cp.start()

        for cp in loads(k, slot):
            cp.wait()

        def x_rows(i, tile):
            rows = pl.ds(i * tile, tile)
            cn = _ln(cbuf[slot, rows, :].astype(F32))
            return _ada(xbuf[slot, rows, :].astype(F32), cn, asc_ref[0, 0:1, :], aw_s[...], ab_ref[0, 0:1, :])

        at = Attend(n_tp, hd, w_s, brow_ref[0:1, :], bt, k_s, qt_s, vt_s, gt_s, lg, o_s, x_rows)
        at.project()

        @pl.when(k >= 1)
        def _():
            ex.start(sample_of(k - 1), 1 - slot)
            service(2 * k - 2)
            service(2 * k - 1)

        @pl.when(k >= 2)
        def _():
            ex.sent(sample_of(k - 2), slot)

        at.attend(slot)
        return 0

    lax.fori_loop(0, S, step, 0)
    ex.start(sample_of(S - 1), (S - 1) % 2)
    lax.fori_loop(2 * S - 2, 2 * L * (p.nz // 2), lambda e, _: (service(e), 0)[1], 0)
    ex.sent(sample_of(S - 2), S % 2)
    ex.sent(sample_of(S - 1), (S - 1) % 2)

    def other(i, _):
        b = i * 2 + (1 - p.c)
        for ring in rings:
            for ch in range(2):
                ring.wait(b, ch)
        return 0

    lax.fori_loop(0, p.nz, other, 0)
    for l in range(L):
        rings[l].drain(wg_hbm.at[l, 0:n_tp - 1])
        keep[l].wait()
    ex.arrived()


def _block0(x, cond, pair_bias, mask_row, wq, brow, asc, aw, ab, wo, wup, wdn):
    S, T, D = x.shape
    C = cond.shape[-1]
    L, _, hd, _ = wq.shape
    hu = wdn.shape[1]
    n_tp = S * 2
    rows_w = hd + 3 * hu
    half = T // 2
    dma = pltpu.SemaphoreType.DMA
    return pl.pallas_call(
        functools.partial(_block0_kernel, (S, T, D, C, n_tp, hd, hu, L)),
        out_shape=(jax.ShapeDtypeStruct((n_tp, hd, half), BF16), jax.ShapeDtypeStruct((L, n_tp, rows_w, D), BF16)),
        in_specs=[ANY, ANY, ANY, VMEM, ANY, VMEM, VMEM, ANY, VMEM, ANY, ANY, ANY],
        out_specs=(ANY, ANY),
        scratch_shapes=[
            pltpu.VMEM((2, T, D), BF16), pltpu.VMEM((2, T, C), BF16), pltpu.VMEM((T, T), BF16), pltpu.VMEM((T, T), F32),
            pltpu.VMEM((4 * HP, D), BF16), pltpu.VMEM((C, 2 * D), BF16), pltpu.VMEM((T, 2 * HP), BF16), pltpu.VMEM((2 * HP, T), BF16),
            pltpu.VMEM((HP, T), BF16), pltpu.VMEM((hd, T), F32), pltpu.VMEM((2, T, QT), F32), pltpu.VMEM((2, hd, T), BF16),
            pltpu.VMEM((L, rows_w, D), BF16),
            dma((2,)), dma((2,)), dma, dma((4,)), dma, dma((4 * L,)), dma((L,)), dma((2, 2)), dma, dma((L,)), dma((L, n_tp, 2))],
        cost_estimate=pl.CostEstimate(flops=2 * S * T * (D * 4 * HP + 2 * T * 256 + 2 * C * D), bytes_accessed=S * T * (D + C) * 2, transcendentals=S * T * T),
        compiler_params=pltpu.CompilerParams(collective_id=0, has_side_effects=True, vmem_limit_bytes=60 << 20),
        name="block0",
    )(x, cond, pair_bias, mask_row, wq, brow, asc, aw, ab, wo, wup, wdn)


def _transition(dims, half_rows, gates, mod1, cn, o_v, act, wall, y_s, h_s, rows):
    D, n_tp, hd, hu = dims
    w_o = wall[:, 0:hd, :].reshape(n_tp * hd, D)
    o_t = o_v[:, :, rows].reshape(n_tp * hd, half_rows)
    t = _dot(o_t, w_o, 0, 0).astype(BF16).astype(F32)
    mid = (act[rows, :].astype(F32) + gates[:, :D] * t).astype(BF16).astype(F32)
    y_s[...] = mod1(mid)
    step = 4 * hu
    for j in range(n_tp * hu // step):
        dv = slice(4 * j, 4 * j + 4)
        u1 = _dot(y_s[...], wall[dv, hd:hd + hu, :].reshape(step, D), 1, 1)
        u2 = _dot(y_s[...], wall[dv, hd + hu:hd + 2 * hu, :].reshape(step, D), 1, 1)
        h_s[:, j * step:(j + 1) * step] = (u1 * _sig(u1) * u2).astype(BF16)
    r = _dot(h_s[...], wall[:, hd + 2 * hu:hd + 3 * hu, :].reshape(n_tp * hu, D)).astype(BF16).astype(F32)
    return (mid + gates[:, D:] * r).astype(BF16)


def _block1_kernel(dims, o0_hbm, act_hbm, cond_hbm, wg_hbm, zw_ref, zb_ref, asc_ref, aw_hbm, ab_ref, bias_hbm, mask_ref, wq_hbm, brow_ref,
                   a_out, o_hbm,
                   o_v, act, cond, wall, aw_s, y_s, h_s, xg, bias_v, bt, w_s, k_s, qt_s, vt_s, gt_s, lg, o_s,
                   l_sem, q_sem, x_send, x_recv, o_send, o_recv):
    S, T, D, C, n_tp, hd, hu = dims
    p = Place(n_tp)
    entered = p.enter(True)
    R = S * T // n_tp
    row0 = p.me * R
    srcs = [(cond_hbm.at[pl.ds(row0, R), :], cond), (o0_hbm, o_v), (act_hbm.at[pl.ds(row0, R), :], act), (wg_hbm.at[0], wall),
            (aw_hbm.at[0, 1], aw_s.at[0]), (aw_hbm.at[1, 0], aw_s.at[1]), (bias_hbm.at[1, 0], bias_v)]
    cps = [pltpu.make_async_copy(a, b, l_sem.at[i]) for i, (a, b) in enumerate(srcs)]
    for cp in cps:
        cp.start()
    w_s[...] = jnp.zeros_like(w_s)
    qt_s[HP:, :] = jnp.zeros((HP, T), BF16)
    order = (1, 0, 2, 3)
    wq = [pltpu.make_async_copy(wq_hbm.at[1, f], w_s.at[i * HP:i * HP + hd, :], q_sem.at[i]) for i, f in enumerate(order)]
    for cp in wq:
        cp.start()
    for i in (0, 4, 5, 1, 2, 3):
        cps[i].wait()

    def view(b, ch):
        return xg.at[pl.ds(b * R + ch * (R // 2), R // 2), :]

    ring = Ring(p, view, x_recv, x_send, 2)
    tile = R // 2
    for ch in range(2):
        rows = pl.ds(ch * tile, tile)
        cb = cond[rows, :]
        cn = _ln(cb.astype(F32))
        gates = _sig(_dot(cb, zw_ref[0]) + zb_ref[0:1, :])
        mod1 = lambda mid: _ada(mid, cn, asc_ref[0, 1:2, :], aw_s[0], ab_ref[0, 1:2, :])
        new = _transition((D, n_tp, hd, hu), tile, gates, mod1, cn, o_v, act, wall, y_s, h_s, rows)
        a_out[rows, :] = new
        xg[pl.ds(row0 + ch * tile, tile), :] = _ada(new.astype(F32), cn, asc_ref[1, 0:1, :], aw_s[1], ab_ref[1, 0:1, :])
        if ch == 0:
            entered()
        ring.own(ch)
    cps[6].wait()
    _load_bias(bias_v, mask_ref, bt)
    for cp in wq:
        cp.wait()
    ex = Exchange(p, o_s, o_hbm, o_send, o_recv)
    turn = 1 - 2 * p.c

    def sample_of(j):
        h = (j + 1) // 2
        return lax.rem(p.z + S + turn * (1 - 2 * lax.rem(j, 2)) * h, S)

    def step(j, _):
        slot = lax.rem(j, 2)
        ring.service(j // 2 + 1, lax.rem(j, 2))

        @pl.when(j >= 1)
        def _():
            ex.start(sample_of(j - 1), 1 - slot)

        s = sample_of(j)
        for ch in range(2):
            ring.wait(s * 2 + (1 - p.c), ch)

        def x_rows(i, t):
            return xg[pl.ds(pl.multiple_of(s * T, T) + i * t, t), :]

        at = Attend(n_tp, hd, w_s, brow_ref[1:2, :], bt, k_s, qt_s, vt_s, gt_s, lg, o_s, x_rows)
        at.project()

        @pl.when(j >= 2)
        def _():
            ex.sent(sample_of(j - 2), slot)

        at.attend(slot)
        return 0

    lax.fori_loop(0, S, step, 0)
    ex.start(sample_of(S - 1), (S - 1) % 2)
    ex.sent(sample_of(S - 2), S % 2)
    ex.sent(sample_of(S - 1), (S - 1) % 2)
    ring.drain(xg.at[0:(n_tp - 1) * R, :])
    ex.arrived()


def _block1(o0, act, cond, wg, zw, zb, asc, aw, ab, pair_bias, mask_row, wq, brow):
    n_tp, hd, R = o0.shape
    D = act.shape[-1]
    C = cond.shape[-1]
    S = n_tp // 2
    T = 2 * R
    hu = (wg.shape[2] - hd) // 3
    dma = pltpu.SemaphoreType.DMA
    return pl.pallas_call(
        functools.partial(_block1_kernel, (S, T, D, C, n_tp, hd, hu)),
        out_shape=(jax.ShapeDtypeStruct((R, D), BF16), jax.ShapeDtypeStruct((n_tp, hd, R), BF16)),
        in_specs=[ANY, ANY, ANY, ANY, VMEM, VMEM, VMEM, ANY, VMEM, ANY, VMEM, ANY, VMEM],
        out_specs=(VMEM, ANY),
        scratch_shapes=[
            pltpu.VMEM((n_tp, hd, R), BF16), pltpu.VMEM((R, D), BF16), pltpu.VMEM((R, C), BF16), pltpu.VMEM(wg.shape[1:], BF16),
            pltpu.VMEM((2, C, 2 * D), BF16), pltpu.VMEM((R // 2, D), BF16), pltpu.VMEM((R // 2, n_tp * hu), BF16),
            pltpu.VMEM((S * T, D), BF16), pltpu.VMEM((T, T), BF16), pltpu.VMEM((T, T), F32),
            pltpu.VMEM((4 * HP, D), BF16), pltpu.VMEM((T, 2 * HP), BF16), pltpu.VMEM((2 * HP, T), BF16),
            pltpu.VMEM((HP, T), BF16), pltpu.VMEM((hd, T), F32), pltpu.VMEM((2, T, QT), F32), pltpu.VMEM((2, hd, T), BF16),
            dma((7,)), dma((4,)), dma, dma((n_tp, 2)), dma((2, 2)), dma],
        cost_estimate=pl.CostEstimate(flops=2 * S * T * (D * 4 * HP + 2 * T * 256), bytes_accessed=S * T * D * 2, transcendentals=S * T * T),
        compiler_params=pltpu.CompilerParams(collective_id=1, has_side_effects=True, vmem_limit_bytes=62 << 20),
        name="block1",
    )(o0, act, cond, wg, zw, zb, asc, aw, ab, pair_bias, mask_row, wq, brow)


def _last_kernel(dims, o_hbm, act_hbm, cond_hbm, wg_hbm, zw_ref, zb_ref, asc_ref, aw_hbm, ab_ref, out_hbm,
                 o_v, act, cond, wall, aw_s, y_s, h_s, new_s, l_sem, c_sem, x_send, x_recv):
    D, C, n_tp, hd, hu, R = dims
    p = Place(n_tp)
    entered = p.enter(False)
    row0 = p.me * R
    srcs = [(cond_hbm.at[pl.ds(row0, R), :], cond), (o_hbm, o_v), (act_hbm, act), (wg_hbm.at[1], wall), (aw_hbm.at[1, 1], aw_s)]
    cps = [pltpu.make_async_copy(a, b, l_sem.at[i]) for i, (a, b) in enumerate(srcs)]
    for cp in cps:
        cp.start()
    for i in (0, 4, 1, 2, 3):
        cps[i].wait()
    tile = R // 2

    def view(b, ch):
        return out_hbm.at[pl.ds(b * R + ch * tile, tile), :]

    ring = Ring(p, view, x_recv, x_send, 2)
    keep = []
    for ch in range(2):
        rows = pl.ds(ch * tile, tile)
        cb = cond[rows, :]
        cn = _ln(cb.astype(F32))
        gates = _sig(_dot(cb, zw_ref[1]) + zb_ref[1:2, :])
        mod1 = lambda mid: _ada(mid, cn, asc_ref[1, 1:2, :], aw_s[...], ab_ref[1, 1:2, :])
        new_s[rows, :] = _transition((D, n_tp, hd, hu), tile, gates, mod1, cn, o_v, act, wall, y_s, h_s, rows)
        if ch == 0:
            entered()
        ring.own(ch, new_s.at[ch * tile:(ch + 1) * tile, :])
        keep.append(pltpu.make_async_copy(new_s.at[ch * tile:(ch + 1) * tile, :], view(p.me, ch), c_sem.at[ch]))
        keep[-1].start()

    lax.fori_loop(0, p.nz, lambda e, _: (ring.service(e // 2 + 1, lax.rem(e, 2)), 0)[1], 0)

    def other(i, _):
        for ch in range(2):
            ring.wait(i * 2 + (1 - p.c), ch)
        return 0

    lax.fori_loop(0, p.nz, other, 0)
    ring.drain(out_hbm.at[0:(n_tp - 1) * R, :])
    for cp in keep:
        cp.wait()


def _last(o, act, cond, wg, zw, zb, asc, aw, ab):
    n_tp, hd, R = o.shape
    D = act.shape[-1]
    C = cond.shape[-1]
    hu = (wg.shape[2] - hd) // 3
    dma = pltpu.SemaphoreType.DMA
    return pl.pallas_call(
        functools.partial(_last_kernel, (D, C, n_tp, hd, hu, R)),
        out_shape=jax.ShapeDtypeStruct((n_tp * R, D), BF16),
        in_specs=[ANY, ANY, ANY, ANY, VMEM, VMEM, VMEM, ANY, VMEM],
        out_specs=ANY,
        scratch_shapes=[
            pltpu.VMEM((n_tp, hd, R), BF16), pltpu.VMEM((R, D), BF16), pltpu.VMEM((R, C), BF16), pltpu.VMEM(wg.shape[1:], BF16),
            pltpu.VMEM((C, 2 * D), BF16), pltpu.VMEM((R // 2, D), BF16), pltpu.VMEM((R // 2, n_tp * hu), BF16), pltpu.VMEM((R, D), BF16),
            dma((5,)), dma((2,)), dma, dma((n_tp, 2))],
        cost_estimate=pl.CostEstimate(flops=2 * R * D * (D + 3 * n_tp * hu + 4 * C), bytes_accessed=wg.size, transcendentals=R * D),
        compiler_params=pltpu.CompilerParams(collective_id=2, has_side_effects=True, vmem_limit_bytes=60 << 20),
        name="last",
    )(o, act, cond, wg, zw, zb, asc, aw, ab)


def solution(mesh):
    def shard_body(token_act, token_cond, pair_bias, token_mask, ada_scale, ada_w, ada_bias, zero_w, zero_b, w_qkvg, b_q, w_o, w_up, w_down):
        S, T, D = token_act.shape
        C = token_cond.shape[-1]
        hd = w_qkvg.shape[-1]
        L = pair_bias.shape[0]
        mask_row = token_mask.reshape(1, T)
        wq = jnp.transpose(w_qkvg, (0, 2, 3, 1))
        wup = jnp.transpose(w_up, (0, 2, 3, 1))
        brow = jnp.pad(b_q, ((0, 0), (HP, 3 * HP - hd)))
        aw = ada_w.reshape(L, 2, C, 2 * D)
        zw = zero_w.reshape(L, C, 2 * D)
        zb = zero_b.reshape(L, 2 * D)
        act = token_act.reshape(S * T, D)
        cond = token_cond.reshape(S * T, C)
        o0, wg = _block0(token_act, token_cond, pair_bias, mask_row, wq, brow, ada_scale, aw, ada_bias, w_o, wup, w_down)
        a1, o1 = _block1(o0, act, cond, wg, zw, zb, ada_scale, aw, ada_bias, pair_bias, mask_row, wq, brow)
        out = _last(o1, a1, cond, wg, zw, zb, ada_scale, aw, ada_bias)
        return out.reshape(S, T, D)

    everywhere = P()
    in_specs = (P('dp', None, None), P('dp', None, None), P(None, 'tp', None, None), P(None), everywhere, everywhere, everywhere, everywhere, everywhere, P(None, None, None, 'tp'), P(None, 'tp'), P(None, 'tp', None), P(None, None, None, 'tp'), P(None, 'tp', None))
    return jax.shard_map(shard_body, mesh=mesh, in_specs=in_specs, out_specs=P('dp', None, None), check_vma=False)
```

time: 1030 us -> 310 us (0.30)
  waiting for transfers between devices: 458 us -> 0 us
  matrix products: 329 us -> 0 us
  Pallas kernels: 0 us -> 279 us
  other arithmetic: 193 us -> 0 us
  between operations: 14.1 us -> 0.03 us
    psum x4 -> x0, waiting for transfers between devices: 458 us -> none  [the longest x2 249 us: shard_body(): trans_out = lax.psum(trans_part, 'tp').astype(jnp.float32)]
    pallas_call x0 -> x3, Pallas kernels: none -> 279 us  [the longest x1 108 us: _block0(): pl.pallas_call(functools.partial(_block0_kernel, (S, T, D, C, n_tp, hd, h...]
    dot_general x42 -> x0, matrix products: 258 us -> none  [the longest x4 104 us: ada_norm(): jnp.einsum('rc,cgd->rgd', cond_in, weight, preferred_element_type=jnp.flo...]
    reduce_sum x26 -> x0, other arithmetic: 124 us -> none  [the longest x5 76.2 us: layer_norm(): row_mean = jnp.mean(values_in, axis=-1, keepdims=True)]
    unnamed x4 -> x0, matrix products: 71.8 us -> none
    convert_element_type x5 -> x0, other arithmetic: 60.6 us -> none  [the longest x1 24.8 us: ada_norm(): (jax.nn.sigmoid(modulation[:, 0] + bias_vec) * layer_norm(act_f32) + modu...]
    reshape x0 -> x2, local copies, waits for them, and re-layouts: none -> 17.5 us  [the longest x1 11.2 us: shard_body(): aw = ada_w.reshape(L, 2, C, 2 * D)]
    slice x10 -> x0, local copies, waits for them, and re-layouts: 14.8 us -> none  [the longest x1 4.34 us: shard_body(): zero_w[layer_idx]]
  transfers between devices with their start and end apart: 4 -> 0, of which waited for: 4 -> 0; matrix products, arithmetic and copies ran while one was open for 15% -> 0% of each run, Pallas kernels for 0% -> 0%
where the time goes in v2:
time: 310 us; the launch traced here: 309 us
  Pallas kernels  279 us (90%)
  local copies, waits for them, and re-layouts  30.6 us (10%)
    pallas_call x1, Pallas kernels, _block0(): pl.pallas_call(functools.partial(_block0_kernel, (S, T, D, C, n_tp, hd, h...  108 us
    pallas_call x1, Pallas kernels, _block1(): pl.pallas_call(functools.partial(_block1_kernel, (S, T, D, C, n_tp, hd, h...  96.1 us
    pallas_call x1, Pallas kernels, _last(): pl.pallas_call(functools.partial(_last_kernel, (D, C, n_tp, hd, hu, R)),...  74.4 us
    unnamed x2, local copies, waits for them, and re-layouts  11.8 us
    reshape x1, local copies, waits for them, and re-layouts, shard_body(): aw = ada_w.reshape(L, 2, C, 2 * D)  11.2 us
    reshape x1, local copies, waits for them, and re-layouts, shard_body(): zw = zero_w.reshape(L, C, 2 * D)  6.29 us

profile of v2, /device:TPU:21, one launch (start us, length us, event | category | flops | bytes accessed | tf_op | source)
XLA Modules:
  0.0 309.3 jit_solution(11925083822755663700)
XLA Ops:
  0.0 1.3 pad.4.brow_ref
  1.3 1.3 copy.15
  2.7 6.3 %reshape.25.zw_ref = bf16[2,384,1536]{2,1,0:T(8,128)(2,1)} reshape(bf16[2,384,2,768]{3,2,1,0:T(2,128)(2,1)} %param.21) | data formatting | bytes 4718592 | tf_op jit(solution)/shard_map/reshape | solution.py:540
  8.9 11.2 %reshape.22.aw_hbm = bf16[2,2,384,1536]{3,2,1,0:T(8,128)(2,1)} reshape(bf16[2,2,384,2,768]{4,3,2,1,0:T(2,128)(2,1)} %param.19) | data formatting | bytes 9437184 | tf_op jit(solution)/shard_map/reshape | solution.py:539
  20.2 108.1 %block0.1 = (bf16[16,48,512]{2,1,0:T(8,128)(2,1)}, bf16[2,16,336,768]{3,2,1,0:T(8,128)(2,1)}) custom-call(bf16[8,1024,768]{2,1,0:T(8,128)(2,1)} %x_hbm.1, bf16[8,1024,384]{2,1,0:T(8,128)(2,1)} %cond_hbm.1, bf16[2,1,1024,1024]{3,2,1,0:T(8,128)(2,1)} %bias_hbm.3, s32[1,1024]{1,0:T(1,128)} %bitcast.17, bf16[2,4,48,768]{3,2,1,0:T(8,128)(2,1)} %bitcast.12, ...), custom_call_target="tpu_custom_call" | custom-call | flops 21474836480 | bytes 18874368 | tf_op jit(solution)/shard_map/block0/pallas_call | solution.py:319
  128.3 96.1 %block1.1 = (bf16[512,768]{1,0:T(8,128)(2,1)}, bf16[16,48,512]{2,1,0:T(8,128)(2,1)}) custom-call(bf16[16,48,512]{2,1,0:T(8,128)(2,1)} %get-tuple-element.9.o0_hbm, bf16[8192,768]{1,0:T(8,128)(2,1)} %bitcast.11, bf16[8192,384]{1,0:T(8,128)(2,1)} %bitcast.9, bf16[2,16,336,768]{3,2,1,0:T(8,128)(2,1)} %get-tuple-element.10.wg_hbm, ...), custom_call_target="tpu_custom_call" | custom-call | flops 11811160064 | bytes 12582912 | tf_op jit(solution)/shard_map/block1/pallas_call | solution.py:445
  224.4 74.4 %last.1 = bf16[8192,768]{1,0:T(8,128)(2,1)} custom-call(bf16[16,48,512]{2,1,0:T(8,128)(2,1)} %get-tuple-element.11.o_hbm, bf16[512,768]{1,0:T(8,128)(2,1)} %get-tuple-element.12.act_hbm, bf16[8192,384]{1,0:T(8,128)(2,1)} %bitcast.10, bf16[2,16,336,768]{3,2,1,0:T(8,128)(2,1)} %get-tuple-element.10.wg_hbm, bf16[2,384,1536]{2,1,0:T(8,128)(2,1)} %reshape.25.zw_ref, ...), custom_call_target="tpu_custom_call" | custom-call | flops 5435817984 | bytes 8257536 | tf_op jit(solution)/shard_map/last/pallas_call | solution.py:514
  298.8 10.5 %copy.17 = bf16[8,1024,768]{2,1,0:T(8,128)(2,1)} copy(bf16[8,1024,768]{2,1,0:T(8,128)(2,1)} %bitcast.8) | data formatting | bytes 25165824

commit v3 on v2

v3 whole, which is shorter than its diff:
```python
import functools
import math

import jax
import jax.numpy as jnp
from jax import lax
from jax.experimental import pallas as pl
from jax.experimental.pallas import tpu as pltpu
from jax.sharding import PartitionSpec as P

LN_EPS = 1e-5
LOG2E = 1.4426950408889634
MESH = pl.DeviceIdType.MESH
BF16 = jnp.bfloat16
F32 = jnp.float32
HP = 64
QT = 256
ANY = pl.BlockSpec(memory_space=pl.ANY)
VMEM = pl.BlockSpec(memory_space=pltpu.VMEM)
VM0, VM1, VM2 = 40 << 20, 40 << 20, 8 << 20


def _ln(x):
    mean = jnp.mean(x, axis=-1, keepdims=True)
    cen = x - mean
    var = jnp.mean(cen * cen, axis=-1, keepdims=True)
    return cen * lax.rsqrt(var + LN_EPS)


def _sig(x):
    return 0.5 * jnp.tanh(0.5 * x) + 0.5


def _dot(a, b, ca=1, cb=0):
    return lax.dot_general(a, b, (((ca,), (cb,)), ((), ())), preferred_element_type=F32)


def _ada(x_f32, cond_normed, scale, w, bias):
    d = x_f32.shape[-1]
    mod = _dot((cond_normed * scale).astype(BF16), w)
    return (_sig(mod[:, :d] + bias) * _ln(x_f32) + mod[:, d:]).astype(BF16)


class Place:
    def __init__(self, n_tp, n_dp):
        self.n = n_tp
        self.n_dp = n_dp
        self.col = lax.axis_index("dp")
        self.nz = n_tp // 2
        self.me = lax.axis_index("tp")
        self.z = self.me // 2
        self.c = lax.rem(self.me, 2)
        self.partner = self.z * 2 + (1 - self.c)

    def at(self, off):
        return lax.rem(self.z + off + self.nz, self.nz) * 2 + self.c

    def column(self, i):
        return lax.rem(self.col + i, self.n_dp)

    def enter(self, everyone):
        barrier = pltpu.get_barrier_semaphore()
        if everyone:
            peers = [{"tp": lax.rem(self.me + i, self.n)} for i in range(1, self.n)]
            peers += [{"dp": self.column(i), "tp": self.me} for i in range(1, self.n_dp)]
        else:
            peers = [{"tp": t} for t in (self.at(1), self.at(-1), self.partner)]
        for peer in peers:
            pl.semaphore_signal(barrier, inc=1, device_id=peer, device_id_type=MESH)
        return lambda: pl.semaphore_wait(barrier, len(peers))


class Ring:
    def __init__(self, place, view, recv_sem, send_sem, n_chunk):
        self.p, self.view, self.recv, self.send, self.n_chunk = place, view, recv_sem, send_sem, n_chunk
        self.far = place.nz // 2

    def _push(self, b, ch, dst, src=None):
        v = self.view(b, ch)
        pltpu.make_async_remote_copy(
            src_ref=v if src is None else src, dst_ref=v, send_sem=self.send, recv_sem=self.recv.at[b, ch],
            device_id={"tp": dst}, device_id_type=MESH).start()

    def own(self, ch, src=None):
        p = self.p
        self._push(p.me, ch, p.at(1), src)
        self._push(p.me, ch, p.at(-1), src)
        self._push(p.me, ch, p.partner, src)

    def wait(self, b, ch):
        v = self.view(b, ch)
        pltpu.make_async_copy(v, v, self.recv.at[b, ch]).wait()

    def service(self, h, ch):
        p = self.p
        for sign, core in ((1, 0), (-1, 1)):
            b = p.at(-sign * h)

            @pl.when((h < self.far) | (p.c == core))
            def _():
                self.wait(b, ch)

                @pl.when((h < self.far - 1) | ((h == self.far - 1) & (p.c == core)))
                def _():
                    self._push(b, ch, p.at(sign))

                self._push(b, ch, p.partner)

    def drain(self, whole):
        pltpu.make_async_copy(whole, whole, self.send).wait()


class Cross:
    def __init__(self, place, buf, lo, hi, recv_sem, near_sem, far_sem):
        self.p, self.buf, self.lo, self.hi = place, buf, lo, hi
        self.recv, self.near, self.far_sem = recv_sem, near_sem, far_sem
        self.far = place.nz // 2

    def _view(self, b):
        return self.buf.at[b, self.lo:self.hi, :]

    def _push(self, b, dst, sem, src=None):
        v = self._view(b)
        pltpu.make_async_remote_copy(
            src_ref=v if src is None else src, dst_ref=v, send_sem=sem, recv_sem=self.recv.at[b],
            device_id=dst, device_id_type=MESH).start()

    def _mine(self, b):
        return lax.rem(b, self.p.n_dp) == self.p.col

    def own(self, src):
        p = self.p

        @pl.when(self._mine(p.me))
        def _():
            self._push(p.me, {"tp": p.at(1)}, self.far_sem.at[p.z], src)
            self._push(p.me, {"tp": p.at(-1)}, self.far_sem.at[p.z], src)

        self._push(p.me, {"tp": p.partner}, self.near, src)

    def wait(self, b):
        v = self._view(b)
        pltpu.make_async_copy(v, v, self.recv.at[b]).wait()

    def _each(self, h, body):
        p = self.p
        for sign, core in ((1, 0), (-1, 1)):
            b = p.at(-sign * h)

            @pl.when((h < self.far) | (p.c == core))
            def _():
                body(b, sign, (h < self.far - 1) | ((h == self.far - 1) & (p.c == core)))

    def along(self, h):
        p = self.p

        def body(b, sign, onward):
            @pl.when(self._mine(b))
            def _():
                self.wait(b)

                @pl.when(onward)
                def _():
                    self._push(b, {"tp": p.at(sign)}, self.far_sem.at[b // 2])

                for i in range(1, p.n_dp):
                    self._push(b, {"dp": p.column(i), "tp": p.me}, self.far_sem.at[b // 2])
                self._push(b, {"tp": p.partner}, self.near)

        self._each(h, body)

    def across(self, h):
        p = self.p

        def body(b, sign, onward):
            @pl.when(jnp.logical_not(self._mine(b)))
            def _():
                self.wait(b)
                self._push(b, {"tp": p.partner}, self.near)

        self._each(h, body)

    def finish(self):
        p = self.p

        def blocks(k, sem):
            v = self.buf.at[0:k, self.lo:self.hi, :]
            pltpu.make_async_copy(v, v, sem).wait()

        def other(i, _):
            self.wait(i * 2 + (1 - p.c))
            return 0

        lax.fori_loop(0, p.nz, other, 0)
        blocks(p.nz, self.near)

        @pl.when(self._mine(p.me))
        def _():
            blocks(2, self.far_sem.at[p.z])

        def body(b, sign, onward):
            @pl.when(self._mine(b))
            def _():
                @pl.when(onward)
                def _():
                    blocks(p.n_dp, self.far_sem.at[b // 2])

                if p.n_dp > 1:
                    @pl.when(jnp.logical_not(onward))
                    def _():
                        blocks(p.n_dp - 1, self.far_sem.at[b // 2])

        def hop(h, _):
            self._each(h, body)
            return 0

        lax.fori_loop(1, self.far + 1, hop, 0)


class Attend:
    def __init__(self, n_tp, hd, w, brow, bt, k_s, qt_s, vt_s, gt_s, lg, o_s, x_rows):
        self.__dict__.update(locals())
        self.T = bt.shape[0]

    def project(self):
        T, hd = self.T, self.hd
        tile = QT
        for i in range(T // tile):
            rows = pl.ds(i * tile, tile)
            res = _dot(self.x_rows(i, tile), self.w[...], 1, 1) + self.brow
            self.k_s[rows, :] = res[:, :2 * HP].astype(BF16)
            rest = res.T
            self.qt_s[0:HP, rows] = rest[HP:2 * HP].astype(BF16)
            ones = lax.broadcasted_iota(jnp.int32, (HP, tile), 0) == hd
            self.vt_s[:, rows] = jnp.where(ones, 1.0, rest[2 * HP:3 * HP]).astype(BF16)
            self.gt_s[:, rows] = _sig(rest[3 * HP:3 * HP + hd])

    def attend(self, slot):
        T, hd = self.T, self.hd
        n = T // QT
        c1 = LOG2E / math.sqrt(hd)

        def scores(i):
            cols = pl.ds(i * QT, QT)
            logits = _dot(self.k_s[...], self.qt_s[:, cols]) * c1 + self.bt[:, cols]
            self.lg[i % 2] = logits
            return jnp.max(logits, axis=0, keepdims=True)

        top = scores(0)
        for i in range(n):
            cols = pl.ds(i * QT, QT)
            nxt = scores(i + 1) if i + 1 < n else None
            probs = jnp.exp2(self.lg[i % 2] - top).astype(BF16)
            mixed = _dot(self.vt_s[...], probs)
            self.o_s[slot, :, cols] = (self.gt_s[:, cols] * (mixed[:hd] / mixed[hd:hd + 1])).astype(BF16)
            top = nxt


def _load_bias(bias_v, mask_ref, bt):
    T = bt.shape[0]
    mask_add = (mask_ref[...].astype(F32) - 1.0) * 1e9

    def step(i, _):
        r = pl.multiple_of(i * 128, 128)
        rows = (bias_v[pl.ds(r, 128), :].astype(F32) + mask_add) * LOG2E
        bt[:, pl.ds(r, 128)] = rows.T
        return 0

    lax.fori_loop(0, T // 128, step, 0)


class Exchange:
    def __init__(self, place, o_s, o_hbm, send_sem, recv_sem):
        self.p, self.o_s, self.o_hbm, self.send, self.recv = place, o_s, o_hbm, send_sem, recv_sem
        self.half = o_s.shape[-1] // 2

    def _each(self, sample, slot, remote, local):
        p = self.p
        for c in range(2):
            dst = sample * 2 + c
            src = self.o_s.at[slot, :, pl.ds(c * self.half, self.half)]
            cp = pltpu.make_async_remote_copy(
                src_ref=src, dst_ref=self.o_hbm.at[p.me], send_sem=self.send.at[slot, c], recv_sem=self.recv,
                device_id={"tp": dst}, device_id_type=MESH)

            @pl.when(dst != p.me)
            def _():
                remote(cp)

            @pl.when(dst == p.me)
            def _():
                local(pltpu.make_async_copy(src, self.o_hbm.at[p.me], self.send.at[slot, c]))

    def start(self, sample, slot):
        self._each(sample, slot, lambda cp: cp.start(), lambda cp: cp.start())

    def sent(self, sample, slot):
        self._each(sample, slot, lambda cp: cp.wait_send(), lambda cp: cp.wait())

    def arrived(self):
        rest = self.o_hbm.at[0:self.p.n - 1]
        pltpu.make_async_copy(rest, rest, self.recv).wait()


def _bias_row(bq, hd):
    return jnp.concatenate([jnp.zeros((1, HP), F32), bq, jnp.zeros((1, 3 * HP - hd), F32)], axis=1)


def _flat(raw):
    c, two, d = raw.shape
    return raw[...].reshape(c, two * d)


def _block0_kernel(dims, x_hbm, cond_hbm, bias_hbm, mask_ref, wq_hbm, bq_ref, asc_ref, aw_hbm, ab_ref, zw_hbm, zb_ref, wo_hbm, wup_hbm, wdn_hbm,
                   o_out, wg, gate_out, mod_out, nxt_out,
                   xbuf, cbuf, bias_v, bt, w_s, raw, aw_s, k_s, qt_s, vt_s, gt_s, lg, o_s, wst, cond,
                   ld_sem, cd_sem, b_sem, q_sem, a_sem, st_sem, o_send, o_recv, w_send, w_recv, c_near, c_far, c_recv):
    S, T, D, C, n_tp, n_dp, hd, hu = dims
    p = Place(n_tp, n_dp)
    entered = p.enter(True)
    rows_w = hd + 3 * hu
    cut = hd + hu
    stage = []
    for src, lo, hi in ((wo_hbm.at[0], 0, hd), (wup_hbm.at[0, 0], hd, cut), (wup_hbm.at[0, 1], cut, hd + 2 * hu),
                        (wdn_hbm.at[0], hd + 2 * hu, rows_w)):
        stage.append(pltpu.make_async_copy(src, wst.at[lo:hi, :], st_sem.at[len(stage)]))
    for cp in stage:
        cp.start()
    sign = 1 - 2 * p.c
    R = S * T // n_tp

    def sample_of(k):
        return lax.rem(p.z + S + sign * (k + 1), S)

    def loads(k, slot):
        s = sample_of(k)
        return [pltpu.make_async_copy(x_hbm.at[s], xbuf.at[slot], ld_sem.at[slot]),
                pltpu.make_async_copy(cond_hbm.at[s], cbuf.at[slot], cd_sem.at[slot])]

    raws = [pltpu.make_async_copy(aw_hbm.at[0, 0], raw.at[0], a_sem.at[0]), pltpu.make_async_copy(zw_hbm.at[0], raw.at[1], a_sem.at[1]),
            pltpu.make_async_copy(aw_hbm.at[0, 1], raw.at[2], a_sem.at[2]), pltpu.make_async_copy(aw_hbm.at[1, 0], raw.at[0], a_sem.at[0])]
    bias_cp = pltpu.make_async_copy(bias_hbm.at[0, 0], bias_v, b_sem)
    bias_cp.start()
    raws[0].start()
    for cp in loads(0, 0):
        cp.start()
    w_s[...] = jnp.zeros_like(w_s)
    qt_s[HP:, :] = jnp.zeros((HP, T), BF16)
    order = (1, 0, 2, 3)
    wq = [pltpu.make_async_copy(wq_hbm.at[0, f], w_s.at[i * HP:i * HP + hd, :], q_sem.at[i]) for i, f in enumerate(order)]
    for cp in wq:
        cp.start()
    for cp in stage:
        cp.wait()
    for cp in wq:
        cp.wait()
    for r in (1, 2):
        raws[r].start()
    cond_cp = pltpu.make_async_copy(cond_hbm.at[p.z, pl.ds(p.c * R, R), :], cond, b_sem)
    entered()
    ring = Ring(p, lambda b, ch: wg.at[b, 0:cut, :], w_recv, w_send, 1)
    cross = Cross(p, wg, cut, rows_w, c_recv, c_near, c_far)
    ring.own(0, wst.at[0:cut, :])
    cross.own(wst.at[cut:rows_w, :])
    bias_cp.wait()
    _load_bias(bias_v, mask_ref, bt)
    cond_cp.start()
    raws[0].wait()
    aw_s[...] = _flat(raw.at[0])
    ex = Exchange(p, o_s, o_out, o_send, o_recv)
    brow = _bias_row(bq_ref[0:1, :], hd)

    def step(k, _):
        slot = lax.rem(k, 2)

        @pl.when(k + 1 < S)
        def _():
            for cp in loads(k + 1, 1 - slot):
                cp.start()

        for cp in loads(k, slot):
            cp.wait()

        def x_rows(i, tile):
            rows = pl.ds(i * tile, tile)
            cn = _ln(cbuf[slot, rows, :].astype(F32))
            return _ada(xbuf[slot, rows, :].astype(F32), cn, asc_ref[0, 0:1, :], aw_s[...], ab_ref[0, 0:1, :])

        at = Attend(n_tp, hd, w_s, brow, bt, k_s, qt_s, vt_s, gt_s, lg, o_s, x_rows)
        at.project()

        @pl.when(k >= 1)
        def _():
            ex.start(sample_of(k - 1), 1 - slot)

        @pl.when((k >= 1) & (k <= p.nz // 2))
        def _():
            ring.service(k, 0)
            cross.along(k)

        @pl.when((k >= 3) & (k <= p.nz // 2 + 2))
        def _():
            cross.across(k - 2)

        @pl.when(k >= 2)
        def _():
            ex.sent(sample_of(k - 2), slot)

        at.attend(slot)
        return 0

    lax.fori_loop(0, S, step, 0)
    ex.start(sample_of(S - 1), (S - 1) % 2)
    raws[3].start()
    wg[p.me] = wst[...]
    cond_cp.wait()
    cn = _ln(cond[...].astype(F32))
    raws[1].wait()
    aw_s[...] = _flat(raw.at[1])
    gate_out[...] = _dot(cond[...], aw_s[...])
    for half in range(2):
        cols = slice(half * D, (half + 1) * D)
        gate_out[:, cols] = _sig(gate_out[:, cols] + zb_ref[0, half:half + 1, :])
    for src, cp, l, j, out in ((2, raws[2], 0, 1, mod_out), (0, raws[3], 1, 0, nxt_out)):
        cp.wait()
        aw_s[...] = _flat(raw.at[src])
        out[...] = _dot((cn * asc_ref[l, j:j + 1, :]).astype(BF16), aw_s[...])
        out[:, :D] = _sig(out[:, :D] + ab_ref[l, j:j + 1, :])
    ex.sent(sample_of(S - 2), S % 2)
    ex.sent(sample_of(S - 1), (S - 1) % 2)

    def other(i, _):
        ring.wait(i * 2 + (1 - p.c), 0)
        return 0

    lax.fori_loop(0, p.nz, other, 0)
    ring.drain(wg.at[0:n_tp - 1, 0:cut, :])
    cross.finish()
    ex.arrived()


def _block0(n_dp, x, cond, pair_bias, mask_row, wq, bq, asc, aw, ab, zw, zb, wo, wup, wdn):
    S, T, D = x.shape
    C = cond.shape[-1]
    _, _, hd, _ = wq.shape
    hu = wdn.shape[1]
    n_tp = S * 2
    rows_w = hd + 3 * hu
    R = T // 2
    dma = pltpu.SemaphoreType.DMA
    return pl.pallas_call(
        functools.partial(_block0_kernel, (S, T, D, C, n_tp, n_dp, hd, hu)),
        out_shape=(pltpu.VMEM((n_tp, hd, R), BF16), pltpu.VMEM((n_tp, rows_w, D), BF16),
                   pltpu.VMEM((R, 2 * D), F32), pltpu.VMEM((R, 2 * D), F32), pltpu.VMEM((R, 2 * D), F32)),
        in_specs=[ANY, ANY, ANY, VMEM, ANY, VMEM, VMEM, ANY, VMEM, ANY, VMEM, ANY, ANY, ANY],
        out_specs=(VMEM,) * 5,
        scratch_shapes=[
            pltpu.VMEM((2, T, D), BF16), pltpu.VMEM((2, T, C), BF16), pltpu.VMEM((T, T), BF16), pltpu.VMEM((T, T), F32),
            pltpu.VMEM((4 * HP, D), BF16), pltpu.VMEM((3, C, 2, D), BF16), pltpu.VMEM((C, 2 * D), BF16),
            pltpu.VMEM((T, 2 * HP), BF16), pltpu.VMEM((2 * HP, T), BF16),
            pltpu.VMEM((HP, T), BF16), pltpu.VMEM((hd, T), F32), pltpu.VMEM((2, T, QT), F32), pltpu.VMEM((2, hd, T), BF16),
            pltpu.VMEM((rows_w, D), BF16), pltpu.VMEM((R, C), BF16),
            dma((2,)), dma((2,)), dma, dma((4,)), dma((3,)), dma((4,)), dma((2, 2)), dma, dma, dma((n_tp, 1)),
            dma, dma((S,)), dma((n_tp,))],
        cost_estimate=pl.CostEstimate(flops=2 * S * T * (D * 4 * HP + 2 * T * 256 + 2 * C * D), bytes_accessed=S * T * (D + C) * 2, transcendentals=S * T * T),
        compiler_params=pltpu.CompilerParams(collective_id=0, has_side_effects=True, vmem_limit_bytes=VM0),
        name="block0",
    )(x, cond, pair_bias, mask_row, wq, bq, asc, aw, ab, zw, zb, wo, wup, wdn)


def _transition(dims, tile, gates, mod1, o_v, act, wall, y_s, h_s, rows):
    D, n_tp, hd, hu = dims
    w_o = wall[:, 0:hd, :].reshape(n_tp * hd, D)
    o_t = o_v[:, :, rows].reshape(n_tp * hd, tile)
    t = _dot(o_t, w_o, 0, 0).astype(BF16).astype(F32)
    mid = (act[rows, :].astype(F32) + gates[rows, :D] * t).astype(BF16).astype(F32)
    y_s[...] = (mod1[rows, :D] * _ln(mid) + mod1[rows, D:]).astype(BF16)
    step = 4 * hu
    for j in range(n_tp * hu // step):
        dv = slice(4 * j, 4 * j + 4)
        u1 = _dot(y_s[...], wall[dv, hd:hd + hu, :].reshape(step, D), 1, 1)
        u2 = _dot(y_s[...], wall[dv, hd + hu:hd + 2 * hu, :].reshape(step, D), 1, 1)
        h_s[:, j * step:(j + 1) * step] = (u1 * _sig(u1) * u2).astype(BF16)
    r = _dot(h_s[...], wall[:, hd + 2 * hu:hd + 3 * hu, :].reshape(n_tp * hu, D)).astype(BF16).astype(F32)
    return (mid + gates[rows, D:] * r).astype(BF16)


def _block1_kernel(dims, o0, w0, gate0, mod0, nxt0, act_hbm, cond_hbm, zw_hbm, zb_ref, asc_ref, aw_hbm, ab_ref, bias_hbm, mask_ref, wq_hbm, bq_ref,
                   wo_hbm, wup_hbm, wdn_hbm,
                   w1, gate1, mod1, a_out, o_out, wg,
                   act, cond, raw, aw_s, y_s, h_s, xg, bias_v, bt, w_s, k_s, qt_s, vt_s, gt_s, lg, o_s, wst,
                   l_sem, q_sem, st_sem, wl_sem, x_send, x_recv, o_send, o_recv, c_near, c_far, c_recv):
    S, T, D, C, n_tp, n_dp, hd, hu = dims
    p = Place(n_tp, n_dp)
    entered = p.enter(True)
    R = S * T // n_tp
    row0 = p.me * R
    rows_w = hd + 3 * hu
    stage = []
    for src, lo, hi in ((wo_hbm.at[1], 0, hd), (wup_hbm.at[1, 0], hd, hd + hu), (wup_hbm.at[1, 1], hd + hu, hd + 2 * hu),
                        (wdn_hbm.at[1], hd + 2 * hu, rows_w)):
        stage.append(pltpu.make_async_copy(src, wst.at[lo:hi, :], st_sem.at[len(stage)]))
    for cp in stage:
        cp.start()
    srcs = [(act_hbm.at[pl.ds(row0, R), :], act), (cond_hbm.at[pl.ds(row0, R), :], cond), (bias_hbm.at[1, 0], bias_v),
            (zw_hbm.at[1], raw.at[0]), (aw_hbm.at[1, 1], raw.at[1])]
    cps = [pltpu.make_async_copy(a, b, l_sem.at[i]) for i, (a, b) in enumerate(srcs)]
    for cp in cps:
        cp.start()
    w_s[...] = jnp.zeros_like(w_s)
    qt_s[HP:, :] = jnp.zeros((HP, T), BF16)
    order = (1, 0, 2, 3)
    wq = [pltpu.make_async_copy(wq_hbm.at[1, f], w_s.at[i * HP:i * HP + hd, :], q_sem.at[i]) for i, f in enumerate(order)]
    for cp in wq:
        cp.start()
    for cp in stage:
        cp.wait()
    cross = Cross(p, wg, 0, rows_w, c_recv, c_near, c_far)
    keep = pltpu.make_async_copy(wst, wg.at[p.me], wl_sem)
    keep.start()
    entered()
    cross.own(wst)
    cps[0].wait()
    tile = R // 2
    ring = Ring(p, lambda b, ch: xg.at[pl.ds(b * R + ch * tile, tile), :], x_recv, x_send, 2)
    for ch in range(2):
        rows = pl.ds(ch * tile, tile)
        new = _transition((D, n_tp, hd, hu), tile, gate0, mod0, o0, act, w0, y_s, h_s, rows)
        a_out[rows, :] = new
        xg[pl.ds(row0 + ch * tile, tile), :] = (nxt0[rows, :D] * _ln(new.astype(F32)) + nxt0[rows, D:]).astype(BF16)
        ring.own(ch)
        cross.along(ch + 1)
    cps[2].wait()
    _load_bias(bias_v, mask_ref, bt)
    for cp in wq:
        cp.wait()
    ex = Exchange(p, o_s, o_out, o_send, o_recv)
    brow = _bias_row(bq_ref[1:2, :], hd)
    turn = 1 - 2 * p.c

    def sample_of(j):
        h = (j + 1) // 2
        return lax.rem(p.z + S + turn * (1 - 2 * lax.rem(j, 2)) * h, S)

    def step(j, _):
        slot = lax.rem(j, 2)
        ring.service(j // 2 + 1, lax.rem(j, 2))

        @pl.when(j <= p.nz // 2 - 3)
        def _():
            cross.along(j + 3)

        @pl.when((j >= 1) & (j <= p.nz // 2))
        def _():
            cross.across(j)

        @pl.when(j >= 1)
        def _():
            ex.start(sample_of(j - 1), 1 - slot)

        s = sample_of(j)
        for ch in range(2):
            ring.wait(s * 2 + (1 - p.c), ch)

        def x_rows(i, t):
            return xg[pl.ds(pl.multiple_of(s * T, T) + i * t, t), :]

        at = Attend(n_tp, hd, w_s, brow, bt, k_s, qt_s, vt_s, gt_s, lg, o_s, x_rows)
        at.project()

        @pl.when(j >= 2)
        def _():
            ex.sent(sample_of(j - 2), slot)

        at.attend(slot)

        @pl.when(j == 1)
        def _():
            cps[1].wait()
            cps[3].wait()
            aw_s[...] = _flat(raw.at[0])
            gate1[...] = _dot(cond[...], aw_s[...])
            for half in range(2):
                cols = slice(half * D, (half + 1) * D)
                gate1[:, cols] = _sig(gate1[:, cols] + zb_ref[1, half:half + 1, :])

        @pl.when(j == 3)
        def _():
            cps[4].wait()
            aw_s[...] = _flat(raw.at[1])
            cn = _ln(cond[...].astype(F32))
            mod1[...] = _dot((cn * asc_ref[1, 1:2, :]).astype(BF16), aw_s[...])
            mod1[:, :D] = _sig(mod1[:, :D] + ab_ref[1, 1:2, :])

        @pl.when(j == S - 2)
        def _():
            cross.finish()
            keep.wait()
            pltpu.make_async_copy(wg, w1, wl_sem).start()

        return 0

    lax.fori_loop(0, S, step, 0)
    ex.start(sample_of(S - 1), (S - 1) % 2)
    pltpu.make_async_copy(wg, w1, wl_sem).wait()
    ex.sent(sample_of(S - 2), S % 2)
    ex.sent(sample_of(S - 1), (S - 1) % 2)
    ring.drain(xg.at[0:(n_tp - 1) * R, :])
    ex.arrived()


def _block1(n_dp, o0, w0, gate0, mod0, nxt0, act, cond, zw, zb, asc, aw, ab, pair_bias, mask_row, wq, bq, wo, wup, wdn):
    n_tp, hd, R = o0.shape
    D = act.shape[-1]
    C = cond.shape[-1]
    S = n_tp // 2
    T = 2 * R
    hu = wdn.shape[1]
    rows_w = hd + 3 * hu
    dma = pltpu.SemaphoreType.DMA
    return pl.pallas_call(
        functools.partial(_block1_kernel, (S, T, D, C, n_tp, n_dp, hd, hu)),
        out_shape=(pltpu.VMEM((n_tp, rows_w, D), BF16), pltpu.VMEM((R, 2 * D), F32), pltpu.VMEM((R, 2 * D), F32),
                   pltpu.VMEM((R, D), BF16), pltpu.VMEM((n_tp, hd, R), BF16), pltpu.HBM((n_tp, rows_w, D), BF16)),
        in_specs=[VMEM, VMEM, VMEM, VMEM, VMEM, ANY, ANY, ANY, VMEM, VMEM, ANY, VMEM, ANY, VMEM, ANY, VMEM, ANY, ANY, ANY],
        out_specs=(VMEM, VMEM, VMEM, VMEM, VMEM, pl.BlockSpec(memory_space=pltpu.HBM)),
        input_output_aliases={1: 0, 2: 1, 3: 2},
        scratch_shapes=[
            pltpu.VMEM((R, D), BF16), pltpu.VMEM((R, C), BF16), pltpu.VMEM((2, C, 2, D), BF16), pltpu.VMEM((C, 2 * D), BF16),
            pltpu.VMEM((R // 2, D), BF16), pltpu.VMEM((R // 2, n_tp * hu), BF16),
            pltpu.VMEM((S * T, D), BF16), pltpu.VMEM((T, T), BF16), pltpu.VMEM((T, T), F32),
            pltpu.VMEM((4 * HP, D), BF16), pltpu.VMEM((T, 2 * HP), BF16), pltpu.VMEM((2 * HP, T), BF16),
            pltpu.VMEM((HP, T), BF16), pltpu.VMEM((hd, T), F32), pltpu.VMEM((2, T, QT), F32), pltpu.VMEM((2, hd, T), BF16),
            pltpu.VMEM((rows_w, D), BF16),
            dma((5,)), dma((4,)), dma((4,)), dma, dma, dma((n_tp, 2)), dma((2, 2)), dma, dma, dma((S,)), dma((n_tp,))],
        cost_estimate=pl.CostEstimate(flops=2 * S * T * (D * 4 * HP + 2 * T * 256), bytes_accessed=S * T * D * 2, transcendentals=S * T * T),
        compiler_params=pltpu.CompilerParams(collective_id=1, has_side_effects=True, vmem_limit_bytes=VM1),
        name="block1",
    )(o0, w0, gate0, mod0, nxt0, act, cond, zw, zb, asc, aw, ab, pair_bias, mask_row, wq, bq, wo, wup, wdn)


def _last_kernel(dims, o_v, act, wall, gate, mod, out, y_s, h_s, x_send, x_recv):
    D, n_tp, n_dp, hd, hu, R = dims
    p = Place(n_tp, n_dp)
    entered = p.enter(False)
    tile = R // 2
    ring = Ring(p, lambda b, ch: out.at[pl.ds(b * R + ch * tile, tile), :], x_recv, x_send, 2)
    for ch in range(2):
        rows = pl.ds(ch * tile, tile)
        out[pl.ds(p.me * R + ch * tile, tile), :] = _transition((D, n_tp, hd, hu), tile, gate, mod, o_v, act, wall, y_s, h_s, rows)
        if ch == 0:
            entered()
        ring.own(ch)

    lax.fori_loop(0, p.nz, lambda e, _: (ring.service(e // 2 + 1, lax.rem(e, 2)), 0)[1], 0)

    def other(i, _):
        for ch in range(2):
            ring.wait(i * 2 + (1 - p.c), ch)
        return 0

    lax.fori_loop(0, p.nz, other, 0)
    ring.drain(out.at[0:(n_tp - 1) * R, :])


def _last(n_dp, o, act, w1, gate, mod):
    n_tp, hd, R = o.shape
    D = act.shape[-1]
    hu = (w1.shape[1] - hd) // 3
    dma = pltpu.SemaphoreType.DMA
    return pl.pallas_call(
        functools.partial(_last_kernel, (D, n_tp, n_dp, hd, hu, R)),
        out_shape=pltpu.VMEM((n_tp * R, D), BF16),
        in_specs=[VMEM] * 5, out_specs=VMEM,
        scratch_shapes=[pltpu.VMEM((R // 2, D), BF16), pltpu.VMEM((R // 2, n_tp * hu), BF16), dma, dma((n_tp, 2))],
        cost_estimate=pl.CostEstimate(flops=2 * R * D * (D + 3 * n_tp * hu), bytes_accessed=w1.size, transcendentals=R * D),
        compiler_params=pltpu.CompilerParams(collective_id=2, has_side_effects=True, vmem_limit_bytes=VM2),
        name="last",
    )(o, act, w1, gate, mod)


def _store_kernel(src, dst, sem):
    cp = pltpu.make_async_copy(src, dst, sem)
    cp.start()
    cp.wait()


def _store(x):
    return pl.pallas_call(
        _store_kernel, out_shape=jax.ShapeDtypeStruct(x.shape, x.dtype), in_specs=[VMEM], out_specs=ANY,
        scratch_shapes=[pltpu.SemaphoreType.DMA], compiler_params=pltpu.CompilerParams(vmem_limit_bytes=1 << 20), name="store")(x)


def solution(mesh):
    n_dp = mesh.shape["dp"]

    def shard_body(token_act, token_cond, pair_bias, token_mask, ada_scale, ada_w, ada_bias, zero_w, zero_b, w_qkvg, b_q, w_o, w_up, w_down):
        S, T, D = token_act.shape
        C = token_cond.shape[-1]
        mask_row = token_mask.reshape(1, T)
        wq = jnp.transpose(w_qkvg, (0, 2, 3, 1))
        wup = jnp.transpose(w_up, (0, 2, 3, 1))
        act = token_act.reshape(S * T, D)
        cond = token_cond.reshape(S * T, C)
        o0, w0, gate0, mod0, nxt0 = _block0(n_dp, token_act, token_cond, pair_bias, mask_row, wq, b_q, ada_scale, ada_w, ada_bias, zero_w, zero_b, w_o, wup, w_down)
        o0, w0, gate0, mod0, nxt0 = (pltpu.with_memory_space_constraint(v, pltpu.VMEM) for v in (o0, w0, gate0, mod0, nxt0))
        w1, gate1, mod1, a1, o1, _ = _block1(n_dp, o0, w0, gate0, mod0, nxt0, act, cond, zero_w, zero_b, ada_scale, ada_w, ada_bias, pair_bias, mask_row, wq, b_q, w_o, wup, w_down)
        o1, a1, w1, gate1, mod1 = (pltpu.with_memory_space_constraint(v, pltpu.VMEM) for v in (o1, a1, w1, gate1, mod1))
        out = pltpu.with_memory_space_constraint(_last(n_dp, o1, a1, w1, gate1, mod1), pltpu.VMEM)
        return _store(out).reshape(S, T, D)

    everywhere = P()
    in_specs = (P('dp', None, None), P('dp', None, None), P(None, 'tp', None, None), P(None), everywhere, everywhere, everywhere, everywhere, everywhere, P(None, None, None, 'tp'), P(None, 'tp'), P(None, 'tp', None), P(None, None, None, 'tp'), P(None, 'tp', None))
    return jax.shard_map(shard_body, mesh=mesh, in_specs=in_specs, out_specs=P('dp', None, None), check_vma=False)
```

time: 310 us -> 248 us (0.80)
  Pallas kernels: 279 us -> 247 us
  local copies, waits for them, and re-layouts: 30.6 us -> 0 us
    pallas_call x3 -> x4, Pallas kernels: 279 us -> 247 us  [the longest x1 105 us: _block1(): pl.pallas_call(functools.partial(_block1_kernel, (S, T, D, C, n_tp, n_dp,...]
    reshape x2 -> x0, local copies, waits for them, and re-layouts: 17.5 us -> none  [the longest x1 11.2 us: shard_body(): aw = ada_w.reshape(L, 2, C, 2 * D)]
    unnamed x2 -> x0, local copies, waits for them, and re-layouts: 11.8 us -> none
where the time goes in v3:
time: 248 us; the launch traced here: 247 us
  Pallas kernels  247 us (100%)
    pallas_call x1, Pallas kernels, _block1(): pl.pallas_call(functools.partial(_block1_kernel, (S, T, D, C, n_tp, n_dp,...  105 us
    pallas_call x1, Pallas kernels, _block0(): pl.pallas_call(functools.partial(_block0_kernel, (S, T, D, C, n_tp, n_dp,...  70.7 us
    pallas_call x1, Pallas kernels, _last(): pl.pallas_call(functools.partial(_last_kernel, (D, n_tp, n_dp, hd, hu, R)...  67.2 us

profile of v3, /device:TPU:21, one launch (start us, length us, event | category | flops | bytes accessed | tf_op | source)
XLA Modules:
  0.0 247.5 jit_solution(16031543594555928523)
XLA Ops:
  0.0 70.7 %block0.1 = (bf16[16,48,512]{2,1,0:T(8,128)(2,1)S(1)}, bf16[16,336,768]{2,1,0:T(8,128)(2,1)S(1)}, f32[512,1536]{1,0:T(8,128)S(1)}, f32[512,1536]{1,0:T(8,128)S(1)}, f32[512,1536]{1,0:T(8,128)S(1)}) custom-call(bf16[8,1024,768]{2,1,0:T(8,128)(2,1)} %x_hbm.1, bf16[8,1024,384]{2,1,0:T(8,128)(2,1)} %cond_hbm.1, bf16[2,1,1024,1024]{3,2,1,0:T(8,128)(2,1)} %bias_hbm.3, ...), custom_call_target="tpu_custom_call" | custom-call | flops 21474836480 | bytes 18874368 | tf_op jit(solution)/shard_map/block0/pallas_call | solution.py:451
  70.7 104.6 %block1.1 = (bf16[16,336,768]{2,1,0:T(8,128)(2,1)S(1)}, f32[512,1536]{1,0:T(8,128)S(1)}, f32[512,1536]{1,0:T(8,128)S(1)}, bf16[512,768]{1,0:T(8,128)(2,1)S(1)}, ...) custom-call(bf16[16,48,512]{2,1,0:T(8,128)(2,1)S(1)} %get-tuple-elem, ...), custom_call_target="tpu_custom_call", output_to_operand_aliasing={{0}: (1, {}), {1}: (2, {}), {2}: (3, {})} | custom-call | flops 11811160064 | bytes 12582912 | tf_op jit(solution)/shard_map/block1/pallas_call | solution.py:621
  175.3 67.2 %last.1.src = bf16[8192,768]{1,0:T(8,128)(2,1)S(1)} custom-call(bf16[16,48,512]{2,1,0:T(8,128)(2,1)S(1)} %get-tuple-element.20.o_v, bf16[512,768]{1,0:T(8,128)(2,1)S(1)} %get-tuple-element.21.act, bf16[16,336,768]{2,1,0:T(8,128)(2,1)S(1)} %get-tuple-element.22.wall, f32[512,1536]{1,0:T(8,128)S(1)} %get-tuple-element.23.gate, ...), custom_call_target="tpu_custom_call" | custom-call | flops 4227858432 | bytes 4128768 | tf_op jit(solution)/shard_map/last/pallas_call | solution.py:671
  242.5 4.8 %store.1 = bf16[8192,768]{1,0:T(8,128)(2,1)} custom-call(bf16[8192,768]{1,0:T(8,128)(2,1)S(1)} %last.1.src), custom_call_target="tpu_custom_call" | custom-call | tf_op jit(solution)/shard_map/store/pallas_call | solution.py:689

commit v4 on v3

--- a/solution.py
+++ b/solution.py
@@ -111,18 +111,19 @@
 
 
 class Cross:
-    def __init__(self, place, buf, lo, hi, recv_sem, near_sem, far_sem):
-        self.p, self.buf, self.lo, self.hi = place, buf, lo, hi
+    def __init__(self, place, buf, lo, hi, n_chunk, recv_sem, near_sem, far_sem):
+        self.p, self.buf, self.lo, self.hi, self.n_chunk = place, buf, lo, hi, n_chunk
         self.recv, self.near, self.far_sem = recv_sem, near_sem, far_sem
         self.far = place.nz // 2
-
-    def _view(self, b):
-        return self.buf.at[b, self.lo:self.hi, :]
-
-    def _push(self, b, dst, sem, src=None):
-        v = self._view(b)
+        self.size = (hi - lo) // n_chunk
+
+    def _view(self, b, ch):
+        return self.buf.at[b, self.lo + ch * self.size:self.lo + (ch + 1) * self.size, :]
+
+    def _push(self, b, ch, dst, sem, src=None):
+        v = self._view(b, ch)
         pltpu.make_async_remote_copy(
-            src_ref=v if src is None else src, dst_ref=v, send_sem=sem, recv_sem=self.recv.at[b],
+            src_ref=v if src is None else src, dst_ref=v, send_sem=sem, recv_sem=self.recv.at[b, ch],
             device_id=dst, device_id_type=MESH).start()
 
     def _mine(self, b):
@@ -130,17 +131,19 @@
 
     def own(self, src):
         p = self.p
-
-        @pl.when(self._mine(p.me))
-        def _():
-            self._push(p.me, {"tp": p.at(1)}, self.far_sem.at[p.z], src)
-            self._push(p.me, {"tp": p.at(-1)}, self.far_sem.at[p.z], src)
-
-        self._push(p.me, {"tp": p.partner}, self.near, src)
-
-    def wait(self, b):
-        v = self._view(b)
-        pltpu.make_async_copy(v, v, self.recv.at[b]).wait()
+        for ch in range(self.n_chunk):
+            part = src.at[self.lo + ch * self.size:self.lo + (ch + 1) * self.size, :]
+
+            @pl.when(self._mine(p.me))
+            def _():
+                self._push(p.me, ch, {"tp": p.at(1)}, self.far_sem.at[p.z], part)
+                self._push(p.me, ch, {"tp": p.at(-1)}, self.far_sem.at[p.z], part)
+
+            self._push(p.me, ch, {"tp": p.partner}, self.near, part)
+
+    def wait(self, b, ch):
+        v = self._view(b, ch)
+        pltpu.make_async_copy(v, v, self.recv.at[b, ch]).wait()
 
     def _each(self, h, body):
         p = self.p
@@ -151,32 +154,32 @@
             def _():
                 body(b, sign, (h < self.far - 1) | ((h == self.far - 1) & (p.c == core)))
 
-    def along(self, h):
+    def along(self, h, ch):
         p = self.p
 
         def body(b, sign, onward):
             @pl.when(self._mine(b))
             def _():
-                self.wait(b)
+                self.wait(b, ch)
 
                 @pl.when(onward)
                 def _():
-                    self._push(b, {"tp": p.at(sign)}, self.far_sem.at[b // 2])
+                    self._push(b, ch, {"tp": p.at(sign)}, self.far_sem.at[b // 2])
 
                 for i in range(1, p.n_dp):
-                    self._push(b, {"dp": p.column(i), "tp": p.me}, self.far_sem.at[b // 2])
-                self._push(b, {"tp": p.partner}, self.near)
+                    self._push(b, ch, {"dp": p.column(i), "tp": p.me}, self.far_sem.at[b // 2])
+                self._push(b, ch, {"tp": p.partner}, self.near)
 
         self._each(h, body)
 
-    def across(self, h):
+    def across(self, h, ch):
         p = self.p
 
         def body(b, sign, onward):
             @pl.when(jnp.logical_not(self._mine(b)))
             def _():
-                self.wait(b)
-                self._push(b, {"tp": p.partner}, self.near)
+                self.wait(b, ch)
+                self._push(b, ch, {"tp": p.partner}, self.near)
 
         self._each(h, body)
 
@@ -188,7 +191,8 @@
             pltpu.make_async_copy(v, v, sem).wait()
 
         def other(i, _):
-            self.wait(i * 2 + (1 - p.c))
+            for ch in range(self.n_chunk):
+                self.wait(i * 2 + (1 - p.c), ch)
             return 0
 
         lax.fori_loop(0, p.nz, other, 0)
@@ -235,7 +239,7 @@
             self.vt_s[:, rows] = jnp.where(ones, 1.0, rest[2 * HP:3 * HP]).astype(BF16)
             self.gt_s[:, rows] = _sig(rest[3 * HP:3 * HP + hd])
 
-    def attend(self, slot):
+    def attend(self, slot, hook=None):
         T, hd = self.T, self.hd
         n = T // QT
         c1 = LOG2E / math.sqrt(hd)
@@ -247,6 +251,8 @@
             return jnp.max(logits, axis=0, keepdims=True)
 
         top = scores(0)
+        if hook is not None:
+            hook()
         for i in range(n):
             cols = pl.ds(i * QT, QT)
             nxt = scores(i + 1) if i + 1 < n else None
@@ -313,37 +319,38 @@
 
 def _block0_kernel(dims, x_hbm, cond_hbm, bias_hbm, mask_ref, wq_hbm, bq_ref, asc_ref, aw_hbm, ab_ref, zw_hbm, zb_ref, wo_hbm, wup_hbm, wdn_hbm,
                    o_out, wg, gate_out, mod_out, nxt_out,
-                   xbuf, cbuf, bias_v, bt, w_s, raw, aw_s, k_s, qt_s, vt_s, gt_s, lg, o_s, wst, cond,
-                   ld_sem, cd_sem, b_sem, q_sem, a_sem, st_sem, o_send, o_recv, w_send, w_recv, c_near, c_far, c_recv):
-    S, T, D, C, n_tp, n_dp, hd, hu = dims
+                   xraw, craw, xn, bias_v, bt, w_s, raw, aw_s, k_s, qt_s, vt_s, gt_s, lg, o_s, wst, cond,
+                   ld_sem, cd_sem, b_sem, q_sem, a_sem, st_sem, o_send, o_recv, n_send, n_recv, n_free, w_send, w_recv, c_near, c_far, c_recv):
+    S, T, D, C, n_tp, n_dp, hd, hu, cut, n_chunk = dims
     p = Place(n_tp, n_dp)
     entered = p.enter(True)
     rows_w = hd + 3 * hu
-    cut = hd + hu
     stage = []
-    for src, lo, hi in ((wo_hbm.at[0], 0, hd), (wup_hbm.at[0, 0], hd, cut), (wup_hbm.at[0, 1], cut, hd + 2 * hu),
+    for src, lo, hi in ((wo_hbm.at[0], 0, hd), (wup_hbm.at[0, 0], hd, hd + hu), (wup_hbm.at[0, 1], hd + hu, hd + 2 * hu),
                         (wdn_hbm.at[0], hd + 2 * hu, rows_w)):
         stage.append(pltpu.make_async_copy(src, wst.at[lo:hi, :], st_sem.at[len(stage)]))
     for cp in stage:
         cp.start()
-    sign = 1 - 2 * p.c
     R = S * T // n_tp
+    mine = pl.ds(p.c * R, R)
 
     def sample_of(k):
-        return lax.rem(p.z + S + sign * (k + 1), S)
+        j = S - 1 - k
+        return lax.rem(p.z + S + (1 - 2 * lax.rem(j, 2)) * ((j + 1) // 2), S)
 
     def loads(k, slot):
         s = sample_of(k)
-        return [pltpu.make_async_copy(x_hbm.at[s], xbuf.at[slot], ld_sem.at[slot]),
-                pltpu.make_async_copy(cond_hbm.at[s], cbuf.at[slot], cd_sem.at[slot])]
+        return [pltpu.make_async_copy(x_hbm.at[s, mine], xraw.at[slot], ld_sem.at[slot]),
+                pltpu.make_async_copy(cond_hbm.at[s, mine], craw.at[slot], cd_sem.at[slot])]
 
     raws = [pltpu.make_async_copy(aw_hbm.at[0, 0], raw.at[0], a_sem.at[0]), pltpu.make_async_copy(zw_hbm.at[0], raw.at[1], a_sem.at[1]),
             pltpu.make_async_copy(aw_hbm.at[0, 1], raw.at[2], a_sem.at[2]), pltpu.make_async_copy(aw_hbm.at[1, 0], raw.at[0], a_sem.at[0])]
+    raws[0].start()
+    for k in range(2):
+        for cp in loads(k, k):
+            cp.start()
     bias_cp = pltpu.make_async_copy(bias_hbm.at[0, 0], bias_v, b_sem)
     bias_cp.start()
-    raws[0].start()
-    for cp in loads(0, 0):
-        cp.start()
     w_s[...] = jnp.zeros_like(w_s)
     qt_s[HP:, :] = jnp.zeros((HP, T), BF16)
     order = (1, 0, 2, 3)
@@ -356,76 +363,118 @@
         cp.wait()
     for r in (1, 2):
         raws[r].start()
-    cond_cp = pltpu.make_async_copy(cond_hbm.at[p.z, pl.ds(p.c * R, R), :], cond, b_sem)
+    cond_cp = pltpu.make_async_copy(cond_hbm.at[p.z, mine], cond, b_sem)
     entered()
     ring = Ring(p, lambda b, ch: wg.at[b, 0:cut, :], w_recv, w_send, 1)
-    cross = Cross(p, wg, cut, rows_w, c_recv, c_near, c_far)
+    cross = Cross(p, wg, cut, rows_w, n_chunk, c_recv, c_near, c_far)
     ring.own(0, wst.at[0:cut, :])
-    cross.own(wst.at[cut:rows_w, :])
+    cross.own(wst)
+
+    def half(slot, dst):
+        v = xn.at[slot, mine]
+        return pltpu.make_async_remote_copy(src_ref=v, dst_ref=v, send_sem=n_send.at[slot], recv_sem=n_recv.at[slot],
+                                            device_id={"tp": p.partner}, device_id_type=MESH)
+
+    def normalise(slot):
+        tile = 256 if R % 256 == 0 else R
+        for i in range(R // tile):
+            rows = pl.ds(i * tile, tile)
+            cn = _ln(craw[slot, rows, :].astype(F32))
+            y = _ada(xraw[slot, rows, :].astype(F32), cn, asc_ref[0, 0:1, :], aw_s[...], ab_ref[0, 0:1, :])
+            xn[slot, pl.ds(pl.multiple_of(p.c * R, R) + i * tile, tile), :] = y
+
+    raws[0].wait()
+    aw_s[...] = _flat(raw.at[0])
+    for cp in loads(0, 0):
+        cp.wait()
+    normalise(0)
     bias_cp.wait()
+    half(0, p.partner).start()
     _load_bias(bias_v, mask_ref, bt)
     cond_cp.start()
-    raws[0].wait()
-    aw_s[...] = _flat(raw.at[0])
     ex = Exchange(p, o_s, o_out, o_send, o_recv)
     brow = _bias_row(bq_ref[0:1, :], hd)
 
     def step(k, _):
         slot = lax.rem(k, 2)
 
+        @pl.when(k + 2 < S)
+        def _():
+            for cp in loads(k + 2, slot):
+                cp.start()
+
+        v = xn.at[slot, pl.ds((1 - p.c) * R, R)]
+        pltpu.make_async_copy(v, v, n_recv.at[slot]).wait()
+        half(slot, p.partner).wait_send()
+        at = Attend(n_tp, hd, w_s, brow, bt, k_s, qt_s, vt_s, gt_s, lg, o_s, lambda i, tile: xn[slot, pl.ds(i * tile, tile), :])
+        at.project()
+
+        @pl.when(k + 2 < S)
+        def _():
+            pl.semaphore_signal(n_free, inc=1, device_id={"tp": p.partner}, device_id_type=MESH)
+
+        @pl.when(k >= 1)
+        def _():
+            ex.start(sample_of(k - 1), 1 - slot)
+
         @pl.when(k + 1 < S)
         def _():
             for cp in loads(k + 1, 1 - slot):
-                cp.start()
-
-        for cp in loads(k, slot):
-            cp.wait()
-
-        def x_rows(i, tile):
-            rows = pl.ds(i * tile, tile)
-            cn = _ln(cbuf[slot, rows, :].astype(F32))
-            return _ada(xbuf[slot, rows, :].astype(F32), cn, asc_ref[0, 0:1, :], aw_s[...], ab_ref[0, 0:1, :])
-
-        at = Attend(n_tp, hd, w_s, brow, bt, k_s, qt_s, vt_s, gt_s, lg, o_s, x_rows)
-        at.project()
-
-        @pl.when(k >= 1)
-        def _():
-            ex.start(sample_of(k - 1), 1 - slot)
-
-        @pl.when((k >= 1) & (k <= p.nz // 2))
-        def _():
-            ring.service(k, 0)
-            cross.along(k)
-
-        @pl.when((k >= 3) & (k <= p.nz // 2 + 2))
-        def _():
-            cross.across(k - 2)
+                cp.wait()
+            normalise(1 - slot)
+
+            @pl.when(k >= 1)
+            def _():
+                pl.semaphore_wait(n_free, 1)
+
+        def at_step(when, *events):
+            @pl.when(k == when)
+            def _():
+                for f, *args in events:
+                    f(*args)
+
+        chunks = range(n_chunk)
+        at_step(1, (ring.service, 1, 0))
+        at_step(2, *((cross.along, 1, ch) for ch in chunks))
+        at_step(3, (ring.service, 2, 0))
+        at_step(4, *((cross.along, 2, ch) for ch in chunks), *((cross.across, 1, ch) for ch in chunks))
+        at_step(5, (ring.service, 3, 0))
+        at_step(6, *((cross.along, 3, ch) for ch in chunks), *((cross.across, 2, ch) for ch in chunks))
+        at_step(7, (ring.service, 4, 0), *((cross.along, 4, ch) for ch in chunks))
 
         @pl.when(k >= 2)
         def _():
             ex.sent(sample_of(k - 2), slot)
 
-        at.attend(slot)
+        def hook():
+            @pl.when(k + 1 < S)
+            def _():
+                half(1 - slot, p.partner).start()
+
+        at.attend(slot, hook)
         return 0
 
     lax.fori_loop(0, S, step, 0)
     ex.start(sample_of(S - 1), (S - 1) % 2)
     raws[3].start()
+    for ch in range(n_chunk):
+        cross.across(3, ch)
     wg[p.me] = wst[...]
     cond_cp.wait()
     cn = _ln(cond[...].astype(F32))
     raws[1].wait()
     aw_s[...] = _flat(raw.at[1])
     gate_out[...] = _dot(cond[...], aw_s[...])
-    for half in range(2):
-        cols = slice(half * D, (half + 1) * D)
-        gate_out[:, cols] = _sig(gate_out[:, cols] + zb_ref[0, half:half + 1, :])
+    for half_d in range(2):
+        cols = slice(half_d * D, (half_d + 1) * D)
+        gate_out[:, cols] = _sig(gate_out[:, cols] + zb_ref[0, half_d:half_d + 1, :])
     for src, cp, l, j, out in ((2, raws[2], 0, 1, mod_out), (0, raws[3], 1, 0, nxt_out)):
         cp.wait()
         aw_s[...] = _flat(raw.at[src])
         out[...] = _dot((cn * asc_ref[l, j:j + 1, :]).astype(BF16), aw_s[...])
         out[:, :D] = _sig(out[:, :D] + ab_ref[l, j:j + 1, :])
+    for ch in range(n_chunk):
+        cross.across(4, ch)
     ex.sent(sample_of(S - 2), S % 2)
     ex.sent(sample_of(S - 1), (S - 1) % 2)
 
@@ -447,22 +496,23 @@
     n_tp = S * 2
     rows_w = hd + 3 * hu
     R = T // 2
+    cut, n_chunk = hd + hu, 2
     dma = pltpu.SemaphoreType.DMA
     return pl.pallas_call(
-        functools.partial(_block0_kernel, (S, T, D, C, n_tp, n_dp, hd, hu)),
+        functools.partial(_block0_kernel, (S, T, D, C, n_tp, n_dp, hd, hu, cut, n_chunk)),
         out_shape=(pltpu.VMEM((n_tp, hd, R), BF16), pltpu.VMEM((n_tp, rows_w, D), BF16),
                    pltpu.VMEM((R, 2 * D), F32), pltpu.VMEM((R, 2 * D), F32), pltpu.VMEM((R, 2 * D), F32)),
         in_specs=[ANY, ANY, ANY, VMEM, ANY, VMEM, VMEM, ANY, VMEM, ANY, VMEM, ANY, ANY, ANY],
         out_specs=(VMEM,) * 5,
         scratch_shapes=[
-            pltpu.VMEM((2, T, D), BF16), pltpu.VMEM((2, T, C), BF16), pltpu.VMEM((T, T), BF16), pltpu.VMEM((T, T), F32),
+            pltpu.VMEM((2, R, D), BF16), pltpu.VMEM((2, R, C), BF16), pltpu.VMEM((2, T, D), BF16), pltpu.VMEM((T, T), BF16), pltpu.VMEM((T, T), F32),
             pltpu.VMEM((4 * HP, D), BF16), pltpu.VMEM((3, C, 2, D), BF16), pltpu.VMEM((C, 2 * D), BF16),
             pltpu.VMEM((T, 2 * HP), BF16), pltpu.VMEM((2 * HP, T), BF16),
             pltpu.VMEM((HP, T), BF16), pltpu.VMEM((hd, T), F32), pltpu.VMEM((2, T, QT), F32), pltpu.VMEM((2, hd, T), BF16),
             pltpu.VMEM((rows_w, D), BF16), pltpu.VMEM((R, C), BF16),
-            dma((2,)), dma((2,)), dma, dma((4,)), dma((3,)), dma((4,)), dma((2, 2)), dma, dma, dma((n_tp, 1)),
-            dma, dma((S,)), dma((n_tp,))],
-        cost_estimate=pl.CostEstimate(flops=2 * S * T * (D * 4 * HP + 2 * T * 256 + 2 * C * D), bytes_accessed=S * T * (D + C) * 2, transcendentals=S * T * T),
+            dma((2,)), dma((2,)), dma, dma((4,)), dma((3,)), dma((4,)), dma((2, 2)), dma, dma((2,)), dma((2,)), pltpu.SemaphoreType.REGULAR,
+            dma, dma((n_tp, 1)), dma, dma((S,)), dma((n_tp, n_chunk))],
+        cost_estimate=pl.CostEstimate(flops=2 * S * T * (D * 4 * HP + 2 * T * 256 + C * D), bytes_accessed=S * T * (D + C), transcendentals=S * T * T),
         compiler_params=pltpu.CompilerParams(collective_id=0, has_side_effects=True, vmem_limit_bytes=VM0),
         name="block0",
     )(x, cond, pair_bias, mask_row, wq, bq, asc, aw, ab, zw, zb, wo, wup, wdn)
@@ -515,7 +565,8 @@
         cp.start()
     for cp in stage:
         cp.wait()
-    cross = Cross(p, wg, 0, rows_w, c_recv, c_near, c_far)
+    n_chunk = 3
+    cross = Cross(p, wg, 0, rows_w, n_chunk, c_recv, c_near, c_far)
     keep = pltpu.make_async_copy(wst, wg.at[p.me], wl_sem)
     keep.start()
     entered()
@@ -529,7 +580,8 @@
         a_out[rows, :] = new
         xg[pl.ds(row0 + ch * tile, tile), :] = (nxt0[rows, :D] * _ln(new.astype(F32)) + nxt0[rows, D:]).astype(BF16)
         ring.own(ch)
-        cross.along(ch + 1)
+        for i in range(n_chunk):
+            cross.along(ch + 1, i)
     cps[2].wait()
     _load_bias(bias_v, mask_ref, bt)
     for cp in wq:
@@ -548,11 +600,13 @@
 
         @pl.when(j <= p.nz // 2 - 3)
         def _():
-            cross.along(j + 3)
+            for i in range(n_chunk):
+                cross.along(j + 3, i)
 
         @pl.when((j >= 1) & (j <= p.nz // 2))
         def _():
-            cross.across(j)
+            for i in range(n_chunk):
+                cross.across(j, i)
 
         @pl.when(j >= 1)
         def _():
@@ -632,7 +686,7 @@
             pltpu.VMEM((4 * HP, D), BF16), pltpu.VMEM((T, 2 * HP), BF16), pltpu.VMEM((2 * HP, T), BF16),
             pltpu.VMEM((HP, T), BF16), pltpu.VMEM((hd, T), F32), pltpu.VMEM((2, T, QT), F32), pltpu.VMEM((2, hd, T), BF16),
             pltpu.VMEM((rows_w, D), BF16),
-            dma((5,)), dma((4,)), dma((4,)), dma, dma, dma((n_tp, 2)), dma((2, 2)), dma, dma, dma((S,)), dma((n_tp,))],
+            dma((5,)), dma((4,)), dma((4,)), dma, dma, dma((n_tp, 2)), dma((2, 2)), dma, dma, dma((S,)), dma((n_tp, 3))],
         cost_estimate=pl.CostEstimate(flops=2 * S * T * (D * 4 * HP + 2 * T * 256), bytes_accessed=S * T * D * 2, transcendentals=S * T * T),
         compiler_params=pltpu.CompilerParams(collective_id=1, has_side_effects=True, vmem_limit_bytes=VM1),
         name="block1",

time: 248 us -> 247 us (level)
    pallas_call x1, Pallas kernels: 105 us -> 101 us  [_block1(): pl.pallas_call(functools.partial(_block1_kernel, (S, T, D, C, n_tp, n_dp,...]
where the time goes in v4:
time: 247 us; the launch traced here: 246 us
  Pallas kernels  246 us (100%)
    pallas_call x1, Pallas kernels, _block1(): pl.pallas_call(functools.partial(_block1_kernel, (S, T, D, C, n_tp, n_dp,...  101 us
    pallas_call x1, Pallas kernels, _block0(): pl.pallas_call(functools.partial(_block0_kernel, (S, T, D, C, n_tp, n_dp,...  72.7 us
    pallas_call x1, Pallas kernels, _last(): pl.pallas_call(functools.partial(_last_kernel, (D, n_tp, n_dp, hd, hu, R)...  67.3 us

profile of v4, /device:TPU:21, one launch (start us, length us, event | category | flops | bytes accessed | tf_op | source)
XLA Modules:
  0.0 246.3 jit_solution(7535181460857091083)
XLA Ops:
  0.0 72.7 %block0.1 = (bf16[16,48,512]{2,1,0:T(8,128)(2,1)S(1)}, bf16[16,336,768]{2,1,0:T(8,128)(2,1)S(1)}, f32[512,1536]{1,0:T(8,128)S(1)}, f32[512,1536]{1,0:T(8,128)S(1)}, f32[512,1536]{1,0:T(8,128)S(1)}) custom-call(bf16[8,1024,768]{2,1,0:T(8,128)(2,1)} %x_hbm.1, bf16[8,1024,384]{2,1,0:T(8,128)(2,1)} %cond_hbm.1, bf16[2,1,1024,1024]{3,2,1,0:T(8,128)(2,1)} %bias_hbm.3, ...), custom_call_target="tpu_custom_call" | custom-call | flops 16642998272 | bytes 9437184 | tf_op jit(solution)/shard_map/block0/pallas_call | solution.py:501
  72.7 101.3 %block1.1 = (bf16[16,336,768]{2,1,0:T(8,128)(2,1)S(1)}, f32[512,1536]{1,0:T(8,128)S(1)}, f32[512,1536]{1,0:T(8,128)S(1)}, bf16[512,768]{1,0:T(8,128)(2,1)S(1)}, ...) custom-call(bf16[16,48,512]{2,1,0:T(8,128)(2,1)S(1)} %get-tuple-elem, ...), custom_call_target="tpu_custom_call", output_to_operand_aliasing={{0}: (1, {}), {1}: (2, {}), {2}: (3, {})} | custom-call | flops 11811160064 | bytes 12582912 | tf_op jit(solution)/shard_map/block1/pallas_call | solution.py:675
  174.0 67.3 %last.1.src = bf16[8192,768]{1,0:T(8,128)(2,1)S(1)} custom-call(bf16[16,48,512]{2,1,0:T(8,128)(2,1)S(1)} %get-tuple-element.20.o_v, bf16[512,768]{1,0:T(8,128)(2,1)S(1)} %get-tuple-element.21.act, bf16[16,336,768]{2,1,0:T(8,128)(2,1)S(1)} %get-tuple-element.22.wall, f32[512,1536]{1,0:T(8,128)S(1)} %get-tuple-element.23.gate, ...), custom_call_target="tpu_custom_call" | custom-call | flops 4227858432 | bytes 4128768 | tf_op jit(solution)/shard_map/last/pallas_call | solution.py:725
  241.3 4.8 %store.1 = bf16[8192,768]{1,0:T(8,128)(2,1)} custom-call(bf16[8192,768]{1,0:T(8,128)(2,1)S(1)} %last.1.src), custom_call_target="tpu_custom_call" | custom-call | tf_op jit(solution)/shard_map/store/pallas_call | solution.py:743

commit v5 on v4

v5 whole, which is shorter than its diff:
```python
import functools
import math

import jax
import jax.numpy as jnp
from jax import lax
from jax.experimental import pallas as pl
from jax.experimental.pallas import tpu as pltpu
from jax.sharding import PartitionSpec as P

LN_EPS = 1e-5
LOG2E = 1.4426950408889634
MESH = pl.DeviceIdType.MESH
BF16 = jnp.bfloat16
F32 = jnp.float32
scope = jax.named_scope
HP = 64
QT = 256
ANY = pl.BlockSpec(memory_space=pl.ANY)
VMEM = pl.BlockSpec(memory_space=pltpu.VMEM)
HBM = pl.BlockSpec(memory_space=pltpu.HBM)
VM0, VM1, VM2 = 40 << 20, 40 << 20, 8 << 20


def _ln(x):
    mean = jnp.mean(x, axis=-1, keepdims=True)
    cen = x - mean
    var = jnp.mean(cen * cen, axis=-1, keepdims=True)
    return cen * lax.rsqrt(var + LN_EPS)


def _sig(x):
    return 0.5 * jnp.tanh(0.5 * x) + 0.5


def _dot(a, b, ca=1, cb=0):
    return lax.dot_general(a, b, (((ca,), (cb,)), ((), ())), preferred_element_type=F32)


def _ada(x_f32, cond_normed, scale, w, bias):
    d = x_f32.shape[-1]
    mod = _dot((cond_normed * scale).astype(BF16), w)
    return (_sig(mod[:, :d] + bias) * _ln(x_f32) + mod[:, d:]).astype(BF16)


class Place:
    def __init__(self, n_tp, n_dp):
        self.n = n_tp
        self.n_dp = n_dp
        self.col = lax.axis_index("dp")
        self.nz = n_tp // 2
        self.me = lax.axis_index("tp")
        self.z = self.me // 2
        self.c = lax.rem(self.me, 2)
        self.partner = self.z * 2 + (1 - self.c)

    def at(self, off):
        return lax.rem(self.z + off + self.nz, self.nz) * 2 + self.c

    def column(self, i):
        return lax.rem(self.col + i, self.n_dp)

    def enter(self, everyone):
        barrier = pltpu.get_barrier_semaphore()
        if everyone:
            peers = [{"tp": lax.rem(self.me + i, self.n)} for i in range(1, self.n)]
            peers += [{"dp": self.column(i), "tp": self.me} for i in range(1, self.n_dp)]
        else:
            peers = [{"tp": t} for t in (self.at(1), self.at(-1), self.partner)]
        for peer in peers:
            pl.semaphore_signal(barrier, inc=1, device_id=peer, device_id_type=MESH)
        return lambda: pl.semaphore_wait(barrier, len(peers))


class Ring:
    def __init__(self, place, view, recv_sem, send_sem, n_chunk):
        self.p, self.view, self.recv, self.send, self.n_chunk = place, view, recv_sem, send_sem, n_chunk
        self.far = place.nz // 2

    def _push(self, b, ch, dst, src=None):
        v = self.view(b, ch)
        pltpu.make_async_remote_copy(
            src_ref=v if src is None else src, dst_ref=v, send_sem=self.send, recv_sem=self.recv.at[b, ch],
            device_id={"tp": dst}, device_id_type=MESH).start()

    def own(self, ch, src=None):
        p = self.p
        self._push(p.me, ch, p.at(1), src)
        self._push(p.me, ch, p.at(-1), src)
        self._push(p.me, ch, p.partner, src)

    def wait(self, b, ch):
        v = self.view(b, ch)
        pltpu.make_async_copy(v, v, self.recv.at[b, ch]).wait()

    def service(self, h, ch):
        p = self.p
        for sign, core in ((1, 0), (-1, 1)):
            b = p.at(-sign * h)

            @pl.when((h < self.far) | (p.c == core))
            def _():
                self.wait(b, ch)

                @pl.when((h < self.far - 1) | ((h == self.far - 1) & (p.c == core)))
                def _():
                    self._push(b, ch, p.at(sign))

                self._push(b, ch, p.partner)

    def drain(self, whole):
        pltpu.make_async_copy(whole, whole, self.send).wait()


class Cross:
    def __init__(self, place, buf, lo, hi, n_chunk, recv_sem, near_sem, far_sem, spread=True):
        self.p, self.buf, self.lo, self.hi, self.n_chunk, self.spread = place, buf, lo, hi, n_chunk, spread
        self.recv, self.near, self.far_sem = recv_sem, near_sem, far_sem
        self.far = place.nz // 2
        self.size = (hi - lo) // n_chunk

    def _rows(self, ch):
        return pl.ds(self.lo + ch * self.size, self.size)

    def _push(self, b, ch, dst, sem, src=None):
        v = self.buf.at[b, self._rows(ch), :]
        pltpu.make_async_remote_copy(
            src_ref=v if src is None else src, dst_ref=v, send_sem=sem, recv_sem=self.recv.at[b, ch],
            device_id=dst, device_id_type=MESH).start()

    def _push_over(self, b, ch, plane):
        p = self.p

        @pl.when(plane)
        def _():
            for i in range(1, p.n_dp):
                self._push(b, ch, {"dp": p.column(i), "tp": p.me}, self.far_sem.at[b // 2])

        self._push(b, ch, {"tp": p.partner}, self.near)

    def _mine(self, b):
        return lax.rem(b, self.p.n_dp) == self.p.col

    def own(self, src):
        p = self.p
        for ch in range(self.n_chunk):
            part = src.at[self._rows(ch), :]

            @pl.when(self._mine(p.me))
            def _():
                for off in (1, -1):
                    self._push(p.me, ch, {"tp": p.at(off)}, self.far_sem.at[p.z], part)

            if self.spread:
                self._push(p.me, ch, {"tp": p.partner}, self.near, part)

    def wait(self, b, ch):
        v = self.buf.at[b, self._rows(ch), :]
        pltpu.make_async_copy(v, v, self.recv.at[b, ch]).wait()

    def _each(self, h, body):
        p = self.p
        for sign, core in ((1, 0), (-1, 1)):
            b = p.at(-sign * h)

            @pl.when((h < self.far) | (p.c == core))
            def _():
                body(b, sign, (h < self.far - 1) | ((h == self.far - 1) & (p.c == core)))

    def along(self, h, ch):
        p = self.p

        def body(b, sign, onward):
            @pl.when(self._mine(b))
            def _():
                self.wait(b, ch)

                @pl.when(onward)
                def _():
                    self._push(b, ch, {"tp": p.at(sign)}, self.far_sem.at[b // 2])

                if self.spread:
                    self._push_over(b, ch, True)

        self._each(h, body)

    def hand_on(self):
        p = self.p

        def block(i, _):
            b = i * 2 + p.c

            @pl.when(self._mine(b) | (i == p.z))
            def _():
                for ch in range(self.n_chunk):
                    self._push_over(b, ch, i != p.z)
            return 0

        lax.fori_loop(0, p.nz, block, 0)

    def across(self, h, ch):
        p = self.p

        def body(b, sign, onward):
            @pl.when(jnp.logical_not(self._mine(b)))
            def _():
                self.wait(b, ch)
                self._push(b, ch, {"tp": p.partner}, self.near)

        self._each(h, body)

    def _sent(self, k, sem):
        if k:
            v = self.buf.at[0:k, self.lo:self.hi, :]
            pltpu.make_async_copy(v, v, sem).wait()

    def finish_near(self):
        p = self.p

        def other(i, _):
            for ch in range(self.n_chunk):
                self.wait(i * 2 + (1 - p.c), ch)
            return 0

        lax.fori_loop(0, p.nz, other, 0)
        self._sent(p.nz, self.near)

    def finish_far(self, ring=True):
        p = self.p
        over = p.n_dp - 1 if self.spread else 0
        if ring:
            @pl.when(self._mine(p.me))
            def _():
                self._sent(2, self.far_sem.at[p.z])

        def body(b, sign, onward):
            sem = self.far_sem.at[b // 2]

            @pl.when(self._mine(b))
            def _():
                if not ring:
                    self._sent(over, sem)
                else:
                    @pl.when(onward)
                    def _():
                        self._sent(over + 1, sem)

                    @pl.when(jnp.logical_not(onward))
                    def _():
                        self._sent(over, sem)

        def hop(h, _):
            self._each(h, body)
            return 0

        lax.fori_loop(1, self.far + 1, hop, 0)


def _copy(src, dst, sem):
    cp = pltpu.make_async_copy(src, dst, sem)
    cp.start()
    return cp


def _stage(l, hd, hu, wo_hbm, wup_hbm, wdn_hbm, wst, sem):
    cps, lo = [], 0
    for src, rows in ((wo_hbm.at[l], hd), (wup_hbm.at[l, 0], hu), (wup_hbm.at[l, 1], hu), (wdn_hbm.at[l], hu)):
        cps.append(_copy(src, wst.at[pl.ds(lo, rows), :], sem.at[len(cps)]))
        lo += rows
    return cps


def _stage_qkvg(l, hd, wq_hbm, w_s, sem):
    w_s[...] = jnp.zeros_like(w_s)
    return [_copy(wq_hbm.at[l, f], w_s.at[pl.ds(i * HP, hd), :], sem.at[i]) for i, f in enumerate((1, 0, 2, 3))]


class Attend:
    def __init__(self, n_tp, hd, w, brow, bt, k_s, qt_s, vt_s, gt_s, lg, o_s, x_rows):
        self.__dict__.update(locals())
        self.T = bt.shape[0]

    def project(self):
        T, hd = self.T, self.hd
        tile = QT
        for i in range(T // tile):
            rows = pl.ds(i * tile, tile)
            res = _dot(self.x_rows(i, tile), self.w[...], 1, 1) + self.brow
            self.k_s[rows, :] = res[:, :2 * HP].astype(BF16)
            rest = res.T
            self.qt_s[0:HP, rows] = rest[HP:2 * HP].astype(BF16)
            ones = lax.broadcasted_iota(jnp.int32, (HP, tile), 0) == hd
            self.vt_s[:, rows] = jnp.where(ones, 1.0, rest[2 * HP:3 * HP]).astype(BF16)
            self.gt_s[:, rows] = _sig(rest[3 * HP:3 * HP + hd])

    def attend(self, slot, hook=None):
        T, hd = self.T, self.hd
        n = T // QT
        c1 = LOG2E / math.sqrt(hd)

        def scores(i):
            cols = pl.ds(i * QT, QT)
            logits = _dot(self.k_s[...], self.qt_s[:, cols]) * c1 + self.bt[:, cols]
            self.lg[i % 2] = logits
            return jnp.max(logits, axis=0, keepdims=True)

        top = scores(0)
        if hook is not None:
            hook()
        for i in range(n):
            cols = pl.ds(i * QT, QT)
            nxt = scores(i + 1) if i + 1 < n else None
            probs = jnp.exp2(self.lg[i % 2] - top).astype(BF16)
            mixed = _dot(self.vt_s[...], probs)
            self.o_s[slot, :, cols] = (self.gt_s[:, cols] * (mixed[:hd] / mixed[hd:hd + 1])).astype(BF16)
            top = nxt


def _load_bias(bias_v, mask_ref, bt):
    T = bt.shape[0]
    mask_add = (mask_ref[...].astype(F32) - 1.0) * 1e9

    def step(i, _):
        r = pl.multiple_of(i * 128, 128)
        rows = (bias_v[pl.ds(r, 128), :].astype(F32) + mask_add) * LOG2E
        bt[:, pl.ds(r, 128)] = rows.T
        return 0

    lax.fori_loop(0, T // 128, step, 0)


class Exchange:
    def __init__(self, place, sample_of, o_s, o_out, send_sem, recv_sem):
        self.p, self.sample_of, self.o_s, self.o_out, self.send, self.recv = place, sample_of, o_s, o_out, send_sem, recv_sem
        self.half = o_s.shape[-1] // 2

    def _each(self, k, remote, local):
        p = self.p
        for c in range(2):
            dst = self.sample_of(k) * 2 + c
            src = self.o_s.at[k, :, pl.ds(c * self.half, self.half)]
            sem = self.send.at[k, c]
            cp = pltpu.make_async_remote_copy(
                src_ref=src, dst_ref=self.o_out.at[p.me], send_sem=sem, recv_sem=self.recv,
                device_id={"tp": dst}, device_id_type=MESH)

            @pl.when(dst != p.me)
            def _():
                remote(cp)

            @pl.when(dst == p.me)
            def _():
                local(pltpu.make_async_copy(src, self.o_out.at[p.me], sem))

    def start(self, k):
        self._each(k, lambda cp: cp.start(), lambda cp: cp.start())

    def finish(self):
        def sent(k, _):
            self._each(k, lambda cp: cp.wait_send(), lambda cp: cp.wait())
            return 0

        lax.fori_loop(0, self.o_s.shape[0], sent, 0)
        rest = self.o_out.at[0:self.p.n - 1]
        pltpu.make_async_copy(rest, rest, self.recv).wait()


def _bias_row(bq, hd):
    return jnp.concatenate([jnp.zeros((1, HP), F32), bq, jnp.zeros((1, 3 * HP - hd), F32)], axis=1)


def _gates(out, cond, w, bias):
    d = bias.shape[-1]
    out[...] = _dot(cond, w)
    for j in range(bias.shape[0]):
        cols = pl.ds(j * d, d)
        out[:, cols] = _sig(out[:, cols] + bias[j:j + 1, :])


def _modulation(out, cond_normed, scale, w, bias):
    d = bias.shape[-1]
    out[...] = _dot((cond_normed * scale).astype(BF16), w)
    out[:, :d] = _sig(out[:, :d] + bias)


def _flat(raw):
    c, two, d = raw.shape
    return raw[...].reshape(c, two * d)


def _block0_kernel(dims, x_hbm, cond_hbm, bias_hbm, mask_ref, wq_hbm, bq_ref, asc_ref, aw_hbm, ab_ref, zw_hbm, zb_ref, wo_hbm, wup_hbm, wdn_hbm,
                   o_out, wg, gate_out, mod_out, nxt_out, w1g,
                   bias_v, bt, w_s, k_s, qt_s, vt_s, gt_s, lg, o_s, xraw, craw, xn, raw, aw_s, wst, wst1, cond,
                   ld_sem, cd_sem, b_sem, q_sem, a_sem, st_sem, o_send, o_recv, n_send, n_recv, n_free, w_send, w_recv, c_near, c_far, c_recv,
                   k_sem, d_far, d_recv):
    S, T, D, C, n_tp, n_dp, hd, hu, cut, n_chunk = dims
    p = Place(n_tp, n_dp)
    entered = p.enter(True)
    rows_w = hd + 3 * hu
    stage = _stage(0, hd, hu, wo_hbm, wup_hbm, wdn_hbm, wst, st_sem.at[0])
    stage1 = _stage(1, hd, hu, wo_hbm, wup_hbm, wdn_hbm, wst1, st_sem.at[1])
    R = S * T // n_tp
    mine = pl.ds(p.c * R, R)

    def sample_of(k):
        j = S - 1 - k
        return lax.rem(p.z + S + (1 - 2 * lax.rem(j, 2)) * ((j + 1) // 2), S)

    def loads(k, slot):
        s = sample_of(k)
        return [pltpu.make_async_copy(x_hbm.at[s, mine], xraw.at[slot], ld_sem.at[slot]),
                pltpu.make_async_copy(cond_hbm.at[s, mine], craw.at[slot], cd_sem.at[slot])]

    raws = [pltpu.make_async_copy(aw_hbm.at[0, 0], raw.at[0], a_sem.at[0]), pltpu.make_async_copy(zw_hbm.at[0], raw.at[1], a_sem.at[1]),
            pltpu.make_async_copy(aw_hbm.at[0, 1], raw.at[2], a_sem.at[2]), pltpu.make_async_copy(aw_hbm.at[1, 0], raw.at[0], a_sem.at[0])]
    raws[0].start()
    for k in range(2):
        for cp in loads(k, k):
            cp.start()
    bias_cp = _copy(bias_hbm.at[0, 0], bias_v, b_sem)
    qt_s[HP:, :] = jnp.zeros((HP, T), BF16)
    wq = _stage_qkvg(0, hd, wq_hbm, w_s, q_sem)
    for cp in stage:
        cp.wait()
    for cp in wq:
        cp.wait()
    for r in (1, 2):
        raws[r].start()
    cond_cp = pltpu.make_async_copy(cond_hbm.at[p.z, mine], cond, b_sem)
    entered()
    ring = Ring(p, lambda b, ch: wg.at[b, 0:cut, :], w_recv, w_send, 1)
    cross = Cross(p, wg, cut, rows_w, n_chunk, c_recv, c_near, c_far)
    cross1 = Cross(p, w1g, 0, rows_w, 1, d_recv, None, d_far, spread=False)
    ring.own(0, wst.at[0:cut, :])
    cross.own(wst)

    def half(slot, dst):
        v = xn.at[slot, mine]
        return pltpu.make_async_remote_copy(src_ref=v, dst_ref=v, send_sem=n_send.at[slot], recv_sem=n_recv.at[slot],
                                            device_id={"tp": p.partner}, device_id_type=MESH)

    def normalise(slot):
        tile = 256 if R % 256 == 0 else R
        for i in range(R // tile):
            rows = pl.ds(i * tile, tile)
            cn = _ln(craw[slot, rows, :].astype(F32))
            y = _ada(xraw[slot, rows, :].astype(F32), cn, asc_ref[0, 0:1, :], aw_s[...], ab_ref[0, 0:1, :])
            xn[slot, pl.ds(pl.multiple_of(p.c * R, R) + i * tile, tile), :] = y

    raws[0].wait()
    aw_s[...] = _flat(raw.at[0])
    for cp in loads(0, 0):
        cp.wait()
    normalise(0)
    bias_cp.wait()
    half(0, p.partner).start()
    _load_bias(bias_v, mask_ref, bt)
    cond_cp.start()
    for cp in stage1:
        cp.wait()
    keep = _copy(wst1, w1g.at[p.me], k_sem)
    ex = Exchange(p, sample_of, o_s, o_out, o_send, o_recv)
    brow = _bias_row(bq_ref[0:1, :], hd)
    events = {}

    def plan(when, f, *args):
        events.setdefault((when % 2, when // 2), []).append((f, args))

    for h in range(1, p.nz // 2 + 1):
        plan(2 * h - 2, ring.service, h, 0)
        for ch in range(n_chunk):
            plan(n_chunk * (h - 1) + ch, cross.along, h, ch)
            plan(n_chunk * h + ch + 1, cross.across, h, ch)
        plan(3 * h + 3, cross1.along, h, 0)
    plan(3, cross1.own, wst1)

    def step(k, _):
        slot = lax.rem(k, 2)

        @pl.when(k + 2 < S)
        def _():
            for cp in loads(k + 2, slot):
                cp.start()

        with scope("b0_half"):
            v = xn.at[slot, pl.ds((1 - p.c) * R, R)]
            pltpu.make_async_copy(v, v, n_recv.at[slot]).wait()
            half(slot, p.partner).wait_send()
        at = Attend(n_tp, hd, w_s, brow, bt, k_s, qt_s, vt_s, gt_s, lg, o_s, lambda i, tile: xn[slot, pl.ds(i * tile, tile), :])
        with scope("b0_proj"):
            at.project()

        @pl.when(k + 2 < S)
        def _():
            pl.semaphore_signal(n_free, inc=1, device_id={"tp": p.partner}, device_id_type=MESH)

        @pl.when(k >= 1)
        def _():
            ex.start(k - 1)

        with scope("b0_norm"):
            @pl.when(k + 1 < S)
            def _():
                for cp in loads(k + 1, 1 - slot):
                    cp.wait()
                normalise(1 - slot)

                @pl.when(k >= 1)
                def _():
                    pl.semaphore_wait(n_free, 1)

        def take(part):
            with scope("b0_ev"):
                for (half_step, when), todo in sorted(events.items(), key=lambda e: e[0]):
                    if half_step == part:
                        @pl.when(k == when)
                        def _():
                            for f, args in todo:
                                f(*args)

        take(0)

        def hook():
            @pl.when(k + 1 < S)
            def _():
                half(1 - slot, p.partner).start()

        with scope("b0_att"):
            at.attend(k, hook)
        take(1)
        return 0

    lax.fori_loop(0, S, step, 0)
    ex.start(S - 1)
    raws[3].start()
    with scope("b0_mods"):
        wg[p.me] = wst[...]
        cond_cp.wait()
        cn = _ln(cond[...].astype(F32))
        raws[1].wait()
        aw_s[...] = _flat(raw.at[1])
        _gates(gate_out, cond[...], aw_s[...], zb_ref.at[0])
        for src, cp, l, j, out in ((2, raws[2], 0, 1, mod_out), (0, raws[3], 1, 0, nxt_out)):
            cp.wait()
            aw_s[...] = _flat(raw.at[src])
            _modulation(out, cn, asc_ref[l, j:j + 1, :], aw_s[...], ab_ref[l, j:j + 1, :])
    for (half_step, when), todo in sorted(events.items(), key=lambda e: (e[0][1], e[0][0])):
        if when >= S:
            for f, args in todo:
                f(*args)

    def other(i, _):
        ring.wait(i * 2 + (1 - p.c), 0)
        return 0

    with scope("b0_ring_end"):
        lax.fori_loop(0, p.nz, other, 0)
        ring.drain(wg.at[0:n_tp - 1, 0:cut, :])
    with scope("b0_cross_end"):
        cross.finish_near()
        cross.finish_far()
        cross1.finish_far()
        keep.wait()
    with scope("b0_arr"):
        ex.finish()


def _head_scratch(S, T, D, hd):
    v = pltpu.VMEM
    return [v((T, T), BF16), v((T, T), F32), v((4 * HP, D), BF16), v((T, 2 * HP), BF16), v((2 * HP, T), BF16), v((HP, T), BF16),
            v((hd, T), F32), v((2, T, QT), F32), v((S, hd, T), BF16)]


def _block0(n_dp, x, cond, pair_bias, mask_row, wq, bq, asc, aw, ab, zw, zb, wo, wup, wdn):
    S, T, D = x.shape
    C = cond.shape[-1]
    _, _, hd, _ = wq.shape
    hu = wdn.shape[1]
    n_tp = S * 2
    rows_w = hd + 3 * hu
    R = T // 2
    cut, n_chunk = hd, 3
    dma = pltpu.SemaphoreType.DMA
    return pl.pallas_call(
        functools.partial(_block0_kernel, (S, T, D, C, n_tp, n_dp, hd, hu, cut, n_chunk)),
        out_shape=(pltpu.VMEM((n_tp, hd, R), BF16), pltpu.VMEM((n_tp, rows_w, D), BF16),
                   *[pltpu.VMEM((R, 2 * D), F32)] * 3, pltpu.HBM((n_tp, rows_w, D), BF16)),
        in_specs=[ANY, ANY, ANY, VMEM, ANY, VMEM, VMEM, ANY, VMEM, ANY, VMEM, ANY, ANY, ANY],
        out_specs=(VMEM,) * 5 + (HBM,),
        scratch_shapes=[
            *_head_scratch(S, T, D, hd),
            pltpu.VMEM((2, R, D), BF16), pltpu.VMEM((2, R, C), BF16), pltpu.VMEM((2, T, D), BF16),
            pltpu.VMEM((3, C, 2, D), BF16), pltpu.VMEM((C, 2 * D), BF16), *[pltpu.VMEM((rows_w, D), BF16)] * 2, pltpu.VMEM((R, C), BF16),
            dma((2,)), dma((2,)), dma, dma((4,)), dma((3,)), dma((2, 4)), dma((S, 2)), dma, dma((2,)), dma((2,)), pltpu.SemaphoreType.REGULAR,
            dma, dma((n_tp, 1)), dma, dma((S,)), dma((n_tp, n_chunk)), dma, dma((S,)), dma((n_tp, 1))],
        cost_estimate=pl.CostEstimate(flops=2 * S * T * (D * 4 * HP + 2 * T * 256 + C * D), bytes_accessed=S * T * (D + C), transcendentals=S * T * T),
        compiler_params=pltpu.CompilerParams(collective_id=0, has_side_effects=True, vmem_limit_bytes=VM0),
        name="block0",
    )(x, cond, pair_bias, mask_row, wq, bq, asc, aw, ab, zw, zb, wo, wup, wdn)


def _transition(dims, tile, gates, mod1, o_v, act, wall, y_s, h_s, rows):
    D, n_tp, hd, hu = dims
    w_o = wall[:, 0:hd, :].reshape(n_tp * hd, D)
    o_t = o_v[:, :, rows].reshape(n_tp * hd, tile)
    t = _dot(o_t, w_o, 0, 0).astype(BF16).astype(F32)
    mid = (act[rows, :].astype(F32) + gates[rows, :D] * t).astype(BF16).astype(F32)
    y_s[...] = (mod1[rows, :D] * _ln(mid) + mod1[rows, D:]).astype(BF16)
    step = 4 * hu
    for j in range(n_tp * hu // step):
        dv = slice(4 * j, 4 * j + 4)
        u1 = _dot(y_s[...], wall[dv, hd:hd + hu, :].reshape(step, D), 1, 1)
        u2 = _dot(y_s[...], wall[dv, hd + hu:hd + 2 * hu, :].reshape(step, D), 1, 1)
        h_s[:, j * step:(j + 1) * step] = (u1 * _sig(u1) * u2).astype(BF16)
    r = _dot(h_s[...], wall[:, hd + 2 * hu:hd + 3 * hu, :].reshape(n_tp * hu, D)).astype(BF16).astype(F32)
    return (mid + gates[rows, D:] * r).astype(BF16)


def _block1_kernel(dims, o0, w0, gate0, mod0, nxt0, act_hbm, cond_hbm, zw_hbm, zb_ref, asc_ref, aw_hbm, ab_ref, bias_hbm, mask_ref, wq_hbm, bq_ref, _,
                   w1, gate1, mod1, a_out, o_out, wg,
                   bias_v, bt, w_s, k_s, qt_s, vt_s, gt_s, lg, o_s, act, cond, raw, aw_s, y_s, h_s, xg,
                   l_sem, q_sem, wl_sem, x_send, x_recv, o_send, o_recv, c_near, c_far, c_recv):
    S, T, D, C, n_tp, n_dp, hd, hu = dims
    p = Place(n_tp, n_dp)
    entered = p.enter(True)
    R = S * T // n_tp
    row0 = p.me * R
    rows_w = hd + 3 * hu
    srcs = [(act_hbm.at[pl.ds(row0, R), :], act), (cond_hbm.at[pl.ds(row0, R), :], cond), (bias_hbm.at[1, 0], bias_v),
            (zw_hbm.at[1], raw.at[0]), (aw_hbm.at[1, 1], raw.at[1])]
    cps = [_copy(a, b, l_sem.at[i]) for i, (a, b) in enumerate(srcs)]
    qt_s[HP:, :] = jnp.zeros((HP, T), BF16)
    wq = _stage_qkvg(1, hd, wq_hbm, w_s, q_sem)
    cross = Cross(p, wg, 0, rows_w, 1, c_recv, c_near, c_far)
    cps[0].wait()
    tile = R // 2
    ring = Ring(p, lambda b, ch: xg.at[pl.ds(b * R + ch * tile, tile), :], x_recv, x_send, 2)
    for ch in range(2):
        rows = pl.ds(ch * tile, tile)
        with scope("b1_mlp"):
            new = _transition((D, n_tp, hd, hu), tile, gate0, mod0, o0, act, w0, y_s, h_s, rows)
            a_out[rows, :] = new
            xg[pl.ds(row0 + ch * tile, tile), :] = (nxt0[rows, :D] * _ln(new.astype(F32)) + nxt0[rows, D:]).astype(BF16)
        if ch == 0:
            with scope("b1_enter"):
                entered()
        ring.own(ch)
        if ch == 0:
            cross.hand_on()
    with scope("b1_bias"):
        cps[2].wait()
        _load_bias(bias_v, mask_ref, bt)
    for cp in wq:
        cp.wait()
    brow = _bias_row(bq_ref[1:2, :], hd)
    turn = 1 - 2 * p.c

    def sample_of(j):
        h = (j + 1) // 2
        return lax.rem(p.z + S + turn * (1 - 2 * lax.rem(j, 2)) * h, S)

    ex = Exchange(p, sample_of, o_s, o_out, o_send, o_recv)

    def step(j, _):
        with scope("b1_svc"):
            ring.service(j // 2 + 1, lax.rem(j, 2))

        @pl.when((j >= 2) & (j <= p.nz // 2 + 1))
        def _():
            with scope("b1_x"):
                cross.across(j - 1, 0)

        @pl.when(j >= 1)
        def _():
            ex.start(j - 1)

        s = sample_of(j)
        with scope("b1_half"):
            for ch in range(2):
                ring.wait(s * 2 + (1 - p.c), ch)

        def x_rows(i, t):
            return xg[pl.ds(pl.multiple_of(s * T, T) + i * t, t), :]

        at = Attend(n_tp, hd, w_s, brow, bt, k_s, qt_s, vt_s, gt_s, lg, o_s, x_rows)
        with scope("b1_proj"):
            at.project()

        with scope("b1_att"):
            at.attend(j)

        @pl.when(j == 1)
        def _():
            cps[1].wait()
            cps[3].wait()
            aw_s[...] = _flat(raw.at[0])
            _gates(gate1, cond[...], aw_s[...], zb_ref.at[1])

        @pl.when(j == 3)
        def _():
            cps[4].wait()
            aw_s[...] = _flat(raw.at[1])
            cn = _ln(cond[...].astype(F32))
            _modulation(mod1, cn, asc_ref[1, 1:2, :], aw_s[...], ab_ref[1, 1:2, :])

        with scope("b1_fin"):
            @pl.when(j == S - 2)
            def _():
                cross.finish_near()
                pltpu.make_async_copy(wg, w1, wl_sem).start()

        return 0

    lax.fori_loop(0, S, step, 0)
    ex.start(S - 1)
    cross.finish_far(ring=False)
    pltpu.make_async_copy(wg, w1, wl_sem).wait()
    with scope("b1_drain"):
        ring.drain(xg.at[0:(n_tp - 1) * R, :])
    with scope("b1_arr"):
        ex.finish()


def _block1(n_dp, o0, w0, gate0, mod0, nxt0, act, cond, zw, zb, asc, aw, ab, pair_bias, mask_row, wq, bq, wg):
    n_tp, hd, R = o0.shape
    D = act.shape[-1]
    C = cond.shape[-1]
    S = n_tp // 2
    T = 2 * R
    rows_w = w0.shape[1]
    hu = (rows_w - hd) // 3
    dma = pltpu.SemaphoreType.DMA
    return pl.pallas_call(
        functools.partial(_block1_kernel, (S, T, D, C, n_tp, n_dp, hd, hu)),
        out_shape=(pltpu.VMEM((n_tp, rows_w, D), BF16), pltpu.VMEM((R, 2 * D), F32), pltpu.VMEM((R, 2 * D), F32),
                   pltpu.VMEM((R, D), BF16), pltpu.VMEM((n_tp, hd, R), BF16), pltpu.HBM((n_tp, rows_w, D), BF16)),
        in_specs=[VMEM, VMEM, VMEM, VMEM, VMEM, ANY, ANY, ANY, VMEM, VMEM, ANY, VMEM, ANY, VMEM, ANY, VMEM, HBM],
        out_specs=(VMEM,) * 5 + (HBM,),
        input_output_aliases={1: 0, 2: 1, 3: 2, 16: 5},
        scratch_shapes=[
            *_head_scratch(S, T, D, hd),
            pltpu.VMEM((R, D), BF16), pltpu.VMEM((R, C), BF16), pltpu.VMEM((2, C, 2, D), BF16), pltpu.VMEM((C, 2 * D), BF16),
            pltpu.VMEM((R // 2, D), BF16), pltpu.VMEM((R // 2, n_tp * hu), BF16), pltpu.VMEM((S * T, D), BF16),
            dma((5,)), dma((4,)), dma, dma, dma((n_tp, 2)), dma((S, 2)), dma, dma, dma((S,)), dma((n_tp, 1))],
        cost_estimate=pl.CostEstimate(flops=2 * S * T * (D * 4 * HP + 2 * T * 256), bytes_accessed=S * T * D * 2, transcendentals=S * T * T),
        compiler_params=pltpu.CompilerParams(collective_id=1, has_side_effects=True, vmem_limit_bytes=VM1),
        name="block1",
    )(o0, w0, gate0, mod0, nxt0, act, cond, zw, zb, asc, aw, ab, pair_bias, mask_row, wq, bq, wg)


def _last_kernel(dims, o_v, act, wall, gate, mod, out, y_s, h_s, x_send, x_recv):
    D, n_tp, n_dp, hd, hu, R = dims
    p = Place(n_tp, n_dp)
    entered = p.enter(False)
    tile = R // 2
    ring = Ring(p, lambda b, ch: out.at[pl.ds(b * R + ch * tile, tile), :], x_recv, x_send, 2)
    for ch in range(2):
        rows = pl.ds(ch * tile, tile)
        with scope("l_mlp"):
            out[pl.ds(p.me * R + ch * tile, tile), :] = _transition((D, n_tp, hd, hu), tile, gate, mod, o_v, act, wall, y_s, h_s, rows)
        if ch == 0:
            entered()
        ring.own(ch)

    with scope("l_svc"):
        lax.fori_loop(0, p.nz, lambda e, _: (ring.service(e // 2 + 1, lax.rem(e, 2)), 0)[1], 0)

    def other(i, _):
        for ch in range(2):
            ring.wait(i * 2 + (1 - p.c), ch)
        return 0

    with scope("l_end"):
        lax.fori_loop(0, p.nz, other, 0)
    ring.drain(out.at[0:(n_tp - 1) * R, :])


def _last(n_dp, o, act, w1, gate, mod):
    n_tp, hd, R = o.shape
    D = act.shape[-1]
    hu = (w1.shape[1] - hd) // 3
    dma = pltpu.SemaphoreType.DMA
    return pl.pallas_call(
        functools.partial(_last_kernel, (D, n_tp, n_dp, hd, hu, R)),
        out_shape=pltpu.VMEM((n_tp * R, D), BF16),
        in_specs=[VMEM] * 5, out_specs=VMEM,
        scratch_shapes=[pltpu.VMEM((R // 2, D), BF16), pltpu.VMEM((R // 2, n_tp * hu), BF16), dma, dma((n_tp, 2))],
        cost_estimate=pl.CostEstimate(flops=2 * R * D * (D + 3 * n_tp * hu), bytes_accessed=w1.size, transcendentals=R * D),
        compiler_params=pltpu.CompilerParams(collective_id=2, has_side_effects=True, vmem_limit_bytes=VM2),
        name="last",
    )(o, act, w1, gate, mod)


def _store_kernel(src, dst, sem):
    cp = pltpu.make_async_copy(src, dst, sem)
    cp.start()
    cp.wait()


def _store(x):
    return pl.pallas_call(
        _store_kernel, out_shape=jax.ShapeDtypeStruct(x.shape, x.dtype), in_specs=[VMEM], out_specs=ANY,
        scratch_shapes=[pltpu.SemaphoreType.DMA], compiler_params=pltpu.CompilerParams(vmem_limit_bytes=1 << 20), name="store")(x)


def solution(mesh):
    n_dp = mesh.shape["dp"]

    def shard_body(token_act, token_cond, pair_bias, token_mask, ada_scale, ada_w, ada_bias, zero_w, zero_b, w_qkvg, b_q, w_o, w_up, w_down):
        S, T, D = token_act.shape
        C = token_cond.shape[-1]
        mask_row = token_mask.reshape(1, T)
        wq = jnp.transpose(w_qkvg, (0, 2, 3, 1))
        wup = jnp.transpose(w_up, (0, 2, 3, 1))
        act = token_act.reshape(S * T, D)
        cond = token_cond.reshape(S * T, C)
        o0, w0, gate0, mod0, nxt0, wg = _block0(n_dp, token_act, token_cond, pair_bias, mask_row, wq, b_q, ada_scale, ada_w, ada_bias, zero_w, zero_b, w_o, wup, w_down)
        o0, w0, gate0, mod0, nxt0 = (pltpu.with_memory_space_constraint(v, pltpu.VMEM) for v in (o0, w0, gate0, mod0, nxt0))
        w1, gate1, mod1, a1, o1, _ = _block1(n_dp, o0, w0, gate0, mod0, nxt0, act, cond, zero_w, zero_b, ada_scale, ada_w, ada_bias, pair_bias, mask_row, wq, b_q, wg)
        o1, a1, w1, gate1, mod1 = (pltpu.with_memory_space_constraint(v, pltpu.VMEM) for v in (o1, a1, w1, gate1, mod1))
        out = pltpu.with_memory_space_constraint(_last(n_dp, o1, a1, w1, gate1, mod1), pltpu.VMEM)
        return _store(out).reshape(S, T, D)

    everywhere = P()
    rows, second, fourth = P('dp'), P(None, 'tp'), P(*[None] * 3, 'tp')
    in_specs = (rows, rows, second) + (everywhere,) * 6 + (fourth, second, second, fourth, second)
    return jax.shard_map(shard_body, mesh=mesh, in_specs=in_specs, out_specs=rows, check_vma=False)
```

time: 247 us -> 238 us (0.964)
  the two profiles are of different devices: /device:TPU:21 before, /device:TPU:93 now
where the time goes in v5:
time: 238 us
  Pallas kernels  238 us (100%)
    pallas_call x1, Pallas kernels, _block1(): pl.pallas_call(functools.partial(_block1_kernel, (S, T, D, C, n_tp, n_dp,...  92.9 us
    pallas_call x1, Pallas kernels, _block0(): pl.pallas_call(functools.partial(_block0_kernel, (S, T, D, C, n_tp, n_dp,...  70.8 us
    pallas_call x1, Pallas kernels, _last(): pl.pallas_call(functools.partial(_last_kernel, (D, n_tp, n_dp, hd, hu, R)...  69.3 us
    pallas_call x1, Pallas kernels, _store(): pl.pallas_call(_store_kernel, out_shape=jax.ShapeDtypeStruct(x.shape, x.d...  4.79 us

profile of v5, /device:TPU:93, one launch (start us, length us, event | category | flops | bytes accessed | tf_op | source)
XLA Modules:
  0.0 237.9 jit_solution(2423668588945386301)
XLA Ops:
  0.0 70.8 %block0.1 = (bf16[16,48,512]{2,1,0:T(8,128)(2,1)S(1)}, bf16[16,336,768]{2,1,0:T(8,128)(2,1)S(1)}, f32[512,1536]{1,0:T(8,128)S(1)}, f32[512,1536]{1,0:T(8,128)S(1...) custom-call(bf16[8,1024,768]{2,1,0:T(8,128)(2,1)} %x_hbm.1, bf16[8,1024,384]{2,1,0:T(8,128)(2,1)} %cond_hbm.1, ...), custom_call_target="tpu_custom_call" | custom-call | flops 16642998272 | bytes 9437184 | tf_op jit(solution)/shard_map/block0/pallas_call | solution.py:584
  70.8 92.9 %block1.1 = (bf16[16,336,768]{2,1,0:T(8,128)(2,1)S(1)}, f32[512,1536]{1,0:T(8,128)S(1)}, f32[512,1536]{1,0:T(8,128)S(1)}, bf16[512,768]{1,0:T(8,128)(2,1)S(1)}, ...) custom-call(bf16[16,48,512]{2,1,0:T(8,128)(2,1)S(1)} %get-tuple-elem, ...), custom_call_target="tpu_custom_call", output_to_operand_aliasing={{0}: (1, {}), {1}: (2, {}), {2}: (3, {}), {5}: (16, {})} | custom-call | flops 11811160064 | bytes 12582912 | tf_op jit(solution)/shard_map/block1/pallas_call | solution.py:733
  163.7 69.3 %last.1.src = bf16[8192,768]{1,0:T(8,128)(2,1)S(1)} custom-call(bf16[16,48,512]{2,1,0:T(8,128)(2,1)S(1)} %get-tuple-element.22.o_v, bf16[512,768]{1,0:T(8,128)(2,1)S(1)} %get-tuple-element.23.act, bf16[16,336,768]{2,1,0:T(8,128)(2,1)S(1)} %get-tuple-element.24.wall, f32[512,1536]{1,0:T(8,128)S(1)} %get-tuple-element.25.gate, ...), custom_call_target="tpu_custom_call" | custom-call | flops 4227858432 | bytes 4128768 | tf_op jit(solution)/shard_map/last/pallas_call | solution.py:783
  233.0 4.8 %store.1 = bf16[8192,768]{1,0:T(8,128)(2,1)} custom-call(bf16[8192,768]{1,0:T(8,128)(2,1)S(1)} %last.1.src), custom_call_target="tpu_custom_call" | custom-call | tf_op jit(solution)/shard_map/store/pallas_call | solution.py:801

commit v6 on v5

--- a/solution.py
+++ b/solution.py
@@ -73,9 +73,10 @@
 
 
 class Ring:
-    def __init__(self, place, view, recv_sem, send_sem, n_chunk):
-        self.p, self.view, self.recv, self.send, self.n_chunk = place, view, recv_sem, send_sem, n_chunk
+    def __init__(self, place, view, recv_sem, send_sem, right=None):
+        self.p, self.view, self.recv, self.send = place, view, recv_sem, send_sem
         self.far = place.nz // 2
+        self.right = right or (lambda ch: place.c == 0)
 
     def _push(self, b, ch, dst, src=None):
         v = self.view(b, ch)
@@ -95,14 +96,15 @@
 
     def service(self, h, ch):
         p = self.p
-        for sign, core in ((1, 0), (-1, 1)):
+        right = self.right(ch)
+        for sign, far in ((1, right), (-1, jnp.logical_not(right))):
             b = p.at(-sign * h)
 
-            @pl.when((h < self.far) | (p.c == core))
+            @pl.when((h < self.far) | far)
             def _():
                 self.wait(b, ch)
 
-                @pl.when((h < self.far - 1) | ((h == self.far - 1) & (p.c == core)))
+                @pl.when((h < self.far - 1) | ((h == self.far - 1) & far))
                 def _():
                     self._push(b, ch, p.at(sign))
 
@@ -428,9 +430,9 @@
         raws[r].start()
     cond_cp = pltpu.make_async_copy(cond_hbm.at[p.z, mine], cond, b_sem)
     entered()
-    ring = Ring(p, lambda b, ch: wg.at[b, 0:cut, :], w_recv, w_send, 1)
+    ring = Ring(p, lambda b, ch: wg.at[b, 0:cut, :], w_recv, w_send)
     cross = Cross(p, wg, cut, rows_w, n_chunk, c_recv, c_near, c_far)
-    cross1 = Cross(p, w1g, 0, rows_w, 1, d_recv, None, d_far, spread=False)
+    cross1 = Cross(p, w1g, 0, rows_w, n_chunk, d_recv, None, d_far, spread=False)
     ring.own(0, wst.at[0:cut, :])
     cross.own(wst)
 
@@ -471,8 +473,8 @@
         for ch in range(n_chunk):
             plan(n_chunk * (h - 1) + ch, cross.along, h, ch)
             plan(n_chunk * h + ch + 1, cross.across, h, ch)
-        plan(3 * h + 3, cross1.along, h, 0)
-    plan(3, cross1.own, wst1)
+            plan(n_chunk * h + ch + S // 2, cross1.along, h, ch)
+    plan(n_chunk, cross1.own, wst1)
 
     def step(k, _):
         slot = lax.rem(k, 2)
@@ -592,7 +594,7 @@
             pltpu.VMEM((2, R, D), BF16), pltpu.VMEM((2, R, C), BF16), pltpu.VMEM((2, T, D), BF16),
             pltpu.VMEM((3, C, 2, D), BF16), pltpu.VMEM((C, 2 * D), BF16), *[pltpu.VMEM((rows_w, D), BF16)] * 2, pltpu.VMEM((R, C), BF16),
             dma((2,)), dma((2,)), dma, dma((4,)), dma((3,)), dma((2, 4)), dma((S, 2)), dma, dma((2,)), dma((2,)), pltpu.SemaphoreType.REGULAR,
-            dma, dma((n_tp, 1)), dma, dma((S,)), dma((n_tp, n_chunk)), dma, dma((S,)), dma((n_tp, 1))],
+            dma, dma((n_tp, 1)), dma, dma((S,)), dma((n_tp, n_chunk)), dma, dma((S,)), dma((n_tp, n_chunk))],
         cost_estimate=pl.CostEstimate(flops=2 * S * T * (D * 4 * HP + 2 * T * 256 + C * D), bytes_accessed=S * T * (D + C), transcendentals=S * T * T),
         compiler_params=pltpu.CompilerParams(collective_id=0, has_side_effects=True, vmem_limit_bytes=VM0),
         name="block0",
@@ -634,7 +636,8 @@
     cross = Cross(p, wg, 0, rows_w, 1, c_recv, c_near, c_far)
     cps[0].wait()
     tile = R // 2
-    ring = Ring(p, lambda b, ch: xg.at[pl.ds(b * R + ch * tile, tile), :], x_recv, x_send, 2)
+    ring = Ring(p, lambda b, ch: xg.at[pl.ds(b * R + ch * tile, tile), :], x_recv, x_send,
+                lambda ch: p.c + ch == 0)
     for ch in range(2):
         rows = pl.ds(ch * tile, tile)
         with scope("b1_mlp"):
@@ -753,7 +756,7 @@
     p = Place(n_tp, n_dp)
     entered = p.enter(False)
     tile = R // 2
-    ring = Ring(p, lambda b, ch: out.at[pl.ds(b * R + ch * tile, tile), :], x_recv, x_send, 2)
+    ring = Ring(p, lambda b, ch: out.at[pl.ds(b * R + ch * tile, tile), :], x_recv, x_send)
     for ch in range(2):
         rows = pl.ds(ch * tile, tile)
         with scope("l_mlp"):

time: 238 us -> 239 us (level)
  the two profiles are of different devices: /device:TPU:93 before, /device:TPU:21 now
where the time goes in v6:
time: 239 us; the launch traced here: 238 us
  Pallas kernels  237 us (99%)
    pallas_call x1, Pallas kernels, _block1(): pl.pallas_call(functools.partial(_block1_kernel, (S, T, D, C, n_tp, n_dp,...  85.9 us
    pallas_call x1, Pallas kernels, _block0(): pl.pallas_call(functools.partial(_block0_kernel, (S, T, D, C, n_tp, n_dp,...  73.8 us
    pallas_call x1, Pallas kernels, _last(): pl.pallas_call(functools.partial(_last_kernel, (D, n_tp, n_dp, hd, hu, R)...  72.8 us
    pallas_call x1, Pallas kernels, _store(): pl.pallas_call(_store_kernel, out_shape=jax.ShapeDtypeStruct(x.shape, x.d...  4.79 us

profile of v6, /device:TPU:21, one launch (start us, length us, event | category | flops | bytes accessed | tf_op | source)
XLA Modules:
  0.0 237.6 jit_solution(13502641824071935506)
XLA Ops:
  0.0 73.8 %block0.1 = (bf16[16,48,512]{2,1,0:T(8,128)(2,1)S(1)}, bf16[16,336,768]{2,1,0:T(8,128)(2,1)S(1)}, f32[512,1536]{1,0:T(8,128)S(1)}, f32[512,1536]{1,0:T(8,128)S(1...) custom-call(bf16[8,1024,768]{2,1,0:T(8,128)(2,1)} %x_hbm.1, bf16[8,1024,384]{2,1,0:T(8,128)(2,1)} %cond_hbm.1, ...), custom_call_target="tpu_custom_call" | custom-call | flops 16642998272 | bytes 9437184 | tf_op jit(solution)/shard_map/block0/pallas_call | solution.py:586
  73.8 85.9 %block1.1 = (bf16[16,336,768]{2,1,0:T(8,128)(2,1)S(1)}, f32[512,1536]{1,0:T(8,128)S(1)}, f32[512,1536]{1,0:T(8,128)S(1)}, bf16[512,768]{1,0:T(8,128)(2,1)S(1)}, ...) custom-call(bf16[16,48,512]{2,1,0:T(8,128)(2,1)S(1)} %get-tuple-elem, ...), custom_call_target="tpu_custom_call", output_to_operand_aliasing={{0}: (1, {}), {1}: (2, {}), {2}: (3, {}), {5}: (16, {})} | custom-call | flops 11811160064 | bytes 12582912 | tf_op jit(solution)/shard_map/block1/pallas_call | solution.py:736
  159.8 72.8 %last.1.src = bf16[8192,768]{1,0:T(8,128)(2,1)S(1)} custom-call(bf16[16,48,512]{2,1,0:T(8,128)(2,1)S(1)} %get-tuple-element.22.o_v, bf16[512,768]{1,0:T(8,128)(2,1)S(1)} %get-tuple-element.23.act, bf16[16,336,768]{2,1,0:T(8,128)(2,1)S(1)} %get-tuple-element.24.wall, f32[512,1536]{1,0:T(8,128)S(1)} %get-tuple-element.25.gate, ...), custom_call_target="tpu_custom_call" | custom-call | flops 4227858432 | bytes 4128768 | tf_op jit(solution)/shard_map/last/pallas_call | solution.py:786
  232.6 4.8 %store.1 = bf16[8192,768]{1,0:T(8,128)(2,1)} custom-call(bf16[8192,768]{1,0:T(8,128)(2,1)S(1)} %last.1.src), custom_call_target="tpu_custom_call" | custom-call | tf_op jit(solution)/shard_map/store/pallas_call | solution.py:804

commit v7 on v6

v7 whole, which is shorter than its diff:
```python
import functools
import math

import jax
import jax.numpy as jnp
from jax import lax
from jax.experimental import pallas as pl
from jax.experimental.pallas import tpu as pltpu
from jax.sharding import PartitionSpec as P

LN_EPS = 1e-5
LOG2E = 1.4426950408889634
MESH = pl.DeviceIdType.MESH
BF16 = jnp.bfloat16
F32 = jnp.float32
scope = jax.named_scope
HP = 64
QT = 256
ANY = pl.BlockSpec(memory_space=pl.ANY)
VMEM = pl.BlockSpec(memory_space=pltpu.VMEM)
HBM = pl.BlockSpec(memory_space=pltpu.HBM)
VM = 50 << 20


def _ln(x):
    mean = jnp.mean(x, axis=-1, keepdims=True)
    cen = x - mean
    var = jnp.mean(cen * cen, axis=-1, keepdims=True)
    return cen * lax.rsqrt(var + LN_EPS)


def _sig(x):
    return 0.5 * jnp.tanh(0.5 * x) + 0.5


def _dot(a, b, ca=1, cb=0):
    return lax.dot_general(a, b, (((ca,), (cb,)), ((), ())), preferred_element_type=F32)


def _ada(x_f32, cond_normed, scale, w, bias):
    d = x_f32.shape[-1]
    mod = _dot((cond_normed * scale).astype(BF16), w)
    return (_sig(mod[:, :d] + bias) * _ln(x_f32) + mod[:, d:]).astype(BF16)


class Place:
    def __init__(self, n_tp, n_dp):
        self.n = n_tp
        self.n_dp = n_dp
        self.col = lax.axis_index("dp")
        self.nz = n_tp // 2
        self.me = lax.axis_index("tp")
        self.z = self.me // 2
        self.c = lax.rem(self.me, 2)
        self.partner = self.z * 2 + (1 - self.c)

    def at(self, off):
        return lax.rem(self.z + off + self.nz, self.nz) * 2 + self.c

    def column(self, i):
        return lax.rem(self.col + i, self.n_dp)

    def enter(self):
        barrier = pltpu.get_barrier_semaphore()
        peers = [{"tp": lax.rem(self.me + i, self.n)} for i in range(1, self.n)]
        peers += [{"dp": self.column(i), "tp": self.me} for i in range(1, self.n_dp)]
        for peer in peers:
            pl.semaphore_signal(barrier, inc=1, device_id=peer, device_id_type=MESH)
        return lambda: pl.semaphore_wait(barrier, len(peers))


class Ring:
    def __init__(self, place, view, recv_sem, send_sem, right=None):
        self.p, self.view, self.recv, self.send = place, view, recv_sem, send_sem
        self.far = place.nz // 2
        self.right = right or (lambda ch: place.c == 0)

    def _push(self, b, ch, dst, src=None):
        v = self.view(b, ch)
        pltpu.make_async_remote_copy(
            src_ref=v if src is None else src, dst_ref=v, send_sem=self.send, recv_sem=self.recv.at[b, ch],
            device_id={"tp": dst}, device_id_type=MESH).start()

    def own(self, ch, src=None):
        p = self.p
        self._push(p.me, ch, p.at(1), src)
        self._push(p.me, ch, p.at(-1), src)
        self._push(p.me, ch, p.partner, src)

    def wait(self, b, ch):
        v = self.view(b, ch)
        pltpu.make_async_copy(v, v, self.recv.at[b, ch]).wait()

    def service(self, h, ch):
        p = self.p
        right = self.right(ch)
        for sign, far in ((1, right), (-1, jnp.logical_not(right))):
            b = p.at(-sign * h)

            @pl.when((h < self.far) | far)
            def _():
                self.wait(b, ch)

                @pl.when((h < self.far - 1) | ((h == self.far - 1) & far))
                def _():
                    self._push(b, ch, p.at(sign))

                self._push(b, ch, p.partner)

    def drain(self, whole):
        pltpu.make_async_copy(whole, whole, self.send).wait()


class Cross:
    def __init__(self, place, buf, lo, hi, n_chunk, recv_sem, near_sem, far_sem, spread=True):
        self.p, self.buf, self.lo, self.hi, self.n_chunk, self.spread = place, buf, lo, hi, n_chunk, spread
        self.recv, self.near, self.far_sem = recv_sem, near_sem, far_sem
        self.far = place.nz // 2
        self.size = (hi - lo) // n_chunk

    def _rows(self, ch):
        return pl.ds(self.lo + ch * self.size, self.size)

    def _push(self, b, ch, dst, sem, src=None):
        v = self.buf.at[b, self._rows(ch), :]
        pltpu.make_async_remote_copy(
            src_ref=v if src is None else src, dst_ref=v, send_sem=sem, recv_sem=self.recv.at[b, ch],
            device_id=dst, device_id_type=MESH).start()

    def _push_over(self, b, ch, plane):
        p = self.p

        @pl.when(plane)
        def _():
            for i in range(1, p.n_dp):
                self._push(b, ch, {"dp": p.column(i), "tp": p.me}, self.far_sem.at[b // 2])

        self._push(b, ch, {"tp": p.partner}, self.near)

    def _mine(self, b):
        return lax.rem(b, self.p.n_dp) == self.p.col

    def own(self, src):
        p = self.p
        for ch in range(self.n_chunk):
            part = src.at[self._rows(ch), :]

            @pl.when(self._mine(p.me))
            def _():
                for off in (1, -1):
                    self._push(p.me, ch, {"tp": p.at(off)}, self.far_sem.at[p.z], part)

            if self.spread:
                self._push(p.me, ch, {"tp": p.partner}, self.near, part)

    def wait(self, b, ch):
        v = self.buf.at[b, self._rows(ch), :]
        pltpu.make_async_copy(v, v, self.recv.at[b, ch]).wait()

    def _each(self, h, body):
        p = self.p
        for sign, core in ((1, 0), (-1, 1)):
            b = p.at(-sign * h)

            @pl.when((h < self.far) | (p.c == core))
            def _():
                body(b, sign, (h < self.far - 1) | ((h == self.far - 1) & (p.c == core)))

    def along(self, h, ch):
        p = self.p

        def body(b, sign, onward):
            @pl.when(self._mine(b))
            def _():
                self.wait(b, ch)

                @pl.when(onward)
                def _():
                    self._push(b, ch, {"tp": p.at(sign)}, self.far_sem.at[b // 2])

                if self.spread:
                    self._push_over(b, ch, True)

        self._each(h, body)

    def hand_on(self):
        p = self.p

        def block(i, _):
            b = i * 2 + p.c

            @pl.when(self._mine(b) | (i == p.z))
            def _():
                for ch in range(self.n_chunk):
                    self._push_over(b, ch, i != p.z)
            return 0

        lax.fori_loop(0, p.nz, block, 0)

    def across(self, h, ch):
        p = self.p

        def body(b, sign, onward):
            @pl.when(jnp.logical_not(self._mine(b)))
            def _():
                self.wait(b, ch)
                self._push(b, ch, {"tp": p.partner}, self.near)

        self._each(h, body)

    def _sent(self, k, sem):
        if k:
            v = self.buf.at[0:k, self.lo:self.hi, :]
            pltpu.make_async_copy(v, v, sem).wait()

    def finish_near(self):
        p = self.p

        def other(i, _):
            for ch in range(self.n_chunk):
                self.wait(i * 2 + (1 - p.c), ch)
            return 0

        lax.fori_loop(0, p.nz, other, 0)
        self._sent(p.nz, self.near)

    def finish_far(self, ring=True):
        p = self.p
        over = p.n_dp - 1 if self.spread else 0
        if ring:
            @pl.when(self._mine(p.me))
            def _():
                self._sent(2, self.far_sem.at[p.z])

        def body(b, sign, onward):
            sem = self.far_sem.at[b // 2]

            @pl.when(self._mine(b))
            def _():
                if not ring:
                    self._sent(over, sem)
                else:
                    @pl.when(onward)
                    def _():
                        self._sent(over + 1, sem)

                    @pl.when(jnp.logical_not(onward))
                    def _():
                        self._sent(over, sem)

        def hop(h, _):
            self._each(h, body)
            return 0

        lax.fori_loop(1, self.far + 1, hop, 0)


def _copy(src, dst, sem):
    cp = pltpu.make_async_copy(src, dst, sem)
    cp.start()
    return cp


def _stage(l, hd, hu, wo_hbm, wup_hbm, wdn_hbm, wst, sem):
    cps, lo = [], 0
    for src, rows in ((wo_hbm.at[l], hd), (wup_hbm.at[l, 0], hu), (wup_hbm.at[l, 1], hu), (wdn_hbm.at[l], hu)):
        cps.append(_copy(src, wst.at[pl.ds(lo, rows), :], sem.at[len(cps)]))
        lo += rows
    return cps


def _stage_qkvg(l, hd, wq_hbm, w_s, sem):
    return [_copy(wq_hbm.at[l, f], w_s.at[pl.ds(i * HP, hd), :], sem.at[i]) for i, f in enumerate((1, 0, 2, 3))]


class Attend:
    def __init__(self, n_tp, hd, w, brow, bt, k_s, qt_s, vt_s, gt_s, lg, o_s, x_rows):
        self.__dict__.update(locals())
        self.T = bt.shape[0]

    def project(self):
        T, hd = self.T, self.hd
        tile = QT
        for i in range(T // tile):
            rows = pl.ds(i * tile, tile)
            res = _dot(self.x_rows(i, tile), self.w[...], 1, 1) + self.brow
            self.k_s[rows, :] = res[:, :2 * HP].astype(BF16)
            rest = res.T
            self.qt_s[0:HP, rows] = rest[HP:2 * HP].astype(BF16)
            ones = lax.broadcasted_iota(jnp.int32, (HP, tile), 0) == hd
            self.vt_s[:, rows] = jnp.where(ones, 1.0, rest[2 * HP:3 * HP]).astype(BF16)
            self.gt_s[:, rows] = _sig(rest[3 * HP:3 * HP + hd])

    def attend(self, slot, hook=None):
        T, hd = self.T, self.hd
        n = T // QT
        c1 = LOG2E / math.sqrt(hd)

        def scores(i):
            cols = pl.ds(i * QT, QT)
            logits = _dot(self.k_s[...], self.qt_s[:, cols]) * c1 + self.bt[:, cols]
            self.lg[i % 2] = logits
            return jnp.max(logits, axis=0, keepdims=True)

        top = scores(0)
        if hook is not None:
            hook()
        for i in range(n):
            cols = pl.ds(i * QT, QT)
            nxt = scores(i + 1) if i + 1 < n else None
            probs = jnp.exp2(self.lg[i % 2] - top).astype(BF16)
            mixed = _dot(self.vt_s[...], probs)
            self.o_s[slot, :, cols] = (self.gt_s[:, cols] * (mixed[:hd] / mixed[hd:hd + 1])).astype(BF16)
            top = nxt


def _load_bias(bias_v, mask_ref, bt):
    T = bt.shape[0]
    mask_add = (mask_ref[...].astype(F32) - 1.0) * 1e9

    def step(i, _):
        r = pl.multiple_of(i * 128, 128)
        rows = (bias_v[pl.ds(r, 128), :].astype(F32) + mask_add) * LOG2E
        bt[:, pl.ds(r, 128)] = rows.T
        return 0

    lax.fori_loop(0, T // 128, step, 0)


class Exchange:
    def __init__(self, place, sample_of, o_s, o_out, send_sem, recv_sem):
        self.p, self.sample_of, self.o_s, self.o_out, self.send, self.recv = place, sample_of, o_s, o_out, send_sem, recv_sem
        self.half = o_s.shape[-1] // 2

    def _each(self, k, remote, local):
        p = self.p
        for c in range(2):
            dst = self.sample_of(k) * 2 + c
            src = self.o_s.at[k, :, pl.ds(c * self.half, self.half)]
            sem = self.send.at[k, c]
            cp = pltpu.make_async_remote_copy(
                src_ref=src, dst_ref=self.o_out.at[p.me], send_sem=sem, recv_sem=self.recv,
                device_id={"tp": dst}, device_id_type=MESH)

            @pl.when(dst != p.me)
            def _():
                remote(cp)

            @pl.when(dst == p.me)
            def _():
                local(pltpu.make_async_copy(src, self.o_out.at[p.me], sem))

    def start(self, k):
        self._each(k, lambda cp: cp.start(), lambda cp: cp.start())

    def sent(self):
        def one(k, _):
            self._each(k, lambda cp: cp.wait_send(), lambda cp: cp.wait())
            return 0

        lax.fori_loop(0, self.o_s.shape[0], one, 0)

    def arrived(self):
        rest = self.o_out.at[0:self.p.n - 1]
        pltpu.make_async_copy(rest, rest, self.recv).wait()


def _bias_row(bq, hd):
    return jnp.concatenate([jnp.zeros((1, HP), F32), bq, jnp.zeros((1, 3 * HP - hd), F32)], axis=1)


def _gates(out, cond, w, bias):
    d = bias.shape[-1]
    out[...] = _dot(cond, w)
    for j in range(bias.shape[0]):
        cols = pl.ds(j * d, d)
        out[:, cols] = _sig(out[:, cols] + bias[j:j + 1, :])


def _modulation(out, cond_normed, scale, w, bias):
    d = bias.shape[-1]
    out[...] = _dot((cond_normed * scale).astype(BF16), w)
    out[:, :d] = _sig(out[:, :d] + bias)


def _flat(raw):
    c, two, d = raw.shape
    return raw[...].reshape(c, two * d)


def _transition(dims, tile, gates, mod1, o_v, act, wall, y_s, h_s, rows):
    D, n_tp, hd, hu = dims
    w_o = wall[:, 0:hd, :].reshape(n_tp * hd, D)
    o_t = o_v[:, :, rows].reshape(n_tp * hd, tile)
    t = _dot(o_t, w_o, 0, 0).astype(BF16).astype(F32)
    mid = (act[rows, :].astype(F32) + gates[rows, :D] * t).astype(BF16).astype(F32)
    y_s[...] = (mod1[rows, :D] * _ln(mid) + mod1[rows, D:]).astype(BF16)
    step = 4 * hu
    for j in range(n_tp * hu // step):
        dv = slice(4 * j, 4 * j + 4)
        u1 = _dot(y_s[...], wall[dv, hd:hd + hu, :].reshape(step, D), 1, 1)
        u2 = _dot(y_s[...], wall[dv, hd + hu:hd + 2 * hu, :].reshape(step, D), 1, 1)
        h_s[:, j * step:(j + 1) * step] = (u1 * _sig(u1) * u2).astype(BF16)
    r = _dot(h_s[...], wall[:, hd + 2 * hu:hd + 3 * hu, :].reshape(n_tp * hu, D)).astype(BF16).astype(F32)
    return (mid + gates[rows, D:] * r).astype(BF16)


def _main_kernel(dims, x_hbm, cond_hbm, bias_hbm, mask_ref, wq_hbm, bq_ref, asc_ref, aw_hbm, ab_ref, zw_hbm, zb_ref, wo_hbm, wup_hbm, wdn_hbm,
                 xg, w1g,
                 bias_v, bt, w_s, k_s, qt_s, vt_s, gt_s, lg, o_s, xraw, craw, xn, raw, aw_s, flat_s, wst, wst1, cond, act, y_s, h_s,
                 wall, gate, mod, nxt, o0, o1,
                 ld_sem, cd_sem, b_sem, q_sem, a_sem, st_sem, own_sem, k_sem, n_send, n_recv, n_free,
                 o_send, o_recv, w_send, w_recv, c_near, c_far, c_recv, d_near, d_far, d_recv, x_send, x_recv, r_send, r_recv, ready):
    S, T, D, C, n_tp, n_dp, hd, hu, n_chunk = dims
    p = Place(n_tp, n_dp)
    entered = p.enter()
    far = p.nz // 2
    rows_w = hd + 3 * hu
    R = S * T // n_tp
    row0 = p.me * R
    tile = R // 2
    mine = pl.ds(p.c * R, R)
    stage = [_stage(l, hd, hu, wo_hbm, wup_hbm, wdn_hbm, w, st_sem.at[l]) for l, w in enumerate((wst, wst1))]

    def toward(k):
        j = S - 1 - k
        return lax.rem(p.z + S + (1 - 2 * lax.rem(j, 2)) * ((j + 1) // 2), S)

    def outward(j):
        return lax.rem(p.z + S + (1 - 2 * p.c) * (1 - 2 * lax.rem(j, 2)) * ((j + 1) // 2), S)

    def loads(k, slot):
        s = toward(k)
        return [pltpu.make_async_copy(x_hbm.at[s, mine], xraw.at[slot], ld_sem.at[slot]),
                pltpu.make_async_copy(cond_hbm.at[s, mine], craw.at[slot], cd_sem.at[slot])]

    raw0 = _copy(aw_hbm.at[0, 0], raw.at[0], a_sem.at[0])
    for k in range(2):
        for cp in loads(k, k):
            cp.start()
    bias_cp = _copy(bias_hbm.at[0, 0], bias_v, b_sem)
    w_s[...] = jnp.zeros_like(w_s)
    qt_s[HP:, :] = jnp.zeros((HP, T), BF16)
    wq = _stage_qkvg(0, hd, wq_hbm, w_s, q_sem)
    for cp in stage[0]:
        cp.wait()
    for cp in wq:
        cp.wait()
    raws = [_copy(src, raw.at[i + 1], a_sem.at[i + 1]) for i, src in enumerate((zw_hbm.at[0], aw_hbm.at[0, 1], aw_hbm.at[1, 0]))]
    own = [_copy(cond_hbm.at[p.z, mine], cond, own_sem.at[0]), _copy(x_hbm.at[p.z, mine], act, own_sem.at[1])]
    entered()
    ring_o = Ring(p, lambda b, ch: wall.at[b, 0:hd, :], w_recv, w_send)
    cross = Cross(p, wall, hd, rows_w, n_chunk, c_recv, c_near, c_far)
    cross1 = Cross(p, w1g, 0, rows_w, n_chunk, d_recv, d_near, d_far)
    ring_x = Ring(p, lambda b, ch: xg.at[pl.ds(b * R + ch * tile, tile), :], x_recv, x_send)
    ring_r = Ring(p, lambda b, ch: xg.at[pl.ds(b * R + ch * tile, tile), :], r_recv, r_send)
    ring_o.own(0, wst.at[0:hd, :])
    cross.own(wst)

    def half(slot):
        v = xn.at[slot, mine]
        return pltpu.make_async_remote_copy(src_ref=v, dst_ref=v, send_sem=n_send.at[slot], recv_sem=n_recv.at[slot],
                                            device_id={"tp": p.partner}, device_id_type=MESH)

    def normalise(slot):
        for i in range(2):
            rows = pl.ds(i * tile, tile)
            cn = _ln(craw[slot, rows, :].astype(F32))
            y = _ada(xraw[slot, rows, :].astype(F32), cn, asc_ref[0, 0:1, :], aw_s[...], ab_ref[0, 0:1, :])
            xn[slot, pl.ds(pl.multiple_of(p.c * R, R) + i * tile, tile), :] = y

    raw0.wait()
    aw_s[...] = _flat(raw.at[0])
    for cp in loads(0, 0):
        cp.wait()
    normalise(0)
    bias_cp.wait()
    half(0).start()
    _load_bias(bias_v, mask_ref, bt)
    bias_cp = _copy(bias_hbm.at[1, 0], bias_v, b_sem)
    for cp in stage[1]:
        cp.wait()
    wall[p.me] = wst[...]
    keep = _copy(wst1, w1g.at[p.me], k_sem)

    def gates(l, i):
        raws[i].wait()
        flat_s[...] = _flat(raw.at[i + 1])
        _gates(gate, cond[...], flat_s[...], zb_ref.at[l])

    def modulation(out, l, j, i):
        raws[i].wait()
        flat_s[...] = _flat(raw.at[i + 1])
        cn = _ln(cond[...].astype(F32))
        _modulation(out, cn, asc_ref[l, j:j + 1, :], flat_s[...], ab_ref[l, j:j + 1, :])

    events = {}

    def plan(when, f, *args):
        events.setdefault(when, []).append((f, args))

    def take(step, k):
        for when in sorted(events):
            if when % 2 == step:
                @pl.when(k == when // 2)
                def _():
                    for f, args in events[when]:
                        f(*args)

    for h in range(1, far + 1):
        plan(n_chunk * (h - 1), ring_o.service, h, 0)
        for ch in range(n_chunk):
            plan(n_chunk * (h - 1) + ch, cross.along, h, ch)
            plan(n_chunk * h + ch + 1, cross.across, h, ch)
    for ch in range(n_chunk):
        plan(2 * S - n_chunk + ch, cross1.along, 1, ch)
    plan(2 * S - 2 * n_chunk, cross1.own, wst1)
    for cp in own:
        plan(3, cp.wait)
    plan(5, gates, 0, 0)
    plan(7, modulation, mod, 0, 1, 1)
    plan(9, modulation, nxt, 1, 0, 2)
    ex = [Exchange(p, order, o_s, o, o_send.at[l], o_recv.at[l]) for l, (order, o) in enumerate(((toward, o0), (outward, o1)))]
    brow = [_bias_row(bq_ref[l:l + 1, :], hd) for l in range(2)]
    heads = (n_tp, hd, w_s)
    work = (bt, k_s, qt_s, vt_s, gt_s, lg, o_s)

    def step0(k, _):
        slot = lax.rem(k, 2)

        @pl.when(k + 2 < S)
        def _():
            for cp in loads(k + 2, slot):
                cp.start()

        with scope("a_half"):
            v = xn.at[slot, pl.ds((1 - p.c) * R, R)]
            pltpu.make_async_copy(v, v, n_recv.at[slot]).wait()
            half(slot).wait_send()
        at = Attend(*heads, brow[0], *work, lambda i, t: xn[slot, pl.ds(i * t, t), :])
        at.project()

        @pl.when(k + 2 < S)
        def _():
            pl.semaphore_signal(n_free, inc=1, device_id={"tp": p.partner}, device_id_type=MESH)

        @pl.when(k >= 1)
        def _():
            ex[0].start(k - 1)

        @pl.when(k + 1 < S)
        def _():
            for cp in loads(k + 1, 1 - slot):
                cp.wait()
            normalise(1 - slot)

            @pl.when(k >= 1)
            def _():
                pl.semaphore_wait(n_free, 1)

        with scope("a_ev0"):
            take(0, k)

        def hook():
            @pl.when(k + 1 < S)
            def _():
                half(1 - slot).start()

        with scope("a_att"):
            at.attend(k, hook)
        with scope("a_ev1"):
            take(1, k)
        return 0

    lax.fori_loop(0, S, step0, 0)
    ex[0].start(S - 1)
    wq = _stage_qkvg(1, hd, wq_hbm, w_s, q_sem)
    raws = [_copy(src, raw.at[i + 1], a_sem.at[i + 1]) for i, src in enumerate((zw_hbm.at[1], aw_hbm.at[1, 1]))]
    for when in sorted(events):
        if when >= 2 * S:
            for f, args in events[when]:
                f(*args)

    def other(i, _):
        ring_o.wait(i * 2 + (1 - p.c), 0)
        return 0

    with scope("b_w0"):
        lax.fori_loop(0, p.nz, other, 0)
        cross.finish_near()
    with scope("b_o0"):
        ex[0].sent()
        ex[0].arrived()
    size = (D, n_tp, hd, hu)
    for ch in range(2):
        rows = pl.ds(ch * tile, tile)
        with scope("b_mlp"):
            new = _transition(size, tile, gate, mod, o0, act, wall, y_s, h_s, rows)
            act[rows, :] = new
            xg[pl.ds(row0 + ch * tile, tile), :] = (nxt[rows, :D] * _ln(new.astype(F32)) + nxt[rows, D:]).astype(BF16)
        ring_x.own(ch)
        if ch == 0:
            with scope("b_along"):
                for i in range(n_chunk):
                    cross1.along(2, i)
    bias_cp.wait()
    _load_bias(bias_v, mask_ref, bt)
    for cp in wq:
        cp.wait()
    ring_o.drain(wall.at[0:n_tp - 1, 0:hd, :])
    cross.finish_far()
    keep.wait()
    events = {}
    for ch in range(n_chunk):
        plan(1, cross1.along, far - 1, ch)
        plan(5, cross1.along, far, ch)
        for h in range(1, far + 1):
            plan(2 * h + 3, cross1.across, h, ch)
    plan(3, gates, 1, 0)
    plan(7, modulation, mod, 1, 1, 1)

    def last_weights():
        cross1.finish_near()
        pltpu.make_async_copy(w1g, wall, k_sem).start()

    plan(2 * S - 3, last_weights)

    def step1(j, _):
        with scope("b_svc"):
            ring_x.service(j // 2 + 1, lax.rem(j, 2))

        @pl.when(j >= 1)
        def _():
            ex[1].start(j - 1)

        s = outward(j)
        with scope("b_half"):
            for ch in range(2):
                ring_x.wait(s * 2 + (1 - p.c), ch)
        at = Attend(*heads, brow[1], *work, lambda i, t: xg[pl.ds(pl.multiple_of(s * T, T) + i * t, t), :])
        with scope("b_att"):
            at.project()
            at.attend(j)
        with scope("b_ev"):
            take(1, j)
        return 0

    lax.fori_loop(0, S, step1, 0)
    ex[1].start(S - 1)
    pltpu.make_async_copy(w1g, wall, k_sem).wait()
    cross1.finish_far()
    ring_x.drain(xg.at[0:(n_tp - 1) * R, :])
    for peer in (p.at(1), p.at(-1), p.partner):
        pl.semaphore_signal(ready, inc=1, device_id={"tp": peer}, device_id_type=MESH)
    with scope("c_o1"):
        ex[1].sent()
        ex[1].arrived()
    for ch in range(2):
        rows = pl.ds(ch * tile, tile)
        with scope("c_mlp"):
            xg[pl.ds(row0 + ch * tile, tile), :] = _transition(size, tile, gate, mod, o1, act, wall, y_s, h_s, rows)
        if ch == 0:
            with scope("c_ready"):
                pl.semaphore_wait(ready, 3)
        ring_r.own(ch)
    with scope("c_svc"):
        lax.fori_loop(0, p.nz, lambda e, _: (ring_r.service(e // 2 + 1, lax.rem(e, 2)), 0)[1], 0)

    def rest(i, _):
        for ch in range(2):
            ring_r.wait(i * 2 + (1 - p.c), ch)
        return 0

    with scope("c_end"):
        lax.fori_loop(0, p.nz, rest, 0)
        ring_r.drain(xg.at[0:(n_tp - 1) * R, :])


def _main(n_dp, x, cond, pair_bias, mask_row, wq, bq, asc, aw, ab, zw, zb, wo, wup, wdn):
    S, T, D = x.shape
    C = cond.shape[-1]
    hd, hu = wq.shape[2], wdn.shape[1]
    n_tp = S * 2
    rows_w = hd + 3 * hu
    R = T // 2
    n_chunk = 3
    dma = pltpu.SemaphoreType.DMA
    v = pltpu.VMEM
    pair, blocks, each = dma((2,)), dma((S,)), dma((n_tp, n_chunk))
    halves = dma((n_tp, 2))
    return pl.pallas_call(
        functools.partial(_main_kernel, (S, T, D, C, n_tp, n_dp, hd, hu, n_chunk)),
        out_shape=(v((n_tp * R, D), BF16), pltpu.HBM((n_tp, rows_w, D), BF16)),
        in_specs=[ANY, ANY, ANY, VMEM, ANY, VMEM, VMEM, ANY, VMEM, ANY, VMEM, ANY, ANY, ANY],
        out_specs=(VMEM, HBM),
        scratch_shapes=[
            v((T, T), BF16), v((T, T), F32), v((4 * HP, D), BF16), v((T, 2 * HP), BF16), v((2 * HP, T), BF16), v((HP, T), BF16),
            v((hd, T), F32), v((2, T, QT), F32), v((S, hd, T), BF16),
            v((2, R, D), BF16), v((2, R, C), BF16), v((2, T, D), BF16), v((4, C, 2, D), BF16), *[v((C, 2 * D), BF16)] * 2,
            *[v((rows_w, D), BF16)] * 2, v((R, C), BF16), v((R, D), BF16), v((R // 2, D), BF16), v((R // 2, n_tp * hu), BF16),
            v((n_tp, rows_w, D), BF16), *[v((R, 2 * D), F32)] * 3, *[v((n_tp, hd, R), BF16)] * 2,
            pair, pair, dma, dma((4,)), dma((4,)), dma((2, 4)), pair, dma, pair, pair, pltpu.SemaphoreType.REGULAR,
            dma((2, S, 2)), pair, dma, dma((n_tp, 1)), dma, blocks, each, dma, blocks, each, dma, halves, dma, halves, pltpu.SemaphoreType.REGULAR],
        cost_estimate=pl.CostEstimate(flops=S * T * T * D, bytes_accessed=S * T * D, transcendentals=S * T * T),
        compiler_params=pltpu.CompilerParams(collective_id=0, has_side_effects=True, vmem_limit_bytes=VM),
        name="blocks",
    )(x, cond, pair_bias, mask_row, wq, bq, asc, aw, ab, zw, zb, wo, wup, wdn)


def _store_kernel(src, dst, sem):
    cp = pltpu.make_async_copy(src, dst, sem)
    cp.start()
    cp.wait()


def _store(x):
    return pl.pallas_call(
        _store_kernel, out_shape=jax.ShapeDtypeStruct(x.shape, x.dtype), in_specs=[VMEM], out_specs=ANY,
        scratch_shapes=[pltpu.SemaphoreType.DMA], compiler_params=pltpu.CompilerParams(vmem_limit_bytes=1 << 20), name="store")(x)


def solution(mesh):
    n_dp = mesh.shape["dp"]

    def shard_body(token_act, token_cond, pair_bias, token_mask, ada_scale, ada_w, ada_bias, zero_w, zero_b, w_qkvg, b_q, w_o, w_up, w_down):
        S, T, D = token_act.shape
        mask_row = token_mask.reshape(1, T)
        wq = jnp.transpose(w_qkvg, (0, 2, 3, 1))
        wup = jnp.transpose(w_up, (0, 2, 3, 1))
        out, _ = _main(n_dp, token_act, token_cond, pair_bias, mask_row, wq, b_q, ada_scale, ada_w, ada_bias, zero_w, zero_b, w_o, wup, w_down)
        out = pltpu.with_memory_space_constraint(out, pltpu.VMEM)
        return _store(out).reshape(S, T, D)

    everywhere = P()
    rows, second, fourth = P('dp'), P(None, 'tp'), P(*[None] * 3, 'tp')
    in_specs = (rows, rows, second) + (everywhere,) * 6 + (fourth, second, second, fourth, second)
    return jax.shard_map(shard_body, mesh=mesh, in_specs=in_specs, out_specs=rows, check_vma=False)
```

time: 239 us -> 229 us (0.958)
  Pallas kernels: 237 us -> 225 us
    pallas_call x3 -> x1, Pallas kernels: 233 us -> 220 us  [_main(): pl.pallas_call(functools.partial(_main_kernel, (S, T, D, C, n_tp, n_dp, h...]
where the time goes in v7:
time: 229 us; the launch traced here: 225 us
  Pallas kernels  225 us (98%)
    pallas_call x1, Pallas kernels, _main(): pl.pallas_call(functools.partial(_main_kernel, (S, T, D, C, n_tp, n_dp, h...  220 us
    pallas_call x1, Pallas kernels, _store(): pl.pallas_call(_store_kernel, out_shape=jax.ShapeDtypeStruct(x.shape, x.d...  4.79 us

profile of v7, /device:TPU:21, one launch (start us, length us, event | category | flops | bytes accessed | tf_op | source)
XLA Modules:
  0.0 225.3 jit_solution(2840391571148207107)
XLA Ops:
  0.0 220.3 %blocks.1 = (bf16[8192,768]{1,0:T(8,128)(2,1)S(1)}, bf16[16,336,768]{2,1,0:T(8,128)(2,1)}) custom-call(bf16[8,1024,768]{2,1,0:T(8,128)(2,1)} %x_hbm.1, bf16[8,1024,384]{2,1,0:T(8,128)(2,1)} %cond_hbm.1, bf16[2,1,1024,1024]{3,2,1,0:T(8,128)(2,1)} %bias_hbm.1, s32[1,1024]{1,0:T(1,128)} %bitcast.6, bf16[2,4,48,768]{3,2,1,0:T(8,128)(2,1)} %bitcast.4, ...), custom_call_target="tpu_custom_call" | custom-call | flops 6442450944 | bytes 6291456 | tf_op jit(solution)/shard_map/blocks/pallas_call | solution.py:691
  220.3 4.8 %store.1 = bf16[8192,768]{1,0:T(8,128)(2,1)} custom-call(bf16[8192,768]{1,0:T(8,128)(2,1)S(1)} %get-tuple-element.6.src), custom_call_target="tpu_custom_call" | custom-call | tf_op jit(solution)/shard_map/store/pallas_call | solution.py:717

commit v8 on v7

--- a/solution.py
+++ b/solution.py
@@ -411,14 +411,15 @@
                  wall, gate, mod, nxt, o0, o1,
                  ld_sem, cd_sem, b_sem, q_sem, a_sem, st_sem, own_sem, k_sem, n_send, n_recv, n_free,
                  o_send, o_recv, w_send, w_recv, c_near, c_far, c_recv, d_near, d_far, d_recv, x_send, x_recv, r_send, r_recv, ready):
-    S, T, D, C, n_tp, n_dp, hd, hu, n_chunk = dims
+    S, T, D, C, n_tp, n_dp, hd, hu, n_chunk, n_tile = dims
     p = Place(n_tp, n_dp)
     entered = p.enter()
     far = p.nz // 2
     rows_w = hd + 3 * hu
+    cut = 2 * hd
     R = S * T // n_tp
     row0 = p.me * R
-    tile = R // 2
+    tile = R // n_tile
     mine = pl.ds(p.c * R, R)
     stage = [_stage(l, hd, hu, wo_hbm, wup_hbm, wdn_hbm, w, st_sem.at[l]) for l, w in enumerate((wst, wst1))]
 
@@ -449,12 +450,12 @@
     raws = [_copy(src, raw.at[i + 1], a_sem.at[i + 1]) for i, src in enumerate((zw_hbm.at[0], aw_hbm.at[0, 1], aw_hbm.at[1, 0]))]
     own = [_copy(cond_hbm.at[p.z, mine], cond, own_sem.at[0]), _copy(x_hbm.at[p.z, mine], act, own_sem.at[1])]
     entered()
-    ring_o = Ring(p, lambda b, ch: wall.at[b, 0:hd, :], w_recv, w_send)
-    cross = Cross(p, wall, hd, rows_w, n_chunk, c_recv, c_near, c_far)
+    ring_o = Ring(p, lambda b, ch: wall.at[b, 0:cut, :], w_recv, w_send)
+    cross = Cross(p, wall, cut, rows_w, n_chunk, c_recv, c_near, c_far)
     cross1 = Cross(p, w1g, 0, rows_w, n_chunk, d_recv, d_near, d_far)
     ring_x = Ring(p, lambda b, ch: xg.at[pl.ds(b * R + ch * tile, tile), :], x_recv, x_send)
     ring_r = Ring(p, lambda b, ch: xg.at[pl.ds(b * R + ch * tile, tile), :], r_recv, r_send)
-    ring_o.own(0, wst.at[0:hd, :])
+    ring_o.own(0, wst.at[0:cut, :])
     cross.own(wst)
 
     def half(slot):
@@ -463,11 +464,12 @@
                                             device_id={"tp": p.partner}, device_id_type=MESH)
 
     def normalise(slot):
+        big = R // 2
         for i in range(2):
-            rows = pl.ds(i * tile, tile)
+            rows = pl.ds(i * big, big)
             cn = _ln(craw[slot, rows, :].astype(F32))
             y = _ada(xraw[slot, rows, :].astype(F32), cn, asc_ref[0, 0:1, :], aw_s[...], ab_ref[0, 0:1, :])
-            xn[slot, pl.ds(pl.multiple_of(p.c * R, R) + i * tile, tile), :] = y
+            xn[slot, pl.ds(pl.multiple_of(p.c * R, R) + i * big, big), :] = y
 
     raw0.wait()
     aw_s[...] = _flat(raw.at[0])
@@ -507,14 +509,15 @@
                     for f, args in events[when]:
                         f(*args)
 
+    first, over = (0, 4, 7, 10), (4, 8, 11, 14)
     for h in range(1, far + 1):
-        plan(n_chunk * (h - 1), ring_o.service, h, 0)
+        plan(first[h - 1] + 1, ring_o.service, h, 0)
         for ch in range(n_chunk):
-            plan(n_chunk * (h - 1) + ch, cross.along, h, ch)
-            plan(n_chunk * h + ch + 1, cross.across, h, ch)
+            plan(first[h - 1] + ch, cross.along, h, ch)
+            plan(over[h - 1] + ch, cross.across, h, ch)
     for ch in range(n_chunk):
-        plan(2 * S - n_chunk + ch, cross1.along, 1, ch)
-    plan(2 * S - 2 * n_chunk, cross1.own, wst1)
+        plan(2 * S + 1, cross1.along, 1, ch)
+    plan(11, cross1.own, wst1)
     for cp in own:
         plan(3, cp.wait)
     plan(5, gates, 0, 0)
@@ -592,32 +595,38 @@
         ex[0].sent()
         ex[0].arrived()
     size = (D, n_tp, hd, hu)
-    for ch in range(2):
-        rows = pl.ds(ch * tile, tile)
+
+    def tile0(ch, _):
+        rows = pl.ds(pl.multiple_of(ch * tile, tile), tile)
         with scope("b_mlp"):
             new = _transition(size, tile, gate, mod, o0, act, wall, y_s, h_s, rows)
             act[rows, :] = new
-            xg[pl.ds(row0 + ch * tile, tile), :] = (nxt[rows, :D] * _ln(new.astype(F32)) + nxt[rows, D:]).astype(BF16)
+            xg[pl.ds(pl.multiple_of(row0 + ch * tile, tile), tile), :] = (nxt[rows, :D] * _ln(new.astype(F32)) + nxt[rows, D:]).astype(BF16)
         ring_x.own(ch)
-        if ch == 0:
+
+        @pl.when(ch == 1)
+        def _():
             with scope("b_along"):
                 for i in range(n_chunk):
                     cross1.along(2, i)
+        return 0
+
+    lax.fori_loop(0, n_tile, tile0, 0)
     bias_cp.wait()
     _load_bias(bias_v, mask_ref, bt)
     for cp in wq:
         cp.wait()
-    ring_o.drain(wall.at[0:n_tp - 1, 0:hd, :])
+    ring_o.drain(wall.at[0:n_tp - 1, 0:cut, :])
     cross.finish_far()
     keep.wait()
     events = {}
     for ch in range(n_chunk):
-        plan(1, cross1.along, far - 1, ch)
-        plan(5, cross1.along, far, ch)
+        plan(3, cross1.along, far - 1, ch)
+        plan(9, cross1.along, far, ch)
         for h in range(1, far + 1):
-            plan(2 * h + 3, cross1.across, h, ch)
-    plan(3, gates, 1, 0)
-    plan(7, modulation, mod, 1, 1, 1)
+            plan(2 * h + 5, cross1.across, h, ch)
+    plan(1, gates, 1, 0)
+    plan(5, modulation, mod, 1, 1, 1)
 
     def last_weights():
         cross1.finish_near()
@@ -627,7 +636,8 @@
 
     def step1(j, _):
         with scope("b_svc"):
-            ring_x.service(j // 2 + 1, lax.rem(j, 2))
+            for i in range(n_tile // 2):
+                ring_x.service(j // 2 + 1, lax.rem(j, 2) * (n_tile // 2) + i)
 
         @pl.when(j >= 1)
         def _():
@@ -635,7 +645,7 @@
 
         s = outward(j)
         with scope("b_half"):
-            for ch in range(2):
+            for ch in range(n_tile):
                 ring_x.wait(s * 2 + (1 - p.c), ch)
         at = Attend(*heads, brow[1], *work, lambda i, t: xg[pl.ds(pl.multiple_of(s * T, T) + i * t, t), :])
         with scope("b_att"):
@@ -655,19 +665,25 @@
     with scope("c_o1"):
         ex[1].sent()
         ex[1].arrived()
-    for ch in range(2):
-        rows = pl.ds(ch * tile, tile)
+    def tile1(ch, _):
+        rows = pl.ds(pl.multiple_of(ch * tile, tile), tile)
         with scope("c_mlp"):
-            xg[pl.ds(row0 + ch * tile, tile), :] = _transition(size, tile, gate, mod, o1, act, wall, y_s, h_s, rows)
-        if ch == 0:
+            xg[pl.ds(pl.multiple_of(row0 + ch * tile, tile), tile), :] = _transition(size, tile, gate, mod, o1, act, wall, y_s, h_s, rows)
+
+        @pl.when(ch == 0)
+        def _():
             with scope("c_ready"):
                 pl.semaphore_wait(ready, 3)
+
         ring_r.own(ch)
+        return 0
+
+    lax.fori_loop(0, n_tile, tile1, 0)
     with scope("c_svc"):
-        lax.fori_loop(0, p.nz, lambda e, _: (ring_r.service(e // 2 + 1, lax.rem(e, 2)), 0)[1], 0)
+        lax.fori_loop(0, far * n_tile, lambda e, _: (ring_r.service(e // n_tile + 1, lax.rem(e, n_tile)), 0)[1], 0)
 
     def rest(i, _):
-        for ch in range(2):
+        for ch in range(n_tile):
             ring_r.wait(i * 2 + (1 - p.c), ch)
         return 0
 
@@ -687,9 +703,10 @@
     dma = pltpu.SemaphoreType.DMA
     v = pltpu.VMEM
     pair, blocks, each = dma((2,)), dma((S,)), dma((n_tp, n_chunk))
-    halves = dma((n_tp, 2))
+    n_tile = 4
+    tiles = dma((n_tp, n_tile))
     return pl.pallas_call(
-        functools.partial(_main_kernel, (S, T, D, C, n_tp, n_dp, hd, hu, n_chunk)),
+        functools.partial(_main_kernel, (S, T, D, C, n_tp, n_dp, hd, hu, n_chunk, n_tile)),
         out_shape=(v((n_tp * R, D), BF16), pltpu.HBM((n_tp, rows_w, D), BF16)),
         in_specs=[ANY, ANY, ANY, VMEM, ANY, VMEM, VMEM, ANY, VMEM, ANY, VMEM, ANY, ANY, ANY],
         out_specs=(VMEM, HBM),
@@ -697,10 +714,10 @@
             v((T, T), BF16), v((T, T), F32), v((4 * HP, D), BF16), v((T, 2 * HP), BF16), v((2 * HP, T), BF16), v((HP, T), BF16),
             v((hd, T), F32), v((2, T, QT), F32), v((S, hd, T), BF16),
             v((2, R, D), BF16), v((2, R, C), BF16), v((2, T, D), BF16), v((4, C, 2, D), BF16), *[v((C, 2 * D), BF16)] * 2,
-            *[v((rows_w, D), BF16)] * 2, v((R, C), BF16), v((R, D), BF16), v((R // 2, D), BF16), v((R // 2, n_tp * hu), BF16),
+            *[v((rows_w, D), BF16)] * 2, v((R, C), BF16), v((R, D), BF16), v((R // n_tile, D), BF16), v((R // n_tile, n_tp * hu), BF16),
             v((n_tp, rows_w, D), BF16), *[v((R, 2 * D), F32)] * 3, *[v((n_tp, hd, R), BF16)] * 2,
             pair, pair, dma, dma((4,)), dma((4,)), dma((2, 4)), pair, dma, pair, pair, pltpu.SemaphoreType.REGULAR,
-            dma((2, S, 2)), pair, dma, dma((n_tp, 1)), dma, blocks, each, dma, blocks, each, dma, halves, dma, halves, pltpu.SemaphoreType.REGULAR],
+            dma((2, S, 2)), pair, dma, dma((n_tp, 1)), dma, blocks, each, dma, blocks, each, dma, tiles, dma, tiles, pltpu.SemaphoreType.REGULAR],
         cost_estimate=pl.CostEstimate(flops=S * T * T * D, bytes_accessed=S * T * D, transcendentals=S * T * T),
         compiler_params=pltpu.CompilerParams(collective_id=0, has_side_effects=True, vmem_limit_bytes=VM),
         name="blocks",

time: 229 us -> 226 us (0.987)
  no operation moved by 1% of the time
where the time goes in v8:
time: 226 us; the launch traced here: 224 us
  Pallas kernels  224 us (99%)
    pallas_call x1, Pallas kernels, _main(): pl.pallas_call(functools.partial(_main_kernel, (S, T, D, C, n_tp, n_dp, h...  219 us
    pallas_call x1, Pallas kernels, _store(): pl.pallas_call(_store_kernel, out_shape=jax.ShapeDtypeStruct(x.shape, x.d...  4.79 us

profile of v8, /device:TPU:21, one launch (start us, length us, event | category | flops | bytes accessed | tf_op | source)
XLA Modules:
  0.0 224.3 jit_solution(1922184191816435898)
XLA Ops:
  0.0 219.3 %blocks.1 = (bf16[8192,768]{1,0:T(8,128)(2,1)S(1)}, bf16[16,336,768]{2,1,0:T(8,128)(2,1)}) custom-call(bf16[8,1024,768]{2,1,0:T(8,128)(2,1)} %x_hbm.1, bf16[8,1024,384]{2,1,0:T(8,128)(2,1)} %cond_hbm.1, bf16[2,1,1024,1024]{3,2,1,0:T(8,128)(2,1)} %bias_hbm.1, s32[1,1024]{1,0:T(1,128)} %bitcast.6, bf16[2,4,48,768]{3,2,1,0:T(8,128)(2,1)} %bitcast.4, ...), custom_call_target="tpu_custom_call" | custom-call | flops 6442450944 | bytes 6291456 | tf_op jit(solution)/shard_map/blocks/pallas_call | solution.py:708
  219.3 4.8 %store.1 = bf16[8192,768]{1,0:T(8,128)(2,1)} custom-call(bf16[8192,768]{1,0:T(8,128)(2,1)S(1)} %get-tuple-element.6.src), custom_call_target="tpu_custom_call" | custom-call | tf_op jit(solution)/shard_map/store/pallas_call | solution.py:734

commit v9 on v8

--- a/solution.py
+++ b/solution.py
@@ -424,7 +424,8 @@
     stage = [_stage(l, hd, hu, wo_hbm, wup_hbm, wdn_hbm, w, st_sem.at[l]) for l, w in enumerate((wst, wst1))]
 
     def toward(k):
-        j = S - 1 - k
+        late, own = k // far, k // (S - 1)
+        j = (1 - late) * (k + 1) + (late - own) * (S + far - 1 - k)
         return lax.rem(p.z + S + (1 - 2 * lax.rem(j, 2)) * ((j + 1) // 2), S)
 
     def outward(j):
@@ -509,15 +510,16 @@
                     for f, args in events[when]:
                         f(*args)
 
-    first, over = (0, 4, 7, 10), (4, 8, 11, 14)
+    first, over, first1 = (0, 4, 7, 10), (4, 8, 11, 14), (8, 11, 14)
     for h in range(1, far + 1):
         plan(first[h - 1] + 1, ring_o.service, h, 0)
         for ch in range(n_chunk):
             plan(first[h - 1] + ch, cross.along, h, ch)
             plan(over[h - 1] + ch, cross.across, h, ch)
-    for ch in range(n_chunk):
-        plan(2 * S + 1, cross1.along, 1, ch)
-    plan(11, cross1.own, wst1)
+    for h in range(1, far):
+        for ch in range(n_chunk):
+            plan(first1[h - 1] + (ch + 1) // 2, cross1.along, h, ch)
+    plan(n_chunk + 1, cross1.own, wst1)
     for cp in own:
         plan(3, cp.wait)
     plan(5, gates, 0, 0)
@@ -608,7 +610,7 @@
         def _():
             with scope("b_along"):
                 for i in range(n_chunk):
-                    cross1.along(2, i)
+                    cross1.along(far, i)
         return 0
 
     lax.fori_loop(0, n_tile, tile0, 0)
@@ -621,8 +623,6 @@
     keep.wait()
     events = {}
     for ch in range(n_chunk):
-        plan(3, cross1.along, far - 1, ch)
-        plan(9, cross1.along, far, ch)
         for h in range(1, far + 1):
             plan(2 * h + 5, cross1.across, h, ch)
     plan(1, gates, 1, 0)

time: 226 us -> 230 us (1.018)
  Pallas kernels: 224 us -> 228 us
    pallas_call x1, Pallas kernels: 219 us -> 223 us  [_main(): pl.pallas_call(functools.partial(_main_kernel, (S, T, D, C, n_tp, n_dp, h...]
where the time goes in v9:
time: 230 us; the launch traced here: 228 us
  Pallas kernels  228 us (99%)
    pallas_call x1, Pallas kernels, _main(): pl.pallas_call(functools.partial(_main_kernel, (S, T, D, C, n_tp, n_dp, h...  223 us
    pallas_call x1, Pallas kernels, _store(): pl.pallas_call(_store_kernel, out_shape=jax.ShapeDtypeStruct(x.shape, x.d...  4.79 us

profile of v9, /device:TPU:21, one launch (start us, length us, event | category | flops | bytes accessed | tf_op | source)
XLA Modules:
  0.0 228.2 jit_solution(9275099276916984058)
XLA Ops:
  0.0 223.3 %blocks.1 = (bf16[8192,768]{1,0:T(8,128)(2,1)S(1)}, bf16[16,336,768]{2,1,0:T(8,128)(2,1)}) custom-call(bf16[8,1024,768]{2,1,0:T(8,128)(2,1)} %x_hbm.1, bf16[8,1024,384]{2,1,0:T(8,128)(2,1)} %cond_hbm.1, bf16[2,1,1024,1024]{3,2,1,0:T(8,128)(2,1)} %bias_hbm.1, s32[1,1024]{1,0:T(1,128)} %bitcast.6, bf16[2,4,48,768]{3,2,1,0:T(8,128)(2,1)} %bitcast.4, ...), custom_call_target="tpu_custom_call" | custom-call | flops 6442450944 | bytes 6291456 | tf_op jit(solution)/shard_map/blocks/pallas_call | solution.py:708
  223.3 4.8 %store.1 = bf16[8192,768]{1,0:T(8,128)(2,1)} custom-call(bf16[8192,768]{1,0:T(8,128)(2,1)S(1)} %get-tuple-element.6.src), custom_call_target="tpu_custom_call" | custom-call | tf_op jit(solution)/shard_map/store/pallas_call | solution.py:734

commit v10 on v9

--- a/solution.py
+++ b/solution.py
@@ -424,8 +424,8 @@
     stage = [_stage(l, hd, hu, wo_hbm, wup_hbm, wdn_hbm, w, st_sem.at[l]) for l, w in enumerate((wst, wst1))]
 
     def toward(k):
-        late, own = k // far, k // (S - 1)
-        j = (1 - late) * (k + 1) + (late - own) * (S + far - 1 - k)
+        late, own = (k + S - 2) // S, k // (S - 1)
+        j = (1 - late) * (k + 1) + (late - own) * (S + 1 - k)
         return lax.rem(p.z + S + (1 - 2 * lax.rem(j, 2)) * ((j + 1) // 2), S)
 
     def outward(j):
@@ -441,12 +441,7 @@
         for cp in loads(k, k):
             cp.start()
     bias_cp = _copy(bias_hbm.at[0, 0], bias_v, b_sem)
-    w_s[...] = jnp.zeros_like(w_s)
-    qt_s[HP:, :] = jnp.zeros((HP, T), BF16)
-    wq = _stage_qkvg(0, hd, wq_hbm, w_s, q_sem)
     for cp in stage[0]:
-        cp.wait()
-    for cp in wq:
         cp.wait()
     raws = [_copy(src, raw.at[i + 1], a_sem.at[i + 1]) for i, src in enumerate((zw_hbm.at[0], aw_hbm.at[0, 1], aw_hbm.at[1, 0]))]
     own = [_copy(cond_hbm.at[p.z, mine], cond, own_sem.at[0]), _copy(x_hbm.at[p.z, mine], act, own_sem.at[1])]
@@ -458,6 +453,9 @@
     ring_r = Ring(p, lambda b, ch: xg.at[pl.ds(b * R + ch * tile, tile), :], r_recv, r_send)
     ring_o.own(0, wst.at[0:cut, :])
     cross.own(wst)
+    w_s[...] = jnp.zeros_like(w_s)
+    qt_s[HP:, :] = jnp.zeros((HP, T), BF16)
+    wq = _stage_qkvg(0, hd, wq_hbm, w_s, q_sem)
 
     def half(slot):
         v = xn.at[slot, mine]
@@ -481,7 +479,7 @@
     half(0).start()
     _load_bias(bias_v, mask_ref, bt)
     bias_cp = _copy(bias_hbm.at[1, 0], bias_v, b_sem)
-    for cp in stage[1]:
+    for cp in stage[1] + wq:
         cp.wait()
     wall[p.me] = wst[...]
     keep = _copy(wst1, w1g.at[p.me], k_sem)
@@ -510,15 +508,15 @@
                     for f, args in events[when]:
                         f(*args)
 
-    first, over, first1 = (0, 4, 7, 10), (4, 8, 11, 14), (8, 11, 14)
+    first, over, first1 = (0, 4, 7, 10), (4, 8, 11, 14), (10, 13)
     for h in range(1, far + 1):
         plan(first[h - 1] + 1, ring_o.service, h, 0)
         for ch in range(n_chunk):
             plan(first[h - 1] + ch, cross.along, h, ch)
             plan(over[h - 1] + ch, cross.across, h, ch)
-    for h in range(1, far):
+    for h, when in enumerate(first1):
         for ch in range(n_chunk):
-            plan(first1[h - 1] + (ch + 1) // 2, cross1.along, h, ch)
+            plan(when + (ch + 1) // 2, cross1.along, h + 1, ch)
     plan(n_chunk + 1, cross1.own, wst1)
     for cp in own:
         plan(3, cp.wait)
@@ -610,7 +608,7 @@
         def _():
             with scope("b_along"):
                 for i in range(n_chunk):
-                    cross1.along(far, i)
+                    cross1.along(far - 1, i)
         return 0
 
     lax.fori_loop(0, n_tile, tile0, 0)
@@ -623,6 +621,7 @@
     keep.wait()
     events = {}
     for ch in range(n_chunk):
+        plan(5, cross1.along, far, ch)
         for h in range(1, far + 1):
             plan(2 * h + 5, cross1.across, h, ch)
     plan(1, gates, 1, 0)

time: 230 us -> 232 us (level); the launches traced: 228 us -> 228 us
  no operation moved by 1% of the time
where the time goes in v10:
time: 232 us; the launch traced here: 228 us
  Pallas kernels  227 us (98%)
    pallas_call x1, Pallas kernels, _main(): pl.pallas_call(functools.partial(_main_kernel, (S, T, D, C, n_tp, n_dp, h...  223 us
    pallas_call x1, Pallas kernels, _store(): pl.pallas_call(_store_kernel, out_shape=jax.ShapeDtypeStruct(x.shape, x.d...  4.79 us

profile of v10, /device:TPU:21, one launch (start us, length us, event | category | flops | bytes accessed | tf_op | source)
XLA Modules:
  0.0 227.5 jit_solution(12063853583734079957)
XLA Ops:
  0.0 222.6 %blocks.1 = (bf16[8192,768]{1,0:T(8,128)(2,1)S(1)}, bf16[16,336,768]{2,1,0:T(8,128)(2,1)}) custom-call(bf16[8,1024,768]{2,1,0:T(8,128)(2,1)} %x_hbm.1, bf16[8,1024,384]{2,1,0:T(8,128)(2,1)} %cond_hbm.1, bf16[2,1,1024,1024]{3,2,1,0:T(8,128)(2,1)} %bias_hbm.1, s32[1,1024]{1,0:T(1,128)} %bitcast.6, bf16[2,4,48,768]{3,2,1,0:T(8,128)(2,1)} %bitcast.4, ...), custom_call_target="tpu_custom_call" | custom-call | flops 6442450944 | bytes 6291456 | tf_op jit(solution)/shard_map/blocks/pallas_call | solution.py:707
  222.6 4.8 %store.1 = bf16[8192,768]{1,0:T(8,128)(2,1)} custom-call(bf16[8192,768]{1,0:T(8,128)(2,1)S(1)} %get-tuple-element.6.src), custom_call_target="tpu_custom_call" | custom-call | tf_op jit(solution)/shard_map/store/pallas_call | solution.py:733

commit v11 on v10

--- a/solution.py
+++ b/solution.py
@@ -112,8 +112,8 @@
 
 
 class Cross:
-    def __init__(self, place, buf, lo, hi, n_chunk, recv_sem, near_sem, far_sem, spread=True):
-        self.p, self.buf, self.lo, self.hi, self.n_chunk, self.spread = place, buf, lo, hi, n_chunk, spread
+    def __init__(self, place, buf, lo, hi, n_chunk, recv_sem, near_sem, far_sem, shift):
+        self.p, self.buf, self.lo, self.hi, self.n_chunk, self.shift = place, buf, lo, hi, n_chunk, shift
         self.recv, self.near, self.far_sem = recv_sem, near_sem, far_sem
         self.far = place.nz // 2
         self.size = (hi - lo) // n_chunk
@@ -127,18 +127,14 @@
             src_ref=v if src is None else src, dst_ref=v, send_sem=sem, recv_sem=self.recv.at[b, ch],
             device_id=dst, device_id_type=MESH).start()
 
-    def _push_over(self, b, ch, plane):
-        p = self.p
-
-        @pl.when(plane)
-        def _():
-            for i in range(1, p.n_dp):
-                self._push(b, ch, {"dp": p.column(i), "tp": p.me}, self.far_sem.at[b // 2])
-
+    def _push_over(self, b, ch):
+        p = self.p
+        for i in range(1, p.n_dp):
+            self._push(b, ch, {"dp": p.column(i), "tp": p.me}, self.far_sem.at[b // 2])
         self._push(b, ch, {"tp": p.partner}, self.near)
 
     def _mine(self, b):
-        return lax.rem(b, self.p.n_dp) == self.p.col
+        return lax.rem(b + self.shift, self.p.n_dp) == self.p.col
 
     def own(self, src):
         p = self.p
@@ -150,8 +146,7 @@
                 for off in (1, -1):
                     self._push(p.me, ch, {"tp": p.at(off)}, self.far_sem.at[p.z], part)
 
-            if self.spread:
-                self._push(p.me, ch, {"tp": p.partner}, self.near, part)
+            self._push(p.me, ch, {"tp": p.partner}, self.near, part)
 
     def wait(self, b, ch):
         v = self.buf.at[b, self._rows(ch), :]
@@ -178,24 +173,9 @@
                 def _():
                     self._push(b, ch, {"tp": p.at(sign)}, self.far_sem.at[b // 2])
 
-                if self.spread:
-                    self._push_over(b, ch, True)
+                self._push_over(b, ch)
 
         self._each(h, body)
-
-    def hand_on(self):
-        p = self.p
-
-        def block(i, _):
-            b = i * 2 + p.c
-
-            @pl.when(self._mine(b) | (i == p.z))
-            def _():
-                for ch in range(self.n_chunk):
-                    self._push_over(b, ch, i != p.z)
-            return 0
-
-        lax.fori_loop(0, p.nz, block, 0)
 
     def across(self, h, ch):
         p = self.p
@@ -224,29 +204,24 @@
         lax.fori_loop(0, p.nz, other, 0)
         self._sent(p.nz, self.near)
 
-    def finish_far(self, ring=True):
-        p = self.p
-        over = p.n_dp - 1 if self.spread else 0
-        if ring:
-            @pl.when(self._mine(p.me))
-            def _():
-                self._sent(2, self.far_sem.at[p.z])
+    def finish_far(self):
+        p = self.p
+        over = p.n_dp - 1
+
+        @pl.when(self._mine(p.me))
+        def _():
+            self._sent(2, self.far_sem.at[p.z])
 
         def body(b, sign, onward):
-            sem = self.far_sem.at[b // 2]
-
             @pl.when(self._mine(b))
             def _():
-                if not ring:
-                    self._sent(over, sem)
-                else:
-                    @pl.when(onward)
-                    def _():
-                        self._sent(over + 1, sem)
-
-                    @pl.when(jnp.logical_not(onward))
-                    def _():
-                        self._sent(over, sem)
+                @pl.when(onward)
+                def _():
+                    self._sent(over + 1, self.far_sem.at[b // 2])
+
+                @pl.when(jnp.logical_not(onward))
+                def _():
+                    self._sent(over, self.far_sem.at[b // 2])
 
         def hop(h, _):
             self._each(h, body)
@@ -424,8 +399,7 @@
     stage = [_stage(l, hd, hu, wo_hbm, wup_hbm, wdn_hbm, w, st_sem.at[l]) for l, w in enumerate((wst, wst1))]
 
     def toward(k):
-        late, own = (k + S - 2) // S, k // (S - 1)
-        j = (1 - late) * (k + 1) + (late - own) * (S + 1 - k)
+        j = S - 1 - k
         return lax.rem(p.z + S + (1 - 2 * lax.rem(j, 2)) * ((j + 1) // 2), S)
 
     def outward(j):
@@ -447,8 +421,8 @@
     own = [_copy(cond_hbm.at[p.z, mine], cond, own_sem.at[0]), _copy(x_hbm.at[p.z, mine], act, own_sem.at[1])]
     entered()
     ring_o = Ring(p, lambda b, ch: wall.at[b, 0:cut, :], w_recv, w_send)
-    cross = Cross(p, wall, cut, rows_w, n_chunk, c_recv, c_near, c_far)
-    cross1 = Cross(p, w1g, 0, rows_w, n_chunk, d_recv, d_near, d_far)
+    cross = Cross(p, wall, cut, rows_w, n_chunk, c_recv, c_near, c_far, 0)
+    cross1 = Cross(p, w1g, 0, rows_w, n_chunk, d_recv, d_near, d_far, 1)
     ring_x = Ring(p, lambda b, ch: xg.at[pl.ds(b * R + ch * tile, tile), :], x_recv, x_send)
     ring_r = Ring(p, lambda b, ch: xg.at[pl.ds(b * R + ch * tile, tile), :], r_recv, r_send)
     ring_o.own(0, wst.at[0:cut, :])
@@ -517,7 +491,7 @@
     for h, when in enumerate(first1):
         for ch in range(n_chunk):
             plan(when + (ch + 1) // 2, cross1.along, h + 1, ch)
-    plan(n_chunk + 1, cross1.own, wst1)
+    plan(6, cross1.own, wst1)
     for cp in own:
         plan(3, cp.wait)
     plan(5, gates, 0, 0)

time: 232 us -> 231 us (level); the launches traced: 228 us -> 230 us
  Pallas kernels: 227 us -> 230 us
    pallas_call x1, Pallas kernels: 223 us -> 226 us  [_main(): pl.pallas_call(functools.partial(_main_kernel, (S, T, D, C, n_tp, n_dp, h...]
where the time goes in v11:
time: 231 us; the launch traced here: 230 us
  Pallas kernels  230 us (100%)
    pallas_call x1, Pallas kernels, _main(): pl.pallas_call(functools.partial(_main_kernel, (S, T, D, C, n_tp, n_dp, h...  226 us
    pallas_call x1, Pallas kernels, _store(): pl.pallas_call(_store_kernel, out_shape=jax.ShapeDtypeStruct(x.shape, x.d...  4.79 us

profile of v11, /device:TPU:21, one launch (start us, length us, event | category | flops | bytes accessed | tf_op | source)
XLA Modules:
  0.0 230.5 jit_solution(12240482829857029387)
XLA Ops:
  0.0 225.5 %blocks.1 = (bf16[8192,768]{1,0:T(8,128)(2,1)S(1)}, bf16[16,336,768]{2,1,0:T(8,128)(2,1)}) custom-call(bf16[8,1024,768]{2,1,0:T(8,128)(2,1)} %x_hbm.1, bf16[8,1024,384]{2,1,0:T(8,128)(2,1)} %cond_hbm.1, bf16[2,1,1024,1024]{3,2,1,0:T(8,128)(2,1)} %bias_hbm.1, s32[1,1024]{1,0:T(1,128)} %bitcast.6, bf16[2,4,48,768]{3,2,1,0:T(8,128)(2,1)} %bitcast.4, ...), custom_call_target="tpu_custom_call" | custom-call | flops 6442450944 | bytes 6291456 | tf_op jit(solution)/shard_map/blocks/pallas_call | solution.py:681
  225.5 4.8 %store.1 = bf16[8192,768]{1,0:T(8,128)(2,1)} custom-call(bf16[8192,768]{1,0:T(8,128)(2,1)S(1)} %get-tuple-element.6.src), custom_call_target="tpu_custom_call" | custom-call | tf_op jit(solution)/shard_map/store/pallas_call | solution.py:707

commit v12 on v11

--- a/solution.py
+++ b/solution.py
@@ -422,7 +422,7 @@
     entered()
     ring_o = Ring(p, lambda b, ch: wall.at[b, 0:cut, :], w_recv, w_send)
     cross = Cross(p, wall, cut, rows_w, n_chunk, c_recv, c_near, c_far, 0)
-    cross1 = Cross(p, w1g, 0, rows_w, n_chunk, d_recv, d_near, d_far, 1)
+    cross1 = Cross(p, w1g, 0, rows_w, n_chunk, d_recv, d_near, d_far, 0)
     ring_x = Ring(p, lambda b, ch: xg.at[pl.ds(b * R + ch * tile, tile), :], x_recv, x_send)
     ring_r = Ring(p, lambda b, ch: xg.at[pl.ds(b * R + ch * tile, tile), :], r_recv, r_send)
     ring_o.own(0, wst.at[0:cut, :])
@@ -482,16 +482,15 @@
                     for f, args in events[when]:
                         f(*args)
 
-    first, over, first1 = (0, 4, 7, 10), (4, 8, 11, 14), (10, 13)
+    first, over = (0, 7, 9, 12), (5, 10, 13, 16)
     for h in range(1, far + 1):
         plan(first[h - 1] + 1, ring_o.service, h, 0)
         for ch in range(n_chunk):
             plan(first[h - 1] + ch, cross.along, h, ch)
             plan(over[h - 1] + ch, cross.across, h, ch)
-    for h, when in enumerate(first1):
-        for ch in range(n_chunk):
-            plan(when + (ch + 1) // 2, cross1.along, h + 1, ch)
-    plan(6, cross1.own, wst1)
+    for ch in range(n_chunk):
+        plan(2 * S + n_chunk, cross1.along, 1, ch)
+    plan(13, cross1.own, wst1)
     for cp in own:
         plan(3, cp.wait)
     plan(5, gates, 0, 0)
@@ -578,11 +577,11 @@
             xg[pl.ds(pl.multiple_of(row0 + ch * tile, tile), tile), :] = (nxt[rows, :D] * _ln(new.astype(F32)) + nxt[rows, D:]).astype(BF16)
         ring_x.own(ch)
 
-        @pl.when(ch == 1)
+        @pl.when(ch == n_tile - 1)
         def _():
             with scope("b_along"):
                 for i in range(n_chunk):
-                    cross1.along(far - 1, i)
+                    cross1.along(2, i)
         return 0
 
     lax.fori_loop(0, n_tile, tile0, 0)
@@ -595,7 +594,8 @@
     keep.wait()
     events = {}
     for ch in range(n_chunk):
-        plan(5, cross1.along, far, ch)
+        plan(3, cross1.along, far - 1, ch)
+        plan(9, cross1.along, far, ch)
         for h in range(1, far + 1):
             plan(2 * h + 5, cross1.across, h, ch)
     plan(1, gates, 1, 0)

time: 231 us -> 226 us (0.978)
  Pallas kernels: 230 us -> 226 us
    pallas_call x1, Pallas kernels: 226 us -> 221 us  [_main(): pl.pallas_call(functools.partial(_main_kernel, (S, T, D, C, n_tp, n_dp, h...]
where the time goes in v12:
time: 226 us
  Pallas kernels  226 us (100%)
    pallas_call x1, Pallas kernels, _main(): pl.pallas_call(functools.partial(_main_kernel, (S, T, D, C, n_tp, n_dp, h...  221 us
    pallas_call x1, Pallas kernels, _store(): pl.pallas_call(_store_kernel, out_shape=jax.ShapeDtypeStruct(x.shape, x.d...  4.79 us

profile of v12, /device:TPU:21, one launch (start us, length us, event | category | flops | bytes accessed | tf_op | source)
XLA Modules:
  0.0 225.8 jit_solution(7883566285675715493)
XLA Ops:
  0.0 220.8 %blocks.1 = (bf16[8192,768]{1,0:T(8,128)(2,1)S(1)}, bf16[16,336,768]{2,1,0:T(8,128)(2,1)}) custom-call(bf16[8,1024,768]{2,1,0:T(8,128)(2,1)} %x_hbm.1, bf16[8,1024,384]{2,1,0:T(8,128)(2,1)} %cond_hbm.1, bf16[2,1,1024,1024]{3,2,1,0:T(8,128)(2,1)} %bias_hbm.1, s32[1,1024]{1,0:T(1,128)} %bitcast.6, bf16[2,4,48,768]{3,2,1,0:T(8,128)(2,1)} %bitcast.4, ...), custom_call_target="tpu_custom_call" | custom-call | flops 6442450944 | bytes 6291456 | tf_op jit(solution)/shard_map/blocks/pallas_call | solution.py:681
  220.8 4.8 %store.1 = bf16[8192,768]{1,0:T(8,128)(2,1)} custom-call(bf16[8192,768]{1,0:T(8,128)(2,1)S(1)} %get-tuple-element.6.src), custom_call_target="tpu_custom_call" | custom-call | tf_op jit(solution)/shard_map/store/pallas_call | solution.py:707

commit v13 on v12

--- a/solution.py
+++ b/solution.py
@@ -482,9 +482,9 @@
                     for f, args in events[when]:
                         f(*args)
 
-    first, over = (0, 7, 9, 12), (5, 10, 13, 16)
+    first, over, whole = (0, 7, 9, 12), (5, 10, 13, 16), (1, 8, 12, 15)
     for h in range(1, far + 1):
-        plan(first[h - 1] + 1, ring_o.service, h, 0)
+        plan(whole[h - 1], ring_o.service, h, 0)
         for ch in range(n_chunk):
             plan(first[h - 1] + ch, cross.along, h, ch)
             plan(over[h - 1] + ch, cross.across, h, ch)
@@ -594,7 +594,7 @@
     keep.wait()
     events = {}
     for ch in range(n_chunk):
-        plan(3, cross1.along, far - 1, ch)
+        plan(5, cross1.along, far - 1, ch)
         plan(9, cross1.along, far, ch)
         for h in range(1, far + 1):
             plan(2 * h + 5, cross1.across, h, ch)

time: 226 us -> 225 us (level)
  no operation moved by 1% of the time
where the time goes in v13:
time: 225 us
  Pallas kernels  225 us (100%)
    pallas_call x1, Pallas kernels, _main(): pl.pallas_call(functools.partial(_main_kernel, (S, T, D, C, n_tp, n_dp, h...  220 us
    pallas_call x1, Pallas kernels, _store(): pl.pallas_call(_store_kernel, out_shape=jax.ShapeDtypeStruct(x.shape, x.d...  4.79 us

profile of v13, /device:TPU:21, one launch (start us, length us, event | category | flops | bytes accessed | tf_op | source)
XLA Modules:
  0.0 225.0 jit_solution(4676492846584246589)
XLA Ops:
  0.0 220.0 %blocks.1 = (bf16[8192,768]{1,0:T(8,128)(2,1)S(1)}, bf16[16,336,768]{2,1,0:T(8,128)(2,1)}) custom-call(bf16[8,1024,768]{2,1,0:T(8,128)(2,1)} %x_hbm.1, bf16[8,1024,384]{2,1,0:T(8,128)(2,1)} %cond_hbm.1, bf16[2,1,1024,1024]{3,2,1,0:T(8,128)(2,1)} %bias_hbm.1, s32[1,1024]{1,0:T(1,128)} %bitcast.6, bf16[2,4,48,768]{3,2,1,0:T(8,128)(2,1)} %bitcast.4, ...), custom_call_target="tpu_custom_call" | custom-call | flops 6442450944 | bytes 6291456 | tf_op jit(solution)/shard_map/blocks/pallas_call | solution.py:681
  220.0 4.8 %store.1 = bf16[8192,768]{1,0:T(8,128)(2,1)} custom-call(bf16[8192,768]{1,0:T(8,128)(2,1)S(1)} %get-tuple-element.6.src), custom_call_target="tpu_custom_call" | custom-call | tf_op jit(solution)/shard_map/store/pallas_call | solution.py:707

commit v14 on v13

--- a/solution.py
+++ b/solution.py
@@ -112,8 +112,8 @@
 
 
 class Cross:
-    def __init__(self, place, buf, lo, hi, n_chunk, recv_sem, near_sem, far_sem, shift):
-        self.p, self.buf, self.lo, self.hi, self.n_chunk, self.shift = place, buf, lo, hi, n_chunk, shift
+    def __init__(self, place, buf, lo, hi, n_chunk, recv_sem, near_sem, far_sem):
+        self.p, self.buf, self.lo, self.hi, self.n_chunk = place, buf, lo, hi, n_chunk
         self.recv, self.near, self.far_sem = recv_sem, near_sem, far_sem
         self.far = place.nz // 2
         self.size = (hi - lo) // n_chunk
@@ -130,21 +130,21 @@
     def _push_over(self, b, ch):
         p = self.p
         for i in range(1, p.n_dp):
-            self._push(b, ch, {"dp": p.column(i), "tp": p.me}, self.far_sem.at[b // 2])
+            self._push(b, ch, {"dp": p.column(i), "tp": p.me}, self.far_sem.at[b // 2, ch])
         self._push(b, ch, {"tp": p.partner}, self.near)
 
-    def _mine(self, b):
-        return lax.rem(b + self.shift, self.p.n_dp) == self.p.col
+    def _mine(self, b, ch):
+        return lax.rem(b + ch, self.p.n_dp) == self.p.col
 
     def own(self, src):
         p = self.p
         for ch in range(self.n_chunk):
             part = src.at[self._rows(ch), :]
 
-            @pl.when(self._mine(p.me))
+            @pl.when(self._mine(p.me, ch))
             def _():
                 for off in (1, -1):
-                    self._push(p.me, ch, {"tp": p.at(off)}, self.far_sem.at[p.z], part)
+                    self._push(p.me, ch, {"tp": p.at(off)}, self.far_sem.at[p.z, ch], part)
 
             self._push(p.me, ch, {"tp": p.partner}, self.near, part)
 
@@ -165,13 +165,13 @@
         p = self.p
 
         def body(b, sign, onward):
-            @pl.when(self._mine(b))
+            @pl.when(self._mine(b, ch))
             def _():
                 self.wait(b, ch)
 
                 @pl.when(onward)
                 def _():
-                    self._push(b, ch, {"tp": p.at(sign)}, self.far_sem.at[b // 2])
+                    self._push(b, ch, {"tp": p.at(sign)}, self.far_sem.at[b // 2, ch])
 
                 self._push_over(b, ch)
 
@@ -181,16 +181,16 @@
         p = self.p
 
         def body(b, sign, onward):
-            @pl.when(jnp.logical_not(self._mine(b)))
+            @pl.when(jnp.logical_not(self._mine(b, ch)))
             def _():
                 self.wait(b, ch)
                 self._push(b, ch, {"tp": p.partner}, self.near)
 
         self._each(h, body)
 
-    def _sent(self, k, sem):
+    def _sent(self, k, rows, sem):
         if k:
-            v = self.buf.at[0:k, self.lo:self.hi, :]
+            v = self.buf.at[0:k, rows, :]
             pltpu.make_async_copy(v, v, sem).wait()
 
     def finish_near(self):
@@ -202,26 +202,27 @@
             return 0
 
         lax.fori_loop(0, p.nz, other, 0)
-        self._sent(p.nz, self.near)
+        self._sent(p.nz, pl.ds(self.lo, self.hi - self.lo), self.near)
 
     def finish_far(self):
         p = self.p
         over = p.n_dp - 1
-
-        @pl.when(self._mine(p.me))
-        def _():
-            self._sent(2, self.far_sem.at[p.z])
+        for ch in range(self.n_chunk):
+            @pl.when(self._mine(p.me, ch))
+            def _():
+                self._sent(2, self._rows(ch), self.far_sem.at[p.z, ch])
 
         def body(b, sign, onward):
-            @pl.when(self._mine(b))
-            def _():
-                @pl.when(onward)
+            for ch in range(self.n_chunk):
+                sent = functools.partial(self._sent, rows=self._rows(ch), sem=self.far_sem.at[b // 2, ch])
+
+                @pl.when(self._mine(b, ch) & onward)
                 def _():
-                    self._sent(over + 1, self.far_sem.at[b // 2])
-
-                @pl.when(jnp.logical_not(onward))
+                    sent(over + 1)
+
+                @pl.when(self._mine(b, ch) & jnp.logical_not(onward))
                 def _():
-                    self._sent(over, self.far_sem.at[b // 2])
+                    sent(over)
 
         def hop(h, _):
             self._each(h, body)
@@ -421,8 +422,8 @@
     own = [_copy(cond_hbm.at[p.z, mine], cond, own_sem.at[0]), _copy(x_hbm.at[p.z, mine], act, own_sem.at[1])]
     entered()
     ring_o = Ring(p, lambda b, ch: wall.at[b, 0:cut, :], w_recv, w_send)
-    cross = Cross(p, wall, cut, rows_w, n_chunk, c_recv, c_near, c_far, 0)
-    cross1 = Cross(p, w1g, 0, rows_w, n_chunk, d_recv, d_near, d_far, 0)
+    cross = Cross(p, wall, cut, rows_w, n_chunk, c_recv, c_near, c_far)
+    cross1 = Cross(p, w1g, 0, rows_w, n_chunk, d_recv, d_near, d_far)
     ring_x = Ring(p, lambda b, ch: xg.at[pl.ds(b * R + ch * tile, tile), :], x_recv, x_send)
     ring_r = Ring(p, lambda b, ch: xg.at[pl.ds(b * R + ch * tile, tile), :], r_recv, r_send)
     ring_o.own(0, wst.at[0:cut, :])
@@ -675,7 +676,7 @@
     n_chunk = 3
     dma = pltpu.SemaphoreType.DMA
     v = pltpu.VMEM
-    pair, blocks, each = dma((2,)), dma((S,)), dma((n_tp, n_chunk))
+    pair, pieces, each = dma((2,)), dma((S, n_chunk)), dma((n_tp, n_chunk))
     n_tile = 4
     tiles = dma((n_tp, n_tile))
     return pl.pallas_call(
@@ -690,7 +691,7 @@
             *[v((rows_w, D), BF16)] * 2, v((R, C), BF16), v((R, D), BF16), v((R // n_tile, D), BF16), v((R // n_tile, n_tp * hu), BF16),
             v((n_tp, rows_w, D), BF16), *[v((R, 2 * D), F32)] * 3, *[v((n_tp, hd, R), BF16)] * 2,
             pair, pair, dma, dma((4,)), dma((4,)), dma((2, 4)), pair, dma, pair, pair, pltpu.SemaphoreType.REGULAR,
-            dma((2, S, 2)), pair, dma, dma((n_tp, 1)), dma, blocks, each, dma, blocks, each, dma, tiles, dma, tiles, pltpu.SemaphoreType.REGULAR],
+            dma((2, S, 2)), pair, dma, dma((n_tp, 1)), dma, pieces, each, dma, pieces, each, dma, tiles, dma, tiles, pltpu.SemaphoreType.REGULAR],
         cost_estimate=pl.CostEstimate(flops=S * T * T * D, bytes_accessed=S * T * D, transcendentals=S * T * T),
         compiler_params=pltpu.CompilerParams(collective_id=0, has_side_effects=True, vmem_limit_bytes=VM),
         name="blocks",

time: 225 us -> 228 us (1.013); the launches traced: 225 us -> 225 us
  no operation moved by 1% of the time
where the time goes in v14:
time: 228 us; the launch traced here: 225 us
  Pallas kernels  225 us (99%)
    pallas_call x1, Pallas kernels, _main(): pl.pallas_call(functools.partial(_main_kernel, (S, T, D, C, n_tp, n_dp, h...  220 us
    pallas_call x1, Pallas kernels, _store(): pl.pallas_call(_store_kernel, out_shape=jax.ShapeDtypeStruct(x.shape, x.d...  4.79 us

profile of v14, /device:TPU:21, one launch (start us, length us, event | category | flops | bytes accessed | tf_op | source)
XLA Modules:
  0.0 225.2 jit_solution(12203699519183865071)
XLA Ops:
  0.0 220.2 %blocks.1 = (bf16[8192,768]{1,0:T(8,128)(2,1)S(1)}, bf16[16,336,768]{2,1,0:T(8,128)(2,1)}) custom-call(bf16[8,1024,768]{2,1,0:T(8,128)(2,1)} %x_hbm.1, bf16[8,1024,384]{2,1,0:T(8,128)(2,1)} %cond_hbm.1, bf16[2,1,1024,1024]{3,2,1,0:T(8,128)(2,1)} %bias_hbm.1, s32[1,1024]{1,0:T(1,128)} %bitcast.6, bf16[2,4,48,768]{3,2,1,0:T(8,128)(2,1)} %bitcast.4, ...), custom_call_target="tpu_custom_call" | custom-call | flops 6442450944 | bytes 6291456 | tf_op jit(solution)/shard_map/blocks/pallas_call | solution.py:682
  220.2 4.8 %store.1 = bf16[8192,768]{1,0:T(8,128)(2,1)} custom-call(bf16[8192,768]{1,0:T(8,128)(2,1)S(1)} %get-tuple-element.6.src), custom_call_target="tpu_custom_call" | custom-call | tf_op jit(solution)/shard_map/store/pallas_call | solution.py:708

commit v15 on v13

--- a/solution.py
+++ b/solution.py
@@ -612,10 +612,6 @@
             for i in range(n_tile // 2):
                 ring_x.service(j // 2 + 1, lax.rem(j, 2) * (n_tile // 2) + i)
 
-        @pl.when(j >= 1)
-        def _():
-            ex[1].start(j - 1)
-
         s = outward(j)
         with scope("b_half"):
             for ch in range(n_tile):
@@ -624,12 +620,12 @@
         with scope("b_att"):
             at.project()
             at.attend(j)
+        ex[1].start(j)
         with scope("b_ev"):
             take(1, j)
         return 0
 
     lax.fori_loop(0, S, step1, 0)
-    ex[1].start(S - 1)
     pltpu.make_async_copy(w1g, wall, k_sem).wait()
     cross1.finish_far()
     ring_x.drain(xg.at[0:(n_tp - 1) * R, :])

time: 225 us -> 228 us (1.013); the launches traced: 225 us -> 225 us
  no operation moved by 1% of the time
where the time goes in v15:
time: 228 us; the launch traced here: 225 us
  Pallas kernels  225 us (99%)
    pallas_call x1, Pallas kernels, _main(): pl.pallas_call(functools.partial(_main_kernel, (S, T, D, C, n_tp, n_dp, h...  220 us
    pallas_call x1, Pallas kernels, _store(): pl.pallas_call(_store_kernel, out_shape=jax.ShapeDtypeStruct(x.shape, x.d...  4.79 us

profile of v15, /device:TPU:21, one launch (start us, length us, event | category | flops | bytes accessed | tf_op | source)
XLA Modules:
  0.0 225.2 jit_solution(11832610516937627932)
XLA Ops:
  0.0 220.2 %blocks.1 = (bf16[8192,768]{1,0:T(8,128)(2,1)S(1)}, bf16[16,336,768]{2,1,0:T(8,128)(2,1)}) custom-call(bf16[8,1024,768]{2,1,0:T(8,128)(2,1)} %x_hbm.1, bf16[8,1024,384]{2,1,0:T(8,128)(2,1)} %cond_hbm.1, bf16[2,1,1024,1024]{3,2,1,0:T(8,128)(2,1)} %bias_hbm.1, s32[1,1024]{1,0:T(1,128)} %bitcast.6, bf16[2,4,48,768]{3,2,1,0:T(8,128)(2,1)} %bitcast.4, ...), custom_call_target="tpu_custom_call" | custom-call | flops 6442450944 | bytes 6291456 | tf_op jit(solution)/shard_map/blocks/pallas_call | solution.py:677
  220.2 4.8 %store.1 = bf16[8192,768]{1,0:T(8,128)(2,1)} custom-call(bf16[8192,768]{1,0:T(8,128)(2,1)S(1)} %get-tuple-element.6.src), custom_call_target="tpu_custom_call" | custom-call | tf_op jit(solution)/shard_map/store/pallas_call | solution.py:703
